TPU v7x, 32 devices: a whole 2x2x4 slice. The times are simulated.
32 devices in a mesh: grp: 4 (over y, x), seq: 2 (over core), mdl: 4 (over z).
Axes of the slice: x: 2, y: 2, z: 4, core: 2. Of those that a mesh axis runs over, the one named last changes fastest.
Arguments:
- layer_input: bfloat16 [1024, 8192], P('seq', 'grp'), may hold values from -64 to 64
- attn_weight: bfloat16 [8192, 8, 1280], P(('grp', 'seq'), 'mdl'), may hold values from -0.0625 to 0.0625
- rate_weight: bfloat16 [8192, 64], P('grp', 'mdl'), may hold values from -0.15625 to 0.15625
- rate_bias: float32 [64], P(('mdl', 'grp')), may hold values from -8 to -3
- decay_rate: float32 [64], P(('mdl', 'grp')), may hold values from 1e-05 to 0.1
- skip_gain: float32 [64], P(('mdl', 'grp')), may hold values from 0.5 to 1.5
Outputs:
- teacher_heads: bfloat16 [1024, 8192], P('seq', ('mdl', 'grp'))
- student_heads: bfloat16 [1024, 8192], P('seq', ('mdl', 'grp'))
All inputs are finite; a program needn't handle non-finite values.
Results may differ from a plain program's by a relative error of at most 0.03.
Values may be sent and summed in bfloat16 or wider, within the bound.
No kernel may reach another device: no remote copies, remote signals or barrier semaphores. Data moves between devices by JAX's collectives and lax.ppermute only.
A program may use at most 192 MiB of HBM per device.

v0:
```python
import jax
import jax.numpy as jnp
from jax import lax
from jax.sharding import PartitionSpec as P

HEADS = 64
KV_HEADS = 8
HEAD_DIM = 128
STRETCH = 256


ROPE_BASE = 500000.0
FAR_BELOW = -1e30


def rope_angles(positions):
    half = HEAD_DIM // 2
    freq = ROPE_BASE ** (-2.0 * jnp.arange(half, dtype=jnp.float32) / HEAD_DIM)
    angle = positions.astype(jnp.float32)[:, None] * freq[None, :]
    return (jnp.cos(angle), jnp.sin(angle))


def rotate(vectors, cosine, sine):
    half = vectors.shape[-1] // 2
    first = vectors[..., :half]
    second = vectors[..., half:]
    cosine = cosine[:, None, :]
    sine = sine[:, None, :]
    return jnp.concatenate(
        [first * cosine - second * sine, second * cosine + first * sine], axis=-1
    )


def state_product(cterm, state):
    high = state.astype(jnp.bfloat16)
    low = (state - high.astype(jnp.float32)).astype(jnp.bfloat16)
    upper = jnp.einsum("thn,hnp->thp", cterm, high, preferred_element_type=jnp.float32)
    return upper + jnp.einsum("thn,hnp->thp", cterm, low, preferred_element_type=jnp.float32)


def key_absorber(queries, own_first, scale, carry, piece):
    top, total, accum = carry
    keys, values = piece
    scores = jnp.einsum("thd,nd->thn", queries, keys, preferred_element_type=jnp.float32) * scale
    query_pos = own_first + jnp.arange(queries.shape[0], dtype=jnp.int32)
    key_pos = jnp.arange(keys.shape[0], dtype=jnp.int32)
    causal = (key_pos[None, :] <= query_pos[:, None])[:, None, :]
    masked = jnp.where(causal, scores, FAR_BELOW)
    new_top = jnp.maximum(top, jnp.max(masked, axis=2))
    weights = jnp.where(causal, jnp.exp(masked - new_top[:, :, None]), 0.0)
    total = jnp.sum(weights, axis=2)
    accum = jnp.einsum(
        "thn,nd->thd", weights.astype(jnp.bfloat16), values, preferred_element_type=jnp.float32
    )
    return (new_top, total, accum)


def body(layer_input, attn_weight, rate_weight, rate_bias, decay_rate, skip_gain):
    tok = layer_input.shape[0]
    kv_local = attn_weight.shape[1]
    heads_local = rate_bias.shape[0]
    group = HEADS // KV_HEADS
    scale = HEAD_DIM ** (-0.5)
    merged = jnp.einsum(
        "td,dkc->tkc",
        layer_input,
        lax.all_gather(attn_weight, "seq", axis=0, tiled=True),
        preferred_element_type=jnp.float32,
    )
    rate_part = jnp.dot(layer_input, rate_weight, preferred_element_type=jnp.float32)
    grp_index = lax.axis_index("grp")
    summed, rate_whole = (
        lax.psum(merged.astype(jnp.bfloat16), "grp").astype(jnp.float32),
        lax.psum(rate_part.astype(jnp.bfloat16), "grp").astype(jnp.float32),
    )
    query_whole = summed[:, :, : group * HEAD_DIM].reshape(tok, kv_local * group * HEAD_DIM)
    query_flat = lax.dynamic_slice_in_dim(
        query_whole, grp_index * heads_local * HEAD_DIM, heads_local * HEAD_DIM, 1
    )
    raw = lax.dynamic_slice_in_dim(rate_whole, grp_index * heads_local, heads_local, 1)
    pairs = summed[:, :, group * HEAD_DIM :]
    kv_index = grp_index * heads_local // group
    pair = lax.dynamic_index_in_dim(pairs, kv_index, 1, keepdims=False)
    keys = pair[:, :HEAD_DIM]
    values = pair[:, HEAD_DIM:].astype(jnp.bfloat16)
    query = query_flat.reshape(tok, heads_local, HEAD_DIM)
    own_first = lax.axis_index("seq") * tok
    cosine, sine = rope_angles(own_first + jnp.arange(tok, dtype=jnp.int32))
    rot_query = rotate(query, cosine, sine).astype(jnp.bfloat16)
    rot_keys = rotate(keys[:, None, :], cosine, sine)[:, 0].astype(jnp.bfloat16)
    start_carry = (
        jnp.full((tok, heads_local), FAR_BELOW, jnp.float32),
        jnp.zeros((tok, heads_local), jnp.float32),
        jnp.zeros((tok, heads_local, HEAD_DIM), jnp.float32),
    )
    top, total, accum = key_absorber(
        rot_query,
        own_first,
        scale,
        start_carry,
        (
            lax.all_gather(rot_keys, "seq", axis=0, tiled=True),
            lax.all_gather(values, "seq", axis=0, tiled=True),
        ),
    )
    teacher = (accum / total[:, :, None]).astype(jnp.bfloat16).reshape(tok, heads_local * HEAD_DIM)
    step = jax.nn.softplus(raw + rate_bias[None, :])
    log_decay = -decay_rate[None, :] * step
    c_all = query.astype(jnp.bfloat16)
    b_all = keys.astype(jnp.bfloat16)
    causal = (
        jnp.arange(STRETCH, dtype=jnp.int32)[:, None]
        >= jnp.arange(STRETCH, dtype=jnp.int32)[None, :]
    )[None]
    state = jnp.zeros((heads_local, HEAD_DIM, HEAD_DIM), jnp.float32)
    before = jnp.zeros((heads_local,), jnp.float32)
    partials = []
    offsets = []
    for index in range(tok // STRETCH):
        first = index * STRETCH
        cpart = c_all[first : first + STRETCH]
        bpart = b_all[first : first + STRETCH]
        xpart = values[first : first + STRETCH]
        decay = log_decay[first : first + STRETCH]
        rate = step[first : first + STRETCH]
        cum = jnp.cumsum(decay, axis=0)
        gram = jnp.einsum("thn,sn->hts", cpart, bpart, preferred_element_type=jnp.float32) * scale
        diff = cum.T[:, :, None] - cum.T[:, None, :]
        mix = jnp.where(
            causal, jnp.exp(jnp.where(causal, diff, -10000.0)) * rate.T[:, None, :] * gram, 0.0
        ).astype(jnp.bfloat16)
        intra = jnp.einsum("hts,sp->thp", mix, xpart, preferred_element_type=jnp.float32)
        carried = state_product(cpart, state) * scale * jnp.exp(cum)[:, :, None]
        weighted = (
            (jnp.exp(cum[-1][None, :] - cum) * rate)[:, :, None]
            * bpart.astype(jnp.float32)[:, None, :]
        ).astype(jnp.bfloat16)
        contribution = jnp.einsum(
            "shn,sp->hnp", weighted, xpart, preferred_element_type=jnp.float32
        )
        state = jnp.exp(cum[-1])[:, None, None] * state + contribution
        partials.append(intra + carried)
        offsets.append(cum + before[None, :])
        before = before + cum[-1]
    totals, states = (
        lax.all_gather(before[None, :].astype(jnp.bfloat16), "seq", axis=0, tiled=True).astype(
            jnp.float32
        ),
        lax.all_gather(state[None].astype(jnp.bfloat16), "seq", axis=0, tiled=True).astype(
            jnp.float32
        ),
    )
    position = lax.axis_index("seq")
    order = jnp.arange(totals.shape[0], dtype=jnp.int32)
    between = ((order[:, None] < order[None, :]) & (order[None, :] < position)).astype(jnp.float32)
    span = jnp.dot(between, totals, precision=lax.Precision.HIGHEST)
    reach_back = jnp.where(order[:, None] < position, jnp.exp(span), 0.0)
    incoming = jnp.einsum("dh,dhnp->hnp", reach_back, states, precision=lax.Precision.HIGHEST)
    inside = jnp.concatenate(partials, axis=0)
    reach = jnp.exp(jnp.concatenate(offsets, axis=0))
    arriving = state_product(c_all, incoming) * scale * reach[:, :, None]
    skipped = skip_gain[None, :, None] * values.astype(jnp.float32)[:, None, :]
    student = (
        (inside + arriving + skipped).astype(jnp.bfloat16).reshape(tok, heads_local * HEAD_DIM)
    )
    return (teacher, student)


def solution(mesh):
    placed = (
        P("seq", "grp"),
        P(("grp", "seq"), "mdl", None),
        P("grp", "mdl"),
        P(("mdl", "grp")),
        P(("mdl", "grp")),
        P(("mdl", "grp")),
    )
    return jax.shard_map(
        body,
        mesh=mesh,
        in_specs=placed,
        out_specs=(P("seq", ("mdl", "grp")), P("seq", ("mdl", "grp"))),
        check_vma=False,
    )
```

profile of v0, /device:TPU:0, one launch (start us, length us, event | category | flops | bytes accessed | tf_op | source)
XLA Modules:
  0.0 193.4 jit_solution(9953566877105075349)
XLA Ops:
  7.2 5.7 %copy.63 = bf16[1024,2,1280]{2,0,1:T(8,128)(2,1)} copy(bf16[1024,2,1280]{2,1,0:T(2,128)(2,1)} %param.7) | data formatting | bytes 10485760 | tf_op args[1]
  13.7 17.5 %psum.15 = bf16[512,16]{0,1:T(8,128)(2,1)S(1)} all-reduce(bf16[512,16]{0,1:T(8,128)(2,1)S(1)} %convolution_convert_fusion.1), channel_id=1, replica_groups=mesh['grp'=4,'seq'=2,'mdl'=4] {'grp'}, use_global_device_ids=true, to_apply=%region_3.4 | all-reduce | flops 8192 | bytes 32768 | tf_op jit(solution)/shard_map/psum | solution.py:74
  31.2 6.2 %all-gather.5.cloned.1.call-done = bf16[2048,2,1280]{2,0,1:T(8,128)(2,1)} async-done(((bf16[1024,2,1280]{2,0,1:T(8,128)(2,1)}), bf16[2048,2,1280]{2,0,1:T(8,128)(2,1)}) %all-gather.5.cloned.1.call-update) | async-done | bytes 10485776 | tf_op jit(solution)/shard_map/all_gather | solution.py:67
  37.4 10.8 %convolution_convert_fusion = bf16[512,2,1280]{2,0,1:T(8,128)(2,1)} fusion(bf16[2048,2,1280]{2,0,1:T(8,128)(2,1)} %all-gather.5.cloned.1.call-done, bf16[512,2048]{1,0:T(8,128)(2,1)S(1)} %copy-done), kind=kOutput, calls=%fused_computation.7 | convolution fusion | flops 5370019840 | bytes 15204352 | tf_op jit(solution)/shard_map/td,dkc->tkc/dot_general | solution.py:64
  48.3 1.2 reduce-window.14
  49.9 1.2 reduce-window.16
  51.7 1.8 all-gather.2
  57.1 1.2 iota_compare_fusion
  58.2 1.8 multiply_cosine_fusion
  60.0 67.8 %all-reduce.2.cloned.1.call-done = bf16[512,2,1280]{2,0,1:T(8,128)(2,1)} async-done(((bf16[512,2,1280]{2,0,1:T(8,128)(2,1)}), bf16[512,2,1280]{2,0,1:T(8,128)(2,1)}) %all-reduce.2.cloned.1.call-update) | async-done | bytes 2621456 | tf_op jit(solution)/shard_map/psum | solution.py:73
  127.8 1.1 slice.106
  130.1 4.0 %slice.103 = f32[512,2,1024]{2,0,1:T(8,128)} slice(bf16[512,2,1280]{2,0,1:T(8,128)(2,1)} %all-reduce.2.cloned.1.call-done), slice={[0:512], [0:2], [0:1024]} | slice | bytes 8388608 | tf_op jit(solution)/shard_map/slice | solution.py:76
  134.1 5.4 %copy.64 = f32[512,2,1024]{0,2,1:T(8,128)} copy(f32[512,2,1024]{2,0,1:T(8,128)} %slice.103) | data formatting | bytes 8388608 | tf_op jit(solution)/shard_map/slice | solution.py:76
  139.5 2.3 %constant_dynamic-slice_fusion.1 = f32[512,512]{0,1:T(8,128)} fusion(f32[512,2048]{0,1:T(8,128)} %bitcast.150, s32[]{:T(128)S(6)} %select_n.43), kind=kLoop, calls=%fused_computation.149 | loop fusion | bytes 2097156 | tf_op jit(solution)/shard_map/dynamic_slice | solution.py:77
  141.7 1.5 copy.65
  144.3 1.7 fusion.27
  149.3 2.0 %all-gather.1 = bf16[8,128,128]{2,1,0:T(8,128)(2,1)S(1)} all-gather(bf16[4,128,128]{2,1,0:T(8,128)(2,1)S(1)} %fusion.30), channel_id=3, replica_groups=mesh['grp'=4,'seq'=2,'mdl'=4] {'seq'}, dimensions={0}, use_global_device_ids=true | all-gather | bytes 393216 | tf_op jit(solution)/shard_map/all_gather | solution.py:149
  151.3 1.5 multiply_reduce_fusion
  152.7 1.8 copy.99
  154.5 2.4 %fusion.88 = f32[4,128,512]{2,1,0:T(8,128)} fusion(bf16[512,4,128]{2,0,1:T(8,128)(2,1)} %copy-done.1, f32[4,128,128]{1,2,0:T(8,128)} %copy.99), kind=kOutput, calls=%fused_computation.112 | convolution fusion | flops 67174400 | bytes 1835008 | tf_op jit(solution)/shard_map/thn,hnp->thp/dot_general | solution.py:37
  156.9 2.2 %fusion.29 = f32[256,4,128]{0,2,1:T(8,128)} fusion(f32[4,128,256]{2,1,0:T(8,128)} %fusion.71, f32[256,4]{0,1:T(4,128)} %get-tuple-element.28, bf16[512,4,128]{2,0,1:T(8,128)(2,1)} %copy-done.1, f32[4,128,128]{2,1,0:T(8,128)S(1)} %convolution_add_fusion.4), kind=kOutput, calls=%fused_computation.37 | convolution fusion | flops 34078720 | bytes 1576960 | tf_op jit(solution)/shard_map/thn,hnp->thp/dot_general | solution.py:38
  159.2 2.7 %fusion.24 = f32[256,4,128]{0,2,1:T(8,128)} fusion(f32[256,4,128]{0,2,1:T(8,128)} %fusion.27, f32[4,256]{1,0:T(4,128)} %get-tuple-element.20, f32[4,256]{1,0:T(4,128)S(1)} %bitcast.160, pred[256,256]{0,1:T(8,128)(4,1)} %iota_compare_fusion.1, bf16[512,4,128]{2,0,1:T(8,128)(2,1)} %copy-done.1, bf16[512,128]{0,1:T(8,128)(2,1)S(1)} %slice.180, ...), kind=kOutput, calls=%fused_computation.31 | convolution fusion | flops 136183808 | bytes 1519616 | tf_op jit(solution)/shard_map/hts,sp->thp/dot_general | solution.py:132
  161.9 2.7 %fusion.25 = f32[256,4,128]{0,2,1:T(8,128)} fusion(f32[256,4,128]{0,2,1:T(8,128)} %fusion.29, f32[4,256]{1,0:T(4,128)} %get-tuple-element.22, f32[4,256]{1,0:T(4,128)} %bitcast.163, pred[256,256]{0,1:T(8,128)(4,1)} %iota_compare_fusion.1, bf16[512,4,128]{2,0,1:T(8,128)(2,1)} %copy-done.1, bf16[512,128]{0,1:T(8,128)(2,1)S(1)} %slice.180, ...), kind=kOutput, calls=%fused_computation.32 | convolution fusion | flops 136183808 | bytes 1519616 | tf_op jit(solution)/shard_map/hts,sp->thp/dot_general | solution.py:132
  164.6 3.0 %fusion.17 = bf16[512,4,128]{0,2,1:T(8,128)(2,1)} fusion(f32[4,128,512]{2,1,0:T(8,128)} %fusion.88, bf16[512,4,128]{2,0,1:T(8,128)(2,1)} %copy-done.1, f32[256,4,128]{0,2,1:T(8,128)} %fusion.25, f32[256,4,128]{0,2,1:T(8,128)} %fusion.24, f32[512,128]{0,1:T(8,128)} %get-tuple-element.16, f32[4]{0:T(128)} %param.11, f32[512,4]{0,1:T(4,128)S(1)} %fusion.97, ...), kind=kOutput, calls=%fused_computation.23 | convolution fusion | flops 69206016 | bytes 3678224 | tf_op jit(solution)/shard_map/thn,hnp->thp/dot_general | solution.py:38
  167.6 2.1 %copy.83 = bf16[512,512]{1,0:T(8,128)(2,1)} copy(bf16[512,512]{0,1:T(8,128)(2,1)} %bitcast.154) | data formatting | bytes 1048576
  169.7 1.6 fusion.80
  171.3 2.2 %all-gather = bf16[1024,1,128]{0,2,1:T(8,128)(2,1)S(1)} all-gather(bf16[512,1,128]{0,2,1:T(8,128)(2,1)S(1)} %pad_maximum_fusion), channel_id=2, replica_groups=mesh['grp'=4,'seq'=2,'mdl'=4] {'seq'}, dimensions={0}, use_global_device_ids=true | all-gather | bytes 393216 | tf_op jit(solution)/shard_map/all_gather | solution.py:102
  173.5 1.4 subtract_convert_fusion
  174.9 3.0 %fusion = (f32[512,4]{0,1:T(4,128)S(1)}, f32[512,4,1024]{2,0,1:T(8,128)S(1)}) fusion(pred[512,1024]{1,0:T(8,128)(4,1)} %iota_compare_fusion, bf16[1024,1,128]{0,2,1:T(8,128)(2,1)S(1)} %all-gather, bf16[512,4,64]{2,0,1:T(8,128)(2,1)S(1)} %get-tuple-element.13, bf16[512,4,64]{2,0,1:T(8,128)(2,1)S(1)} %get-tuple-element.12), kind=kOutput, calls=%fused_computation.2 | convolution fusion | flops 544208896 | bytes 9707520 | tf_op jit(solution)/shard_map/thd,nd->thn/dot_general | solution.py:44
  177.9 2.0 %all_gather.17 = bf16[1024,128]{0,1:T(8,128)(2,1)S(1)} all-gather(bf16[512,128]{0,1:T(8,128)(2,1)S(1)} %copy-done.5), channel_id=1, replica_groups=mesh['grp'=4,'seq'=2,'mdl'=4] {'seq'}, dimensions={0}, use_global_device_ids=true | all-gather | bytes 393216 | tf_op jit(solution)/shard_map/all_gather | solution.py:103
  179.9 2.9 %fusion.1 = f32[512,4]{0,1:T(4,128)S(1)} fusion(f32[512,4,1024]{2,0,1:T(8,128)S(1)} %get-tuple-element.36, f32[512,4]{0,1:T(4,128)S(1)} %broadcast_maximum_fusion, pred[512,1024]{1,0:T(8,128)(4,1)S(1)} %copy-done.2), kind=kLoop, calls=%fused_computation.3 | loop fusion | flops 10483712 | bytes 8929280 | tf_op jit(solution)/shard_map/reduce_sum | solution.py:51
  182.9 2.7 %divide_convert_fusion = bf16[512,4,128]{0,2,1:T(8,128)(2,1)S(1)} fusion(f32[512,4,1024]{2,0,1:T(8,128)S(1)} %get-tuple-element.36, f32[512,4]{0,1:T(4,128)S(1)} %broadcast_maximum_fusion, pred[512,1024]{1,0:T(8,128)(4,1)S(1)} %copy-done.2, f32[512,4]{0,1:T(4,128)S(1)} %fusion.1, bf16[1024,128]{0,1:T(8,128)(2,1)S(1)} %all_gather.17), kind=kOutput, calls=%fused_computation.53 | convolution fusion | flops 547880960 | bytes 9715712 | tf_op jit(solution)/shard_map/thn,nd->thd/dot_general | solution.py:52
  (72 shorter events, 11.7 us)
Async XLA Ops:
  7.2 5.8 %copy-start = (bf16[512,2048]{1,0:T(8,128)(2,1)S(1)}, bf16[512,2048]{1,0:T(8,128)(2,1)}, u32[]{:S(2)}) copy-start(bf16[512,2048]{1,0:T(8,128)(2,1)} %param.6) | copy-start | bytes 6291460
  7.2 5.8 %copy-start.10 = (f32[4]{0:T(128)S(1)}, f32[4]{0:T(128)}, u32[]{:S(2)}) copy-start(f32[4]{0:T(128)} %param.10) | copy-start | bytes 52
  7.2 5.8 %copy-start.6 = (bf16[2048,16]{0,1:T(8,128)(2,1)S(1)}, bf16[2048,16]{0,1:T(8,128)(2,1)}, u32[]{:S(2)}) copy-start(bf16[2048,16]{0,1:T(8,128)(2,1)} %param.8) | copy-start | bytes 196612
  7.2 30.2 %all-gather.5.cloned.1.call-start = ((), (), s32[]{:S(2)}) async-start(), calls=%async_computation | async-start | bytes 15728640 | tf_op jit(solution)/shard_map/all_gather | solution.py:67
  12.9 114.8 %all-reduce.2.cloned.1.call-start = ((), (), s32[]{:S(2)}) async-start(), calls=%async_computation.1 | async-start | bytes 5242880 | tf_op jit(solution)/shard_map/psum | solution.py:73
  31.2 17.0 %copy-start.9 = (f32[4]{0:T(128)S(1)}, f32[4]{0:T(128)}, u32[]{:S(2)}) copy-start(f32[4]{0:T(128)} %param.9) | copy-start | bytes 52
  51.5 77.4 %copy-start.7 = (f32[1,4,2,128]{3,1,2,0:T(4,128)}, f32[1,4,2,128]{3,1,2,0:T(4,128)S(1)}, u32[]{:S(2)}) copy-start(f32[1,4,2,128]{3,1,2,0:T(4,128)S(1)} %copy.127) | copy-start | bytes 12292
  54.3 74.6 %copy-start.8 = (f32[64]{0:T(128)}, f32[64]{0:T(128)S(1)}, u32[]{:S(2)}) copy-start(f32[64]{0:T(128)S(1)} %multiply_power_fusion) | copy-start | bytes 772
  129.2 14.2 %copy-start.4 = (bf16[512,256]{0,1:T(8,128)(2,1)}, bf16[512,256]{0,1:T(8,128)(2,1)S(1)}, u32[]{:S(2)}) copy-start(bf16[512,256]{0,1:T(8,128)(2,1)S(1)} %bitcast_convert_fusion) | copy-start | bytes 786436
  143.4 3.7 %copy-start.1 = (bf16[512,4,128]{2,0,1:T(8,128)(2,1)}, bf16[512,4,128]{2,0,1:T(8,128)(2,1)S(1)}, u32[]{:S(2)}) copy-start(bf16[512,4,128]{2,0,1:T(8,128)(2,1)S(1)} %convert_element_type.102) | copy-start | bytes 1572868
  159.2 14.3 %copy-start.3 = (f32[512,64]{1,0:T(8,128)S(1)}, f32[512,64]{1,0:T(8,128)}, u32[]{:S(2)}) copy-start(f32[512,64]{1,0:T(8,128)} %get-tuple-element.33) | copy-start | bytes 393220
  167.6 10.3 %copy-start.5 = (bf16[512,128]{0,1:T(8,128)(2,1)S(1)}, bf16[512,128]{0,1:T(8,128)(2,1)}, u32[]{:S(2)}) copy-start(bf16[512,128]{0,1:T(8,128)(2,1)} %get-tuple-element.17) | copy-start | bytes 393220
  169.7 10.2 %copy-start.2 = (pred[512,1024]{1,0:T(8,128)(4,1)S(1)}, pred[512,1024]{1,0:T(8,128)(4,1)}, u32[]{:S(2)}) copy-start(pred[512,1024]{1,0:T(8,128)(4,1)} %iota_compare_fusion) | copy-start | bytes 1572868
Sparse Core Ops, SparseCore 0:
  13.0 24.3 all-gather.4
  48.3 79.3 all-reduce.1
where the time goes:
time: 194 us; the launch traced here: 193 us
  waiting for transfers between devices  74 us (38%)
  matrix products  35.9 us (19%)
  local copies, waits for them, and re-layouts  27.5 us (14%)
  blocking collectives  25.5 us (13%)
  other arithmetic  16.1 us (8%)
  between operations  14.4 us (7%)
    psum x1, waiting for transfers between devices, body(): lax.psum(merged.astype(jnp.bfloat16), 'grp').astype(jnp.float32)  67.8 us
    psum x1, blocking collectives, body(): lax.psum(rate_part.astype(jnp.bfloat16), 'grp').astype(jnp.float32)  17.5 us
    dot_general x1, matrix products, body(): jnp.einsum('td,dkc->tkc', layer_input, lax.all_gather(attn_weight, 'seq',...  10.8 us
    slice x2, local copies, waits for them, and re-layouts, body(): summed[:, :, :group * HEAD_DIM].reshape(tok, kv_local * group * HEAD_DIM)  9.39 us
    unnamed x27, local copies, waits for them, and re-layouts  8.8 us
    all_gather x1, waiting for transfers between devices, body(): lax.all_gather(attn_weight, 'seq', axis=0, tiled=True)  6.21 us
    another operation x7, other arithmetic  5.51 us
    dot_general x2, matrix products, body(): jnp.einsum('hts,sp->thp', mix, xpart, preferred_element_type=jnp.float32)  5.41 us
  transfers between devices with their start and end apart: 2, of which 2 were waited for; matrix products, arithmetic and copies ran while one was open for 5% of the time, Pallas kernels for 0%

commit v1 on v0

--- a/solution.py
+++ b/solution.py
@@ -1,6 +1,10 @@
+import functools
+
 import jax
 import jax.numpy as jnp
 from jax import lax
+from jax.experimental import pallas as pl
+from jax.experimental.pallas import tpu as pltpu
 from jax.sharding import PartitionSpec as P
 
 HEADS = 64
@@ -166,6 +170,360 @@
     return (teacher, student)
 
 
+LANES = 128
+VMEM_GRANT = 24 * 1024 * 1024
+F32 = jnp.float32
+BF16 = jnp.bfloat16
+
+
+def cost(flops, moved):
+    return pl.CostEstimate(flops=flops, bytes_accessed=moved, transcendentals=0)
+
+
+def project_kernel(ids, x_ref, w0, w1, w2, w3, out_ref):
+    weights = jnp.concatenate([w0[0], w1[0], w2[0], w3[0]], axis=1)
+    out_ref[...] = jnp.dot(x_ref[...], weights, preferred_element_type=F32).astype(BF16)
+
+
+def project_add_kernel(ids, x_ref, w0, w1, w2, w3, r_ref, send_ref, keep_ref):
+    half = keep_ref.shape[1]
+    sent = jnp.concatenate([w0[0], w1[0]], axis=1)
+    kept = jnp.concatenate([w2[0], w3[0]], axis=1)
+    first = jnp.dot(x_ref[...], sent, preferred_element_type=F32)
+    send_ref[...] = (first + r_ref[:, :half].astype(F32)).astype(BF16)
+    second = jnp.dot(x_ref[...], kept, preferred_element_type=F32)
+    keep_ref[...] = second + r_ref[:, half:].astype(F32)
+
+
+def weight_spec(rows, place):
+    def index(step, ids):
+        kv, col = place(ids[0], ids[1])
+        return (kv, 0, col)
+
+    return pl.BlockSpec((1, rows, LANES), index)
+
+
+def project(ids, x, x_block, weights, places):
+    tok, rows = x.shape[0], weights.shape[1]
+    wide = len(places) * LANES
+    return pl.pallas_call(
+        project_kernel,
+        grid_spec=pltpu.PrefetchScalarGridSpec(
+            num_scalar_prefetch=1,
+            grid=(1,),
+            in_specs=[pl.BlockSpec((tok, rows), x_block)]
+            + [weight_spec(rows, place) for place in places],
+            out_specs=pl.BlockSpec((tok, wide), lambda step, ids: (0, 0)),
+        ),
+        out_shape=jax.ShapeDtypeStruct((tok, wide), BF16),
+        compiler_params=pltpu.CompilerParams(vmem_limit_bytes=VMEM_GRANT),
+        cost_estimate=cost(2 * tok * rows * wide, 2 * rows * (tok + wide)),
+    )(ids, x, *([weights] * len(places)))
+
+
+def project_add(ids, x, x_block, weights, places, received):
+    tok, rows = x.shape[0], weights.shape[1]
+    wide = len(places) * LANES
+    half = wide // 2
+    return pl.pallas_call(
+        project_add_kernel,
+        grid_spec=pltpu.PrefetchScalarGridSpec(
+            num_scalar_prefetch=1,
+            grid=(1,),
+            in_specs=[pl.BlockSpec((tok, rows), x_block)]
+            + [weight_spec(rows, place) for place in places]
+            + [pl.BlockSpec((tok, wide), lambda step, ids: (0, 0))],
+            out_specs=[
+                pl.BlockSpec((tok, half), lambda step, ids: (0, 0)),
+                pl.BlockSpec((tok, half), lambda step, ids: (0, 0)),
+            ],
+        ),
+        out_shape=[
+            jax.ShapeDtypeStruct((tok, half), BF16),
+            jax.ShapeDtypeStruct((tok, half), F32),
+        ],
+        compiler_params=pltpu.CompilerParams(vmem_limit_bytes=VMEM_GRANT),
+        cost_estimate=cost(2 * tok * rows * wide, 2 * rows * (tok + wide)),
+    )(ids, x, *([weights] * len(places)), received)
+
+
+def turn(vectors, cosine, sine):
+    return vectors * cosine + pltpu.roll(vectors, HEAD_DIM // 2, 1) * sine
+
+
+def keys_kernel(keep_ref, u_ref, z_ref, cos_ref, sin_ref, rotv_ref, bterm_ref):
+    pair = keep_ref[...] + u_ref[...].astype(F32) + z_ref[...].astype(F32)
+    keys = pair[:, :HEAD_DIM]
+    rotv_ref[:, :HEAD_DIM] = turn(keys, cos_ref[...], sin_ref[...]).astype(BF16)
+    rotv_ref[:, HEAD_DIM:] = pair[:, HEAD_DIM:].astype(BF16)
+    bterm_ref[...] = keys.astype(BF16)
+
+
+def whole(shape):
+    return pl.BlockSpec(shape, lambda: (0,) * len(shape))
+
+
+def keys_call(keep, u, z, cosine, sine):
+    tok = keep.shape[0]
+    shapes = [(tok, 2 * HEAD_DIM), (tok, HEAD_DIM)]
+    return pl.pallas_call(
+        keys_kernel,
+        in_specs=[whole(a.shape) for a in (keep, u, z, cosine, sine)],
+        out_specs=[whole(s) for s in shapes],
+        out_shape=[jax.ShapeDtypeStruct(s, BF16) for s in shapes],
+        compiler_params=pltpu.CompilerParams(vmem_limit_bytes=VMEM_GRANT),
+        cost_estimate=cost(10**8, 10**6),
+    )(keep, u, z, cosine, sine)
+
+
+def decays_of(raw, bias, rate):
+    step = jax.nn.softplus(raw + bias)
+    return step, -rate * step
+
+
+def running(decay):
+    count = decay.shape[1]
+    rows = lax.broadcasted_iota(jnp.int32, (count, count), 0)
+    cols = lax.broadcasted_iota(jnp.int32, (count, count), 1)
+    below = (cols <= rows).astype(F32)
+    dims = (((1,), (1,)), ((), ()))
+    across = lax.dot_general(
+        decay, below, dims, precision=lax.Precision.HIGHEST, preferred_element_type=F32
+    )
+    down = lax.dot_general(
+        below, decay, dims, precision=lax.Precision.HIGHEST, preferred_element_type=F32
+    )
+    return across, down
+
+
+def states_kernel(
+    stretch, raw_ref, bias_ref, rate_ref, rotv_ref, bterm_ref,
+    across_ref, down_ref, step_ref, first_ref, last_ref,
+):
+    heads = raw_ref.shape[0]
+    tok = raw_ref.shape[1]
+    step, decay = decays_of(raw_ref[...], bias_ref[...], rate_ref[...])
+    step_ref[...] = step
+    states = [jnp.zeros((HEAD_DIM, HEAD_DIM), F32)] * heads
+    for index in range(tok // stretch):
+        span = slice(index * stretch, (index + 1) * stretch)
+        across, down = running(decay[:, span])
+        across_ref[:, span] = across
+        down_ref[span, :] = down
+        keys = bterm_ref[span, :].astype(F32)
+        values = rotv_ref[span, HEAD_DIM:]
+        ends = jnp.exp(across[:, stretch - 1 :])
+        tail = jnp.exp(across[:, stretch - 1 :] - across) * step[:, span]
+        eye = (
+            lax.broadcasted_iota(jnp.int32, (heads, heads), 0)
+            == lax.broadcasted_iota(jnp.int32, (heads, heads), 1)
+        ).astype(F32)
+        tail = lax.dot_general(
+            tail, eye, (((0,), (0,)), ((), ())),
+            precision=lax.Precision.HIGHEST, preferred_element_type=F32,
+        )
+        for head in range(heads):
+            weighted = (keys * tail[:, head : head + 1]).astype(BF16)
+            fresh = lax.dot_general(
+                weighted, values, (((0,), (0,)), ((), ())), preferred_element_type=F32
+            )
+            states[head] = ends[head : head + 1, :] * states[head] + fresh
+            if index == 0:
+                first_ref[head] = states[head]
+    for head in range(heads):
+        last_ref[head] = states[head].astype(BF16)
+
+
+def states_call(raw, bias, rate, rotv, bterm):
+    heads, tok = raw.shape
+    square = (heads, HEAD_DIM, HEAD_DIM)
+    shapes = [((heads, tok), F32), ((tok, heads), F32), ((heads, tok), F32), (square, F32), (square, BF16)]
+    return pl.pallas_call(
+        functools.partial(states_kernel, STRETCH),
+        in_specs=[whole(a.shape) for a in (raw, bias, rate, rotv, bterm)],
+        out_specs=[whole(s) for s, _ in shapes],
+        out_shape=[jax.ShapeDtypeStruct(s, d) for s, d in shapes],
+        compiler_params=pltpu.CompilerParams(vmem_limit_bytes=VMEM_GRANT),
+        cost_estimate=cost(10**9, 10**6),
+    )(raw, bias, rate, rotv, bterm)
+
+
+def heads_kernel(stretch, numbers, ids, *refs):
+    pieces = refs[: 3 * len(numbers)]
+    (cos_ref, sin_ref, rotv_ref, bterm_ref, prev_ref, across_ref, down_ref, step_ref,
+     first_ref, arrived_ref, skip_ref) = refs[3 * len(numbers) : 3 * len(numbers) + 11]
+    outs = refs[-2 * len(numbers) :]
+    tok = rotv_ref.shape[0]
+    scale = HEAD_DIM ** (-0.5)
+    power = scale * 1.4426950408889634
+    later = (ids[2] > 0).astype(F32)
+    blocked = (1.0 - later) * FAR_BELOW
+    rows = lax.broadcasted_iota(jnp.int32, (stretch, stretch), 0)
+    cols = lax.broadcasted_iota(jnp.int32, (stretch, stretch), 1)
+    causal = cols <= rows
+    last = (((1,), (1,)), ((), ()))
+    ones = jnp.ones((tok, HEAD_DIM), BF16)
+    own_keys = rotv_ref[:, :HEAD_DIM]
+    prev_keys = prev_ref[:, :HEAD_DIM]
+    own_values = jnp.concatenate([rotv_ref[:, HEAD_DIM:], ones], axis=1)
+    prev_values = jnp.concatenate([prev_ref[:, HEAD_DIM:], ones], axis=1)
+    for at, head in enumerate(numbers):
+        keep_ref, u_ref, z_ref = pieces[3 * at : 3 * at + 3]
+        teacher_ref, student_ref = outs[2 * at : 2 * at + 2]
+        query = keep_ref[...] + u_ref[...].astype(F32) + z_ref[...].astype(F32)
+        turned = turn(query, cos_ref[...], sin_ref[...]).astype(BF16)
+        cterm = query.astype(BF16)
+        state = arrived_ref[head].astype(F32) * later
+        skip = skip_ref[0, head]
+        for index in range(tok // stretch):
+            span = slice(index * stretch, (index + 1) * stretch)
+            queries = turned[span]
+            far = lax.dot_general(queries, prev_keys, last, preferred_element_type=F32) + blocked
+            near = lax.dot_general(
+                queries, own_keys[: (index + 1) * stretch], last, preferred_element_type=F32
+            )
+            diagonal = jnp.where(causal, near[:, index * stretch :], FAR_BELOW)
+            near = diagonal if index == 0 else jnp.concatenate([near[:, : index * stretch], diagonal], axis=1)
+            top = jnp.maximum(jnp.max(far, axis=1, keepdims=True), jnp.max(near, axis=1, keepdims=True))
+            far = jnp.exp2((far - top) * power).astype(BF16)
+            near = jnp.exp2((near - top) * power).astype(BF16)
+            mixed = jnp.dot(far, prev_values, preferred_element_type=F32) + jnp.dot(
+                near, own_values[: (index + 1) * stretch], preferred_element_type=F32
+            )
+            teacher_ref[span, :] = (mixed[:, :HEAD_DIM] / mixed[:, HEAD_DIM:]).astype(BF16)
+            values = rotv_ref[span, HEAD_DIM:]
+            down = down_ref[span, head : head + 1]
+            across = across_ref[head : head + 1, span]
+            gram = lax.dot_general(
+                cterm[span], bterm_ref[span, :], last, preferred_element_type=F32
+            ) * (step_ref[head : head + 1, span] * scale)
+            mix = jnp.where(causal, jnp.exp(jnp.where(causal, down - across, -1e4)) * gram, 0.0)
+            inner = jnp.dot(mix.astype(BF16), values, preferred_element_type=F32)
+            high = state.astype(BF16)
+            low = (state - high.astype(F32)).astype(BF16)
+            carried = jnp.dot(cterm[span], high, preferred_element_type=F32) + jnp.dot(
+                cterm[span], low, preferred_element_type=F32
+            )
+            carried = carried * (jnp.exp(down) * scale)
+            student_ref[span, :] = (inner + carried + skip * values.astype(F32)).astype(BF16)
+            if index == 0:
+                ends = jnp.exp(across[:, stretch - 1 :])
+                state = ends * state + first_ref[head]
+
+
+def heads_call(ids, numbers, pieces, shared):
+    tok = shared[2].shape[0]
+    wide = lambda a, col: pl.BlockSpec((tok, LANES), lambda step, ids, col=col: (0, col))
+    flat = lambda a: pl.BlockSpec(a.shape, lambda step, ids, n=a.ndim: (0,) * n)
+    specs, args = [], []
+    for keep, u, z in pieces:
+        specs += [wide(keep, 1), wide(u, 1), wide(z, 0)]
+        args += [keep, u, z]
+    specs += [flat(a) for a in shared[:-1]] + [pl.BlockSpec(memory_space=pltpu.SMEM)]
+    count = 2 * len(numbers)
+    return pl.pallas_call(
+        functools.partial(heads_kernel, STRETCH, numbers),
+        grid_spec=pltpu.PrefetchScalarGridSpec(
+            num_scalar_prefetch=1,
+            grid=(1,),
+            in_specs=specs,
+            out_specs=[pl.BlockSpec((tok, LANES), lambda step, ids: (0, 0))] * count,
+        ),
+        out_shape=[jax.ShapeDtypeStruct((tok, LANES), BF16)] * count,
+        compiler_params=pltpu.CompilerParams(vmem_limit_bytes=VMEM_GRANT),
+        cost_estimate=cost(2 * 10**9, 3 * 10**6),
+    )(ids, *args, *shared)
+
+
+def pair_body(layer_input, attn_weight, rate_weight, rate_bias, decay_rate, skip_gain):
+    tok, share = layer_input.shape
+    rows = attn_weight.shape[0]
+    heads = rate_bias.shape[0]
+    group = HEADS // KV_HEADS
+    grp = lax.axis_index("grp")
+    seq = lax.axis_index("seq")
+    high, low = grp // 2, grp % 2
+    ids = jnp.stack([high, low, seq]).astype(jnp.int32)
+    count = lax.axis_size("grp")
+    swap_high = [(g, g ^ 2) for g in range(count)]
+    swap_low = [(g, g ^ 1) for g in range(count)]
+    swap_seq = [(0, 1), (1, 0)]
+    onward = [(0, 1)]
+    over_high = lambda a: lax.ppermute(a, "grp", swap_high)
+    over_low = lambda a: lax.ppermute(a, "grp", swap_low)
+    over_seq = lambda a: lax.ppermute(a, "seq", swap_seq)
+
+    other = over_seq(lax.dynamic_slice_in_dim(layer_input, (1 - seq) * rows, rows, 1))
+    weights = jnp.transpose(attn_weight, (1, 0, 2))
+    other_block = lambda step, ids: (0, 0)
+    own_block = lambda step, ids: (0, ids[2])
+
+    raw = jnp.einsum("dh,td->ht", rate_weight, layer_input, preferred_element_type=F32)
+    raw = lax.dynamic_slice_in_dim(raw, high * 2 * heads, 2 * heads, 0) + over_high(
+        lax.dynamic_slice_in_dim(raw, (1 - high) * 2 * heads, 2 * heads, 0)
+    )
+    raw = lax.dynamic_slice_in_dim(raw, low * heads, heads, 0) + over_low(
+        lax.dynamic_slice_in_dim(raw, (1 - low) * heads, heads, 0)
+    )
+
+    cosine, sine = rope_angles(seq * tok + jnp.arange(tok, dtype=jnp.int32))
+    cosine = jnp.concatenate([cosine, cosine], axis=1)
+    sine = jnp.concatenate([-sine, sine], axis=1)
+
+    def pair_places(col):
+        return [
+            lambda h, l: (1 - h, col), lambda h, l: (1 - h, col + 1),
+            lambda h, l: (h, col), lambda h, l: (h, col + 1),
+        ]
+
+    def high_places(j):
+        return [
+            lambda h, l: (1 - h, (1 - l) * heads + j), lambda h, l: (1 - h, l * heads + j),
+            lambda h, l: (h, (1 - l) * heads + j), lambda h, l: (h, l * heads + j),
+        ]
+
+    def low_places(j):
+        return [
+            lambda h, l: (1 - h, (1 - l) * heads + j), lambda h, l: (h, (1 - l) * heads + j),
+            lambda h, l: (1 - h, l * heads + j), lambda h, l: (h, l * heads + j),
+        ]
+
+    half = heads // 2
+    plan = [("kv", None, pair_places(group), over_high, over_low)]
+    for j in range(half):
+        plan.append(("q", j, high_places(j), over_high, over_low))
+        plan.append(("q", half + j, low_places(half + j), over_low, over_high))
+    crossed = [
+        over_seq(project(ids, other, other_block, weights, places))
+        for _, _, places, _, _ in plan
+    ]
+    pieces = {}
+    for (kind, j, places, first, second), received in zip(plan, crossed):
+        send, keep = project_add(ids, layer_input, own_block, weights, places, received)
+        u = first(send)
+        if kind == "kv":
+            z = second((keep + u.astype(F32)).astype(BF16))
+            rotv, bterm = keys_call(keep, u, z, cosine, sine)
+            prev = lax.ppermute(rotv, "seq", onward)
+            across, down, step, first_state, last_state = states_call(
+                raw, rate_bias[:, None], decay_rate[:, None], rotv, bterm
+            )
+            arrived = lax.ppermute(last_state, "seq", onward)
+        else:
+            z = second((keep[:, :LANES] + u[:, :LANES].astype(F32)).astype(BF16))
+            pieces[j] = (keep, u, z)
+    shared = (
+        cosine, sine, rotv, bterm, prev, across, down, step, first_state, arrived, skip_gain[None, :],
+    )
+    teacher, student = [None] * heads, [None] * heads
+    for j in range(half):
+        numbers = (j, half + j)
+        outs = heads_call(ids, numbers, [pieces[n] for n in numbers], shared)
+        for at, n in enumerate(numbers):
+            teacher[n], student[n] = outs[2 * at], outs[2 * at + 1]
+    return jnp.concatenate(teacher, axis=1), jnp.concatenate(student, axis=1)
+
+
 def solution(mesh):
     placed = (
         P("seq", "grp"),
@@ -175,8 +533,15 @@
         P(("mdl", "grp")),
         P(("mdl", "grp")),
     )
+    chips = mesh.shape["grp"] * mesh.shape["mdl"]
+    paired = (
+        mesh.shape["seq"] == 2
+        and mesh.shape["grp"] == 4
+        and KV_HEADS == 2 * mesh.shape["mdl"]
+        and HEADS // chips == 4
+    )
     return jax.shard_map(
-        body,
+        pair_body if paired else body,
         mesh=mesh,
         in_specs=placed,
         out_specs=(P("seq", ("mdl", "grp")), P("seq", ("mdl", "grp"))),

time: 194 us -> 71.3 us (0.37)
  waiting for transfers between devices: 74 us -> 10.9 us
  matrix products: 35.9 us -> 0.64 us
  blocking collectives: 25.5 us -> 0 us
  Pallas kernels: 0 us -> 24.2 us
  starting transfers between devices: 0.08 us -> 20.6 us
  local copies, waits for them, and re-layouts: 27.5 us -> 10.6 us
  between operations: 14.4 us -> 0.92 us
  other arithmetic: 16.1 us -> 3.2 us
    psum x1 -> x0, waiting for transfers between devices: 67.8 us -> none  [body(): lax.psum(merged.astype(jnp.bfloat16), 'grp').astype(jnp.float32)]
    dot_general x14 -> x1, matrix products: 35.9 us -> 0.64 us  [pair_body(): jnp.einsum('dh,td->ht', rate_weight, layer_input, preferred_element_type=...]
    pallas_call x0 -> x14, Pallas kernels: none -> 24.2 us  [the longest x2 7.43 us: heads_call(): pl.pallas_call(functools.partial(heads_kernel, STRETCH, numbers), grid_sp...]
    ppermute x0 -> x20, starting transfers between devices: none -> 20.6 us  [the longest x6 8.61 us: pair_body(): over_low = lambda a: lax.ppermute(a, 'grp', swap_low)]
    psum x1 -> x0, blocking collectives: 17.5 us -> none  [body(): lax.psum(rate_part.astype(jnp.bfloat16), 'grp').astype(jnp.float32)]
    slice x8 -> x0, local copies, waits for them, and re-layouts: 11.1 us -> none  [the longest x2 9.39 us: body(): summed[:, :, :group * HEAD_DIM].reshape(tok, kv_local * group * HEAD_DIM)]
    ppermute x0 -> x20, waiting for transfers between devices: none -> 10.9 us  [the longest x6 5.87 us: pair_body(): over_low = lambda a: lax.ppermute(a, 'grp', swap_low)]
    all_gather x4 -> x0, blocking collectives: 7.97 us -> none  [the longest x1 2.17 us: body(): lax.all_gather(rot_keys, 'seq', axis=0, tiled=True)]
  transfers between devices with their start and end apart: 2 -> 20, of which waited for: 2 -> 4; matrix products, arithmetic and copies ran while one was open for 5% -> 11% of each run, Pallas kernels for 0% -> 29%
where the time goes in v1:
time: 71.3 us; the launch traced here: 71 us
  Pallas kernels  24.2 us (34%)
  starting transfers between devices  20.6 us (29%)
  waiting for transfers between devices  10.9 us (15%)
  local copies, waits for them, and re-layouts  10.6 us (15%)
  other arithmetic  3.2 us (4%)
  between operations  0.92 us (1%)
    ppermute x6, starting transfers between devices, pair_body(): over_low = lambda a: lax.ppermute(a, 'grp', swap_low)  8.61 us
    unnamed x17, local copies, waits for them, and re-layouts  7.97 us
    pallas_call x2, Pallas kernels, heads_call(): pl.pallas_call(functools.partial(heads_kernel, STRETCH, numbers), grid_sp...  7.43 us
    ppermute x6, starting transfers between devices, pair_body(): over_high = lambda a: lax.ppermute(a, 'grp', swap_high)  7.14 us
    pallas_call x5, Pallas kernels, project(): pl.pallas_call(project_kernel, grid_spec=pltpu.PrefetchScalarGridSpec(num...  6.85 us
    pallas_call x5, Pallas kernels, project_add(): pl.pallas_call(project_add_kernel, grid_spec=pltpu.PrefetchScalarGridSpec...  6.82 us
    ppermute x6, waiting for transfers between devices, pair_body(): over_low = lambda a: lax.ppermute(a, 'grp', swap_low)  5.87 us
    ppermute x6, waiting for transfers between devices, pair_body(): over_high = lambda a: lax.ppermute(a, 'grp', swap_high)  5.01 us
  transfers between devices with their start and end apart: 20, of which 4 were waited for; matrix products, arithmetic and copies ran while one was open for 11% of the time, Pallas kernels for 29%

profile of v1, /device:TPU:0, one launch (start us, length us, event | category | flops | bytes accessed | tf_op | source)
XLA Modules:
  0.0 71.0 jit_solution(11304718440644623757)
XLA Ops:
  0.7 2.4 %constant_dynamic-slice_fusion.2 = bf16[512,1024]{1,0:T(8,128)(2,1)} fusion(bf16[512,2048]{1,0:T(8,128)(2,1)} %x_ref.9, s32[]{:T(128)S(6)} %select_n.28), kind=kLoop, calls=%fused_computation.18 | loop fusion | bytes 2097156 | tf_op jit(solution)/shard_map/dynamic_slice | solution.py:456
  4.3 2.5 %collective-permute-start.11 = (f32[8,512]{1,0:T(8,128)S(1)}, f32[8,512]{1,0:T(8,128)S(1)}, u32[]{:S(2)}, u32[]{:S(2)}) collective-permute-start(f32[8,512]{1,0:T(8,128)S(1)} %constant_dynamic-slice_fusion.1), channel_id=1, source_target_pairs={{0,16},{8,24},{16,0},{24,8},{1,17},{9,25},{17,1},{25,9},{2,18},{10... | collective-permute-start | bytes 49160 | tf_op jit(solution)/shard_map/ppermute | solution.py:452
  7.0 5.5 %copy.12 = bf16[1024,2,1280]{2,0,1:T(8,128)(2,1)} copy(bf16[1024,2,1280]{2,1,0:T(2,128)(2,1)} %param.7) | data formatting | bytes 10485760 | tf_op args[1]
  12.5 1.0 %fusion = (f32[512,64]{1,0:T(8,128)S(1)}, f32[512,64]{1,0:T(8,128)S(1)}, f32[512,64]{1,0:T(8,128)S(1)}) fusion(f32[64]{0:T(128)S(1)} %multiply_power_fusion, f32[512]{0:T(512)S(1)} %add_convert_fusion.5), kind=kLoop, calls=%fused_computation.12 | loop fusion | flops 65536 | bytes 395520 | tf_op jit(solution)/shard_map/neg | solution.py:471
  13.8 2.5 %copy-done.1 = bf16[1024,2,1280]{2,0,1:T(8,128)(2,1)S(1)} copy-done((bf16[1024,2,1280]{2,0,1:T(8,128)(2,1)S(1)}, bf16[1024,2,1280]{2,0,1:T(8,128)(2,1)}, u32[]{:S(2)}) %copy-start.1) | copy-done | bytes 5242904
  16.3 1.4 %shard_map.77 = bf16[512,512]{1,0:T(8,128)(2,1)S(1)} custom-call(s32[3]{0:T(128)S(1)} %pad_add_fusion.ids, bf16[512,1024]{1,0:T(8,128)(2,1)S(1)} %collective-permute-done.x_ref, bf16[2,1024,1280]{2,1,0:T(8,128)(2,1)S(1)} %bitcast.11, bf16[2,1024,1280]{2,1,0:T(8,128)(2,1)S(1)} %bitcast.12, bf16[2,1024,1280]{2,1,0:T(8,128)(2,1)S(1)} %bitcast.13, ...), custom_call_target="tpu_custom_call" | custom-call | flops 536870912 | bytes 2097152 | tf_op jit(solution)/shard_map/pallas_call | solution.py:209
  17.9 1.4 %shard_map.79 = bf16[512,512]{1,0:T(8,128)(2,1)S(1)} custom-call(s32[3]{0:T(128)S(1)} %pad_add_fusion.ids, bf16[512,1024]{1,0:T(8,128)(2,1)S(1)} %collective-permute-done.x_ref, bf16[2,1024,1280]{2,1,0:T(8,128)(2,1)S(1)} %bitcast.15, bf16[2,1024,1280]{2,1,0:T(8,128)(2,1)S(1)} %bitcast.16, bf16[2,1024,1280]{2,1,0:T(8,128)(2,1)S(1)} %bitcast.17, ...), custom_call_target="tpu_custom_call" | custom-call | flops 536870912 | bytes 2097152 | tf_op jit(solution)/shard_map/pallas_call | solution.py:209
  19.7 1.4 %shard_map.81 = bf16[512,512]{1,0:T(8,128)(2,1)S(1)} custom-call(s32[3]{0:T(128)S(1)} %pad_add_fusion.ids, bf16[512,1024]{1,0:T(8,128)(2,1)S(1)} %collective-permute-done.x_ref, bf16[2,1024,1280]{2,1,0:T(8,128)(2,1)S(1)} %bitcast.19, bf16[2,1024,1280]{2,1,0:T(8,128)(2,1)S(1)} %bitcast.20, bf16[2,1024,1280]{2,1,0:T(8,128)(2,1)S(1)} %bitcast.21, ...), custom_call_target="tpu_custom_call" | custom-call | flops 536870912 | bytes 2097152 | tf_op jit(solution)/shard_map/pallas_call | solution.py:209
  21.3 1.4 %shard_map.86 = bf16[512,512]{1,0:T(8,128)(2,1)S(1)} custom-call(s32[3]{0:T(128)S(1)} %pad_add_fusion.ids, bf16[512,1024]{1,0:T(8,128)(2,1)S(1)} %collective-permute-done.x_ref, bf16[2,1024,1280]{2,1,0:T(8,128)(2,1)S(1)} %bitcast.23, bf16[2,1024,1280]{2,1,0:T(8,128)(2,1)S(1)} %bitcast.24, bf16[2,1024,1280]{2,1,0:T(8,128)(2,1)S(1)} %bitcast.25, ...), custom_call_target="tpu_custom_call" | custom-call | flops 536870912 | bytes 2097152 | tf_op jit(solution)/shard_map/pallas_call | solution.py:209
  23.1 1.4 %shard_map.88 = bf16[512,512]{1,0:T(8,128)(2,1)S(1)} custom-call(s32[3]{0:T(128)S(1)} %pad_add_fusion.ids, bf16[512,1024]{1,0:T(8,128)(2,1)S(1)} %collective-permute-done.x_ref, bf16[2,1024,1280]{2,1,0:T(8,128)(2,1)S(1)} %bitcast.30, bf16[2,1024,1280]{2,1,0:T(8,128)(2,1)S(1)} %bitcast.28, bf16[2,1024,1280]{2,1,0:T(8,128)(2,1)S(1)} %bitcast.29, ...), custom_call_target="tpu_custom_call" | custom-call | flops 536870912 | bytes 2097152 | tf_op jit(solution)/shard_map/pallas_call | solution.py:209
  24.8 1.5 %collective-permute-start.12 = (f32[4,512]{1,0:T(4,128)S(1)}, f32[4,512]{1,0:T(4,128)S(1)}, u32[]{:S(2)}, u32[]{:S(2)}) collective-permute-start(f32[4,512]{1,0:T(4,128)S(1)} %constant_dynamic-slice_fusion), channel_id=1, source_target_pairs={{0,8},{8,0},{16,24},{24,16},{1,9},{9,1},{17,25},{25,17},{2,10},{10... | collective-permute-start | bytes 24584 | tf_op jit(solution)/shard_map/ppermute | solution.py:453
  26.3 1.4 %shard_map.78 = (bf16[512,256]{1,0:T(8,128)(2,1)S(1)}, f32[512,256]{1,0:T(8,128)S(1)}) custom-call(s32[3]{0:T(128)S(1)} %pad_add_fusion.ids, bf16[512,2048]{1,0:T(8,128)(2,1)S(1)} %copy-done.2, bf16[2,1024,1280]{2,1,0:T(8,128)(2,1)S(1)} %bitcast.33, bf16[2,1024,1280]{2,1,0:T(8,128)(2,1)S(1)} %bitcast.34, bf16[2,1024,1280]{2,1,0:T(8,128)(2,1)S(1)} %bitcast.35, ...), custom_call_target="tpu_custom_call" | custom-call | flops 536870912 | bytes 2097152 | tf_op jit(solution)/shard_map/pallas_call | solution.py:228
  28.8 1.4 %shard_map.80 = (bf16[512,256]{1,0:T(8,128)(2,1)S(1)}, f32[512,256]{1,0:T(8,128)S(1)}) custom-call(s32[3]{0:T(128)S(1)} %pad_add_fusion.ids, bf16[512,2048]{1,0:T(8,128)(2,1)S(1)} %copy-done.2, bf16[2,1024,1280]{2,1,0:T(8,128)(2,1)S(1)} %bitcast.37, bf16[2,1024,1280]{2,1,0:T(8,128)(2,1)S(1)} %bitcast.38, bf16[2,1024,1280]{2,1,0:T(8,128)(2,1)S(1)} %bitcast.39, ...), custom_call_target="tpu_custom_call" | custom-call | flops 536870912 | bytes 2097152 | tf_op jit(solution)/shard_map/pallas_call | solution.py:228
  30.2 1.8 %collective-permute-start.5 = (bf16[512,256]{1,0:T(8,128)(2,1)S(1)}, bf16[512,256]{1,0:T(8,128)(2,1)S(1)}, u32[]{:S(2)}, u32[]{:S(2)}) collective-permute-start(bf16[512,256]{1,0:T(8,128)(2,1)S(1)} %get-tuple-element.30), channel_id=1, source_target_pairs={{0,8},{8,0},{16,24},{24,16},{1,9},{9,1},{17,25},{25,17},{2,10},{10... | collective-permute-start | bytes 786440 | tf_op jit(solution)/shard_map/ppermute | solution.py:453
  31.9 1.4 %shard_map.82 = (bf16[512,256]{1,0:T(8,128)(2,1)S(1)}, f32[512,256]{1,0:T(8,128)S(1)}) custom-call(s32[3]{0:T(128)S(1)} %pad_add_fusion.ids, bf16[512,2048]{1,0:T(8,128)(2,1)S(1)} %copy-done.2, bf16[2,1024,1280]{2,1,0:T(8,128)(2,1)S(1)} %bitcast.41, bf16[2,1024,1280]{2,1,0:T(8,128)(2,1)S(1)} %bitcast.42, bf16[2,1024,1280]{2,1,0:T(8,128)(2,1)S(1)} %bitcast.43, ...), custom_call_target="tpu_custom_call" | custom-call | flops 536870912 | bytes 2097152 | tf_op jit(solution)/shard_map/pallas_call | solution.py:228
  33.3 1.6 %collective-permute-start.8 = (bf16[512,256]{1,0:T(8,128)(2,1)S(1)}, bf16[512,256]{1,0:T(8,128)(2,1)S(1)}, u32[]{:S(2)}, u32[]{:S(2)}) collective-permute-start(bf16[512,256]{1,0:T(8,128)(2,1)S(1)} %get-tuple-element.32), channel_id=1, source_target_pairs={{0,16},{8,24},{16,0},{24,8},{1,17},{9,25},{17,1},{25,9},{2,18},{10... | collective-permute-start | bytes 786440 | tf_op jit(solution)/shard_map/ppermute | solution.py:452
  34.9 1.4 %shard_map.87 = (bf16[512,256]{1,0:T(8,128)(2,1)S(1)}, f32[512,256]{1,0:T(8,128)S(1)}) custom-call(s32[3]{0:T(128)S(1)} %pad_add_fusion.ids, bf16[512,2048]{1,0:T(8,128)(2,1)S(1)} %copy-done.2, bf16[2,1024,1280]{2,1,0:T(8,128)(2,1)S(1)} %bitcast.45, bf16[2,1024,1280]{2,1,0:T(8,128)(2,1)S(1)} %bitcast.46, bf16[2,1024,1280]{2,1,0:T(8,128)(2,1)S(1)} %bitcast.47, ...), custom_call_target="tpu_custom_call" | custom-call | flops 536870912 | bytes 2097152 | tf_op jit(solution)/shard_map/pallas_call | solution.py:228
  36.8 1.4 %shard_map.89 = (bf16[512,256]{1,0:T(8,128)(2,1)S(1)}, f32[512,256]{1,0:T(8,128)S(1)}) custom-call(s32[3]{0:T(128)S(1)} %pad_add_fusion.ids, bf16[512,2048]{1,0:T(8,128)(2,1)S(1)} %copy-done.2, bf16[2,1024,1280]{2,1,0:T(8,128)(2,1)S(1)} %bitcast.49, bf16[2,1024,1280]{2,1,0:T(8,128)(2,1)S(1)} %bitcast.50, bf16[2,1024,1280]{2,1,0:T(8,128)(2,1)S(1)} %bitcast.51, ...), custom_call_target="tpu_custom_call" | custom-call | flops 536870912 | bytes 2097152 | tf_op jit(solution)/shard_map/pallas_call | solution.py:228
  38.6 1.8 %collective-permute-start.3 = (bf16[512,128]{1,0:T(8,128)(2,1)S(1)}, bf16[512,128]{1,0:T(8,128)(2,1)S(1)}, u32[]{:S(2)}, u32[]{:S(2)}) collective-permute-start(bf16[512,128]{1,0:T(8,128)(2,1)S(1)} %add_convert_fusion.4), channel_id=1, source_target_pairs={{0,8},{8,0},{16,24},{24,16},{1,9},{9,1},{17,25},{25,17},{2,10},{10... | collective-permute-start | bytes 393224 | tf_op jit(solution)/shard_map/ppermute | solution.py:453
  40.4 2.7 %collective-permute-done.8.u_ref = bf16[512,256]{1,0:T(8,128)(2,1)S(1)} collective-permute-done((bf16[512,256]{1,0:T(8,128)(2,1)S(1)}, bf16[512,256]{1,0:T(8,128)(2,1)S(1)}, u32[]{:S(2)}, u32[]{:S(2)}) %collective-permute-start.8) | collective-permute-done | bytes 262176 | tf_op jit(solution)/shard_map/ppermute | solution.py:452
  43.1 1.8 %collective-permute-start.9 = (bf16[512,256]{1,0:T(8,128)(2,1)S(1)}, bf16[512,256]{1,0:T(8,128)(2,1)S(1)}, u32[]{:S(2)}, u32[]{:S(2)}) collective-permute-start(bf16[512,256]{1,0:T(8,128)(2,1)S(1)} %add_convert_fusion), channel_id=1, source_target_pairs={{0,8},{8,0},{16,24},{24,16},{1,9},{9,1},{17,25},{25,17},{2,10},{10... | collective-permute-start | bytes 786440 | tf_op jit(solution)/shard_map/ppermute | solution.py:453
  44.9 2.3 %collective-permute-done.15.refs_1_ = bf16[512,256]{1,0:T(8,128)(2,1)S(1)} collective-permute-done((bf16[512,256]{1,0:T(8,128)(2,1)S(1)}, bf16[512,256]{1,0:T(8,128)(2,1)S(1)}, u32[]{:S(2)}, u32[]{:S(2)}) %collective-permute-start.15) | collective-permute-done | bytes 262176 | tf_op jit(solution)/shard_map/ppermute | solution.py:452
  47.2 1.4 %collective-permute-start.16 = (bf16[512,128]{1,0:T(8,128)(2,1)S(1)}, bf16[512,128]{1,0:T(8,128)(2,1)S(1)}, u32[]{:S(2)}, u32[]{:S(2)}) collective-permute-start(bf16[512,128]{1,0:T(8,128)(2,1)S(1)} %add_convert_fusion.2), channel_id=1, source_target_pairs={{0,8},{8,0},{16,24},{24,16},{1,9},{9,1},{17,25},{25,17},{2,10},{10... | collective-permute-start | bytes 393224 | tf_op jit(solution)/shard_map/ppermute | solution.py:453
  49.2 5.1 %collective-permute-done.9.z_ref = bf16[512,256]{1,0:T(8,128)(2,1)S(1)} collective-permute-done((bf16[512,256]{1,0:T(8,128)(2,1)S(1)}, bf16[512,256]{1,0:T(8,128)(2,1)S(1)}, u32[]{:S(2)}, u32[]{:S(2)}) %collective-permute-start.9) | collective-permute-done | bytes 262176 | tf_op jit(solution)/shard_map/ppermute | solution.py:453
  54.5 1.3 %collective-permute-start.10 = (bf16[512,256]{1,0:T(8,128)(2,1)S(1)}, bf16[512,256]{1,0:T(8,128)(2,1)S(1)}, u32[]{:S(2)}, u32[]{:S(2)}) collective-permute-start(bf16[512,256]{1,0:T(8,128)(2,1)S(1)} %get-tuple-element.33.rotv_ref.refs_8_), channel_id=1, source_target_pairs={{0,4},{1,5},{2,6},{3,7},{8,12},{9,13},{10,14},{11,15},{16,20},{17,... | collective-permute-start | bytes 786440 | tf_op jit(solution)/shard_map/ppermute | solution.py:507
  55.8 2.9 %shard_map.84 = (f32[4,512]{1,0:T(4,128)S(1)}, f32[512,4]{1,0:T(8,128)S(1)}, f32[4,512]{1,0:T(4,128)S(1)}, f32[4,128,128]{2,1,0:T(8,128)S(1)}, bf16[4,128,128]{2,1,0:T(8,128)(2,1)S(1)}) custom-call(f32[4,512]{1,0:T(4,128)S(1)} %dynamic-slice_add_fusion.1.raw_ref, f32[4,1]{1,0:T(4,128)S(1)} %copy.9.bias_ref, f32[4,1]{1,0:T(4,128)S(1)} %copy.10.rate_ref, ...), custom_call_target="tpu_custom_call" | custom-call | flops 1000000000 | bytes 1000000 | tf_op jit(solution)/shard_map/pallas_call | solution.py:341
  58.7 1.5 %collective-permute-start.13 = (bf16[4,128,128]{2,1,0:T(8,128)(2,1)S(1)}, bf16[4,128,128]{2,1,0:T(8,128)(2,1)S(1)}, u32[]{:S(2)}, u32[]{:S(2)}) collective-permute-start(bf16[4,128,128]{2,1,0:T(8,128)(2,1)S(1)} %get-tuple-element.39), channel_id=1, source_target_pairs={{0,4},{1,5},{2,6},{3,7},{8,12},{9,13},{10,14},{11,15},{16,20},{17,... | collective-permute-start | bytes 393224 | tf_op jit(solution)/shard_map/ppermute | solution.py:511
  60.3 1.6 %collective-permute-start.6 = (bf16[512,128]{1,0:T(8,128)(2,1)S(1)}, bf16[512,128]{1,0:T(8,128)(2,1)S(1)}, u32[]{:S(2)}, u32[]{:S(2)}) collective-permute-start(bf16[512,128]{1,0:T(8,128)(2,1)S(1)} %add_convert_fusion.3), channel_id=1, source_target_pairs={{0,16},{8,24},{16,0},{24,8},{1,17},{9,25},{17,1},{25,9},{2,18},{10... | collective-permute-start | bytes 393224 | tf_op jit(solution)/shard_map/ppermute | solution.py:452
  61.9 3.7 %shard_map.90 = (bf16[512,128]{1,0:T(8,128)(2,1)S(1)}, bf16[512,128]{1,0:T(8,128)(2,1)S(1)}, bf16[512,128]{1,0:T(8,128)(2,1)S(1)}, bf16[512,128]{1,0:T(8,128)(2,1)S(1)}) custom-call(s32[3]{0:T(128)S(1)} %pad_add_fusion.ids, f32[512,256]{1,0:T(8,128)S(1)} %get-tuple-element.41.refs_0_, bf16[512,256]{1,0:T(8,128)(2,1)S(1)} %collective-permute-done.15.refs_1_, ...), custom_call_target="tpu_custom_call" | custom-call | flops 2000000000 | bytes 3000000 | tf_op jit(solution)/shard_map/pallas_call | solution.py:424
  65.6 3.7 %shard_map.85 = (bf16[512,128]{1,0:T(8,128)(2,1)S(1)}, bf16[512,128]{1,0:T(8,128)(2,1)S(1)}, bf16[512,128]{1,0:T(8,128)(2,1)S(1)}, bf16[512,128]{1,0:T(8,128)(2,1)S(1)}) custom-call(s32[3]{0:T(128)S(1)} %pad_add_fusion.ids, f32[512,256]{1,0:T(8,128)S(1)} %get-tuple-element.27.refs_0_, bf16[512,256]{1,0:T(8,128)(2,1)S(1)} %collective-permute-done.2.refs_1_, ...), custom_call_target="tpu_custom_call" | custom-call | flops 2000000000 | bytes 3000000 | tf_op jit(solution)/shard_map/pallas_call | solution.py:424
  69.3 0.9 %pad_maximum_fusion = bf16[512,512]{1,0:T(8,128)(2,1)} fusion(bf16[512,128]{1,0:T(8,128)(2,1)S(1)} %get-tuple-element.47, bf16[512,128]{1,0:T(8,128)(2,1)S(1)} %get-tuple-element.46, bf16[512,128]{1,0:T(8,128)(2,1)S(1)} %get-tuple-element.45, bf16[512,128]{1,0:T(8,128)(2,1)S(1)} %get-tuple-element.40), kind=kLoop, calls=%fused_computation.1 | loop fusion | flops 2097152 | bytes 1048576 | tf_op jit(solution)/shard_map/concatenate | solution.py:524
  70.2 0.9 %pad_maximum_fusion.1 = bf16[512,512]{1,0:T(8,128)(2,1)} fusion(bf16[512,128]{1,0:T(8,128)(2,1)S(1)} %get-tuple-element.51, bf16[512,128]{1,0:T(8,128)(2,1)S(1)} %get-tuple-element.50, bf16[512,128]{1,0:T(8,128)(2,1)S(1)} %get-tuple-element.49, bf16[512,128]{1,0:T(8,128)(2,1)S(1)} %get-tuple-element.48), kind=kLoop, calls=%fused_computation.2 | loop fusion | flops 2097152 | bytes 1048576 | tf_op jit(solution)/shard_map/concatenate | solution.py:524
  (60 shorter events, 6.3 us)
Async XLA Ops:
  0.6 3.0 %copy-start = (bf16[2048,16]{0,1:T(8,128)(2,1)S(1)}, bf16[2048,16]{0,1:T(8,128)(2,1)}, u32[]{:S(2)}) copy-start(bf16[2048,16]{0,1:T(8,128)(2,1)} %param.8) | copy-start | bytes 196612
  0.6 3.0 %copy-start.2 = (bf16[512,2048]{1,0:T(8,128)(2,1)S(1)}, bf16[512,2048]{1,0:T(8,128)(2,1)}, u32[]{:S(2)}) copy-start(bf16[512,2048]{1,0:T(8,128)(2,1)} %x_ref.9) | copy-start | bytes 6291460
  0.7 6.1 %copy-start.4 = (f32[4]{0:T(128)S(1)}, f32[4]{0:T(128)}, u32[]{:S(2)}) copy-start(f32[4]{0:T(128)} %param.9) | copy-start | bytes 52
  0.7 6.2 %copy-start.5 = (f32[4]{0:T(128)S(1)}, f32[4]{0:T(128)}, u32[]{:S(2)}) copy-start(f32[4]{0:T(128)} %param.10) | copy-start | bytes 52
  3.1 10.6 %collective-permute-start = (bf16[512,1024]{1,0:T(8,128)(2,1)}, bf16[512,1024]{1,0:T(8,128)(2,1)S(1)}, u32[]{:S(2)}, u32[]{:S(2)}) collective-permute-start(bf16[512,1024]{1,0:T(8,128)(2,1)} %constant_dynamic-slice_fusion.2), channel_id=1, source_target_pairs={{0,4},{4,0},{1,5},{5,1},{2,6},{6,2},{3,7},{7,3},{8,12},{12,8},{9,1... | collective-permute-start | bytes 3145736 | tf_op jit(solution)/shard_map/ppermute | solution.py:454
  4.3 13.7 %collective-permute-start.11 = (f32[8,512]{1,0:T(8,128)S(1)}, f32[8,512]{1,0:T(8,128)S(1)}, u32[]{:S(2)}, u32[]{:S(2)}) collective-permute-start(f32[8,512]{1,0:T(8,128)S(1)} %constant_dynamic-slice_fusion.1), channel_id=1, source_target_pairs={{0,16},{8,24},{16,0},{24,8},{1,17},{9,25},{17,1},{25,9},{2,18},{10... | collective-permute-start | bytes 49160 | tf_op jit(solution)/shard_map/ppermute | solution.py:452
  13.8 2.5 %copy-start.1 = (bf16[1024,2,1280]{2,0,1:T(8,128)(2,1)S(1)}, bf16[1024,2,1280]{2,0,1:T(8,128)(2,1)}, u32[]{:S(2)}) copy-start(bf16[1024,2,1280]{2,0,1:T(8,128)(2,1)} %copy.12) | copy-start | bytes 15728644
  17.6 7.1 %collective-permute-start.1 = (bf16[512,512]{1,0:T(8,128)(2,1)S(1)}, bf16[512,512]{1,0:T(8,128)(2,1)S(1)}, u32[]{:S(2)}, u32[]{:S(2)}) collective-permute-start(bf16[512,512]{1,0:T(8,128)(2,1)S(1)} %shard_map.77), channel_id=1, source_target_pairs={{0,4},{4,0},{1,5},{5,1},{2,6},{6,2},{3,7},{7,3},{8,12},{12,8},{9,1... | collective-permute-start | bytes 1572872 | tf_op jit(solution)/shard_map/ppermute | solution.py:454
  19.3 9.5 %collective-permute-start.4 = (bf16[512,512]{1,0:T(8,128)(2,1)S(1)}, bf16[512,512]{1,0:T(8,128)(2,1)S(1)}, u32[]{:S(2)}, u32[]{:S(2)}) collective-permute-start(bf16[512,512]{1,0:T(8,128)(2,1)S(1)} %shard_map.79), channel_id=1, source_target_pairs={{0,4},{4,0},{1,5},{5,1},{2,6},{6,2},{3,7},{7,3},{8,12},{12,8},{9,1... | collective-permute-start | bytes 1572872 | tf_op jit(solution)/shard_map/ppermute | solution.py:454
  21.0 10.9 %collective-permute-start.7 = (bf16[512,512]{1,0:T(8,128)(2,1)S(1)}, bf16[512,512]{1,0:T(8,128)(2,1)S(1)}, u32[]{:S(2)}, u32[]{:S(2)}) collective-permute-start(bf16[512,512]{1,0:T(8,128)(2,1)S(1)} %shard_map.81), channel_id=1, source_target_pairs={{0,4},{4,0},{1,5},{5,1},{2,6},{6,2},{3,7},{7,3},{8,12},{12,8},{9,1... | collective-permute-start | bytes 1572872 | tf_op jit(solution)/shard_map/ppermute | solution.py:454
  21.3 5.0 %slice-start = ((s8[5242880]{0:T(1024)(128)(4,1)}), s8[4194304]{0:T(1024)(128)(4,1)S(1)}, s32[]{:S(2)}) async-start(s8[5242880]{0:T(1024)(128)(4,1)} %bitcast.31), calls=%async_computation | async-start | bytes 8388608
  22.7 3.6 %slice-start.1 = ((s8[5242880]{0:T(1024)(128)(4,1)}), s8[1048576]{0:T(1024)(128)(4,1)S(1)}, s32[]{:S(2)}) async-start(s8[5242880]{0:T(1024)(128)(4,1)} %bitcast.31), calls=%async_computation.1 | async-start | bytes 2097152
  22.7 12.1 %collective-permute-start.14 = (bf16[512,512]{1,0:T(8,128)(2,1)S(1)}, bf16[512,512]{1,0:T(8,128)(2,1)S(1)}, u32[]{:S(2)}, u32[]{:S(2)}) collective-permute-start(bf16[512,512]{1,0:T(8,128)(2,1)S(1)} %shard_map.86), channel_id=1, source_target_pairs={{0,4},{4,0},{1,5},{5,1},{2,6},{6,2},{3,7},{7,3},{8,12},{12,8},{9,1... | collective-permute-start | bytes 1572872 | tf_op jit(solution)/shard_map/ppermute | solution.py:454
  24.5 12.4 %collective-permute-start.17 = (bf16[512,512]{1,0:T(8,128)(2,1)S(1)}, bf16[512,512]{1,0:T(8,128)(2,1)S(1)}, u32[]{:S(2)}, u32[]{:S(2)}) collective-permute-start(bf16[512,512]{1,0:T(8,128)(2,1)S(1)} %shard_map.88), channel_id=1, source_target_pairs={{0,4},{4,0},{1,5},{5,1},{2,6},{6,2},{3,7},{7,3},{8,12},{12,8},{9,1... | collective-permute-start | bytes 1572872 | tf_op jit(solution)/shard_map/ppermute | solution.py:454
  24.8 3.7 %collective-permute-start.12 = (f32[4,512]{1,0:T(4,128)S(1)}, f32[4,512]{1,0:T(4,128)S(1)}, u32[]{:S(2)}, u32[]{:S(2)}) collective-permute-start(f32[4,512]{1,0:T(4,128)S(1)} %constant_dynamic-slice_fusion), channel_id=1, source_target_pairs={{0,8},{8,0},{16,24},{24,16},{1,9},{9,1},{17,25},{25,17},{2,10},{10... | collective-permute-start | bytes 24584 | tf_op jit(solution)/shard_map/ppermute | solution.py:453
  28.5 10.1 %collective-permute-start.2 = (bf16[512,256]{1,0:T(8,128)(2,1)S(1)}, bf16[512,256]{1,0:T(8,128)(2,1)S(1)}, u32[]{:S(2)}, u32[]{:S(2)}) collective-permute-start(bf16[512,256]{1,0:T(8,128)(2,1)S(1)} %get-tuple-element.28), channel_id=1, source_target_pairs={{0,16},{8,24},{16,0},{24,8},{1,17},{9,25},{17,1},{25,9},{2,18},{10... | collective-permute-start | bytes 786440 | tf_op jit(solution)/shard_map/ppermute | solution.py:452
  30.2 28.6 %collective-permute-start.5 = (bf16[512,256]{1,0:T(8,128)(2,1)S(1)}, bf16[512,256]{1,0:T(8,128)(2,1)S(1)}, u32[]{:S(2)}, u32[]{:S(2)}) collective-permute-start(bf16[512,256]{1,0:T(8,128)(2,1)S(1)} %get-tuple-element.30), channel_id=1, source_target_pairs={{0,8},{8,0},{16,24},{24,16},{1,9},{9,1},{17,25},{25,17},{2,10},{10... | collective-permute-start | bytes 786440 | tf_op jit(solution)/shard_map/ppermute | solution.py:453
  33.3 9.8 %collective-permute-start.8 = (bf16[512,256]{1,0:T(8,128)(2,1)S(1)}, bf16[512,256]{1,0:T(8,128)(2,1)S(1)}, u32[]{:S(2)}, u32[]{:S(2)}) collective-permute-start(bf16[512,256]{1,0:T(8,128)(2,1)S(1)} %get-tuple-element.32), channel_id=1, source_target_pairs={{0,16},{8,24},{16,0},{24,8},{1,17},{9,25},{17,1},{25,9},{2,18},{10... | collective-permute-start | bytes 786440 | tf_op jit(solution)/shard_map/ppermute | solution.py:452
  36.2 11.0 %collective-permute-start.15 = (bf16[512,256]{1,0:T(8,128)(2,1)S(1)}, bf16[512,256]{1,0:T(8,128)(2,1)S(1)}, u32[]{:S(2)}, u32[]{:S(2)}) collective-permute-start(bf16[512,256]{1,0:T(8,128)(2,1)S(1)} %get-tuple-element.42), channel_id=1, source_target_pairs={{0,16},{8,24},{16,0},{24,8},{1,17},{9,25},{17,1},{25,9},{2,18},{10... | collective-permute-start | bytes 786440 | tf_op jit(solution)/shard_map/ppermute | solution.py:452
  38.2 10.4 %collective-permute-start.18 = (bf16[512,256]{1,0:T(8,128)(2,1)S(1)}, bf16[512,256]{1,0:T(8,128)(2,1)S(1)}, u32[]{:S(2)}, u32[]{:S(2)}) collective-permute-start(bf16[512,256]{1,0:T(8,128)(2,1)S(1)} %get-tuple-element.44), channel_id=1, source_target_pairs={{0,8},{8,0},{16,24},{24,16},{1,9},{9,1},{17,25},{25,17},{2,10},{10... | collective-permute-start | bytes 786440 | tf_op jit(solution)/shard_map/ppermute | solution.py:453
  38.6 27.0 %collective-permute-start.3 = (bf16[512,128]{1,0:T(8,128)(2,1)S(1)}, bf16[512,128]{1,0:T(8,128)(2,1)S(1)}, u32[]{:S(2)}, u32[]{:S(2)}) collective-permute-start(bf16[512,128]{1,0:T(8,128)(2,1)S(1)} %add_convert_fusion.4), channel_id=1, source_target_pairs={{0,8},{8,0},{16,24},{24,16},{1,9},{9,1},{17,25},{25,17},{2,10},{10... | collective-permute-start | bytes 393224 | tf_op jit(solution)/shard_map/ppermute | solution.py:453
  43.1 11.2 %collective-permute-start.9 = (bf16[512,256]{1,0:T(8,128)(2,1)S(1)}, bf16[512,256]{1,0:T(8,128)(2,1)S(1)}, u32[]{:S(2)}, u32[]{:S(2)}) collective-permute-start(bf16[512,256]{1,0:T(8,128)(2,1)S(1)} %add_convert_fusion), channel_id=1, source_target_pairs={{0,8},{8,0},{16,24},{24,16},{1,9},{9,1},{17,25},{25,17},{2,10},{10... | collective-permute-start | bytes 786440 | tf_op jit(solution)/shard_map/ppermute | solution.py:453
  47.2 13.0 %collective-permute-start.16 = (bf16[512,128]{1,0:T(8,128)(2,1)S(1)}, bf16[512,128]{1,0:T(8,128)(2,1)S(1)}, u32[]{:S(2)}, u32[]{:S(2)}) collective-permute-start(bf16[512,128]{1,0:T(8,128)(2,1)S(1)} %add_convert_fusion.2), channel_id=1, source_target_pairs={{0,8},{8,0},{16,24},{24,16},{1,9},{9,1},{17,25},{25,17},{2,10},{10... | collective-permute-start | bytes 393224 | tf_op jit(solution)/shard_map/ppermute | solution.py:453
  48.7 13.2 %collective-permute-start.19 = (bf16[512,128]{1,0:T(8,128)(2,1)S(1)}, bf16[512,128]{1,0:T(8,128)(2,1)S(1)}, u32[]{:S(2)}, u32[]{:S(2)}) collective-permute-start(bf16[512,128]{1,0:T(8,128)(2,1)S(1)} %add_convert_fusion.1), channel_id=1, source_target_pairs={{0,16},{8,24},{16,0},{24,8},{1,17},{9,25},{17,1},{25,9},{2,18},{10... | collective-permute-start | bytes 393224 | tf_op jit(solution)/shard_map/ppermute | solution.py:452
  54.5 7.4 %collective-permute-start.10 = (bf16[512,256]{1,0:T(8,128)(2,1)S(1)}, bf16[512,256]{1,0:T(8,128)(2,1)S(1)}, u32[]{:S(2)}, u32[]{:S(2)}) collective-permute-start(bf16[512,256]{1,0:T(8,128)(2,1)S(1)} %get-tuple-element.33.rotv_ref.refs_8_), channel_id=1, source_target_pairs={{0,4},{1,5},{2,6},{3,7},{8,12},{9,13},{10,14},{11,15},{16,20},{17,... | collective-permute-start | bytes 786440 | tf_op jit(solution)/shard_map/ppermute | solution.py:507
  55.8 6.1 %copy-start.3 = (f32[4]{0:T(128)S(1)}, f32[4]{0:T(128)}, u32[]{:S(2)}) copy-start(f32[4]{0:T(128)} %param.11) | copy-start | bytes 52
  58.7 3.1 %collective-permute-start.13 = (bf16[4,128,128]{2,1,0:T(8,128)(2,1)S(1)}, bf16[4,128,128]{2,1,0:T(8,128)(2,1)S(1)}, u32[]{:S(2)}, u32[]{:S(2)}) collective-permute-start(bf16[4,128,128]{2,1,0:T(8,128)(2,1)S(1)} %get-tuple-element.39), channel_id=1, source_target_pairs={{0,4},{1,5},{2,6},{3,7},{8,12},{9,13},{10,14},{11,15},{16,20},{17,... | collective-permute-start | bytes 393224 | tf_op jit(solution)/shard_map/ppermute | solution.py:511
  60.3 5.4 %collective-permute-start.6 = (bf16[512,128]{1,0:T(8,128)(2,1)S(1)}, bf16[512,128]{1,0:T(8,128)(2,1)S(1)}, u32[]{:S(2)}, u32[]{:S(2)}) collective-permute-start(bf16[512,128]{1,0:T(8,128)(2,1)S(1)} %add_convert_fusion.3), channel_id=1, source_target_pairs={{0,16},{8,24},{16,0},{24,8},{1,17},{9,25},{17,1},{25,9},{2,18},{10... | collective-permute-start | bytes 393224 | tf_op jit(solution)/shard_map/ppermute | solution.py:452

commit v2 on v0

--- a/solution.py
+++ b/solution.py
@@ -1,7 +1,13 @@
+import functools
+import math
+
 import jax
 import jax.numpy as jnp
 from jax import lax
+from jax.experimental import pallas as pl
+from jax.experimental.pallas import tpu as pltpu
 from jax.sharding import PartitionSpec as P
+
 
 HEADS = 64
 KV_HEADS = 8
@@ -93,7 +99,7 @@
         jnp.zeros((tok, heads_local), jnp.float32),
         jnp.zeros((tok, heads_local, HEAD_DIM), jnp.float32),
     )
-    top, total, accum = key_absorber(
+    _, total, accum = key_absorber(
         rot_query,
         own_first,
         scale,
@@ -166,6 +172,455 @@
     return (teacher, student)
 
 
+LANES = 128
+EXTRA = 16
+VMEM_GRANT = 24 * 1024 * 1024
+F32 = jnp.float32
+BF16 = jnp.bfloat16
+LAST = (((1,), (1,)), ((), ()))
+
+
+def cost(flops, moved):
+    return pl.CostEstimate(flops=flops, bytes_accessed=moved, transcendentals=0)
+
+
+def joined(refs):
+    return jnp.concatenate([ref[(0,) * (len(ref.shape) - 2)] for ref in refs], axis=1)
+
+
+def project_kernel(ids, x_ref, w0, w1, w2, w3, out_ref):
+    out_ref[...] = jnp.dot(
+        x_ref[...], joined((w0, w1, w2, w3)), preferred_element_type=F32
+    ).astype(BF16)
+
+
+def add_halves(x_ref, w0, w1, w2, w3, r_ref, send_ref, keep_ref):
+    tok, half = keep_ref.shape
+    first = jnp.dot(x_ref[...], joined((w0, w1)), preferred_element_type=F32)
+    send_ref[:tok, :] = (first + r_ref[:, :half].astype(F32)).astype(BF16)
+    second = jnp.dot(x_ref[...], joined((w2, w3)), preferred_element_type=F32)
+    keep_ref[...] = second + r_ref[:, half:].astype(F32)
+
+
+def project_add_kernel(ids, *refs):
+    add_halves(*refs)
+
+
+def folded(rates):
+    half = rates.shape[1] // 2
+    return jnp.concatenate([rates[:, :half], rates[:, half:]], axis=0)
+
+
+def unfolded(rows):
+    half = rows.shape[0] // 2
+    return jnp.concatenate([rows[:half], rows[half:]], axis=1)
+
+
+def project_pair_kernel(ids, raw_ref, *refs):
+    add_halves(*refs)
+    send_ref, tok = refs[-2], refs[-1].shape[0]
+    away = EXTRA // 2
+    rates = jnp.where(ids[0] == 0, raw_ref[away:, :], raw_ref[:away, :])
+    send_ref[tok:, :] = folded(rates).astype(BF16)
+
+
+def own_rates(ids, raw_ref, u_ref):
+    tok = raw_ref.shape[1]
+    own = EXTRA // 2
+    rates = jnp.where(ids[0] == 0, raw_ref[:own, :], raw_ref[own:, :])
+    return rates + unfolded(u_ref[tok:, :].astype(F32))
+
+
+def pair_middle_kernel(ids, raw_ref, keep_ref, u_ref, send_ref):
+    tok = keep_ref.shape[0]
+    send_ref[:tok, :] = (keep_ref[...] + u_ref[:tok, :].astype(F32)).astype(BF16)
+    send_ref[tok:, :] = folded(own_rates(ids, raw_ref, u_ref)).astype(BF16)
+
+
+def middle_kernel(ids, keep_ref, u_ref, send_ref):
+    send_ref[...] = (keep_ref[...] + u_ref[...].astype(F32)).astype(BF16)
+
+
+def prepare_kernel(ids, x_ref, rates_ref, raw_ref, cos_ref, sin_ref):
+    raw_ref[...] = lax.dot_general(
+        rates_ref[...], x_ref[...], LAST, preferred_element_type=F32
+    )
+    tok, wide = cos_ref.shape
+    half = wide // 2
+    row = lax.broadcasted_iota(jnp.int32, (tok, wide), 0) + ids[2] * tok
+    lane = lax.broadcasted_iota(jnp.int32, (1, wide), 1)
+    slot = jnp.where(lane < half, lane, lane - half).astype(F32)
+    freq = jnp.exp(slot * (-2.0 / wide * math.log(ROPE_BASE)))
+    angle = row.astype(F32) * freq
+    cos_ref[...] = jnp.cos(angle)
+    sine = jnp.sin(angle)
+    sin_ref[...] = jnp.where(lane < half, -sine, sine)
+
+
+def weight_spec(weights, place):
+    ndim = weights.ndim
+    block = (1,) * (ndim - 2) + (weights.shape[-2], LANES)
+    return pl.BlockSpec(block, lambda step, ids: place(ids[0], ids[1]))
+
+
+def flat(shape):
+    return pl.BlockSpec(shape, lambda step, ids, n=len(shape): (0,) * n)
+
+
+def call(kernel, ids, specs, args, shapes, flops, aliases={}, out_specs=None):
+    return pl.pallas_call(
+        kernel,
+        grid_spec=pltpu.PrefetchScalarGridSpec(
+            num_scalar_prefetch=1,
+            grid=(1,),
+            in_specs=specs,
+            out_specs=out_specs or [flat(s) for s, _ in shapes],
+        ),
+        out_shape=[jax.ShapeDtypeStruct(s, d) for s, d in shapes],
+        input_output_aliases=aliases,
+        compiler_params=pltpu.CompilerParams(vmem_limit_bytes=VMEM_GRANT),
+        cost_estimate=cost(flops, 3 * 10**6),
+    )(ids, *args)
+
+
+def project(ids, x, x_block, weights, places):
+    tok, rows = x.shape[0], weights.shape[-2]
+    wide = len(places) * LANES
+    specs = [pl.BlockSpec((tok, rows), x_block)]
+    specs += [weight_spec(weights, place) for place in places]
+    args = [x] + [weights] * len(places)
+    return call(project_kernel, ids, specs, args, [((tok, wide), BF16)], 2 * tok * rows * wide)[0]
+
+
+def project_add(ids, x, x_block, weights, places, received, raw=None):
+    tok, rows = x.shape[0], weights.shape[-2]
+    wide = len(places) * LANES
+    half = wide // 2
+    specs = [pl.BlockSpec((tok, rows), x_block)]
+    specs += [weight_spec(weights, place) for place in places] + [flat(received.shape)]
+    args = [x] + [weights] * len(places) + [received]
+    tall, kernel = tok, project_add_kernel
+    if raw is not None:
+        specs, args = [flat(raw.shape)] + specs, [raw] + args
+        tall, kernel = tok + EXTRA, project_pair_kernel
+    shapes = [((tall, half), BF16), ((tok, half), F32)]
+    return call(kernel, ids, specs, args, shapes, 2 * tok * rows * wide)
+
+
+def turn(vectors, cosine, sine):
+    return vectors * cosine + pltpu.roll(vectors, HEAD_DIM // 2, 1) * sine
+
+
+def split_sum(rows, mask):
+    high = rows.astype(BF16)
+    rest = rows - high.astype(F32)
+    middle = rest.astype(BF16)
+    low = (rest - middle.astype(F32)).astype(BF16)
+    count = rows.shape[0]
+    parts = jnp.concatenate([high.astype(F32), middle.astype(F32), low.astype(F32)], axis=0)
+    sums = lax.dot_general(parts.astype(BF16), mask, LAST, preferred_element_type=F32)
+    return sums[:count] + (sums[count : 2 * count] + sums[2 * count :])
+
+
+def context_kernel(
+    stretch, ids, raw_ref, keep_ref, u_ref, z_ref, cos_ref, sin_ref, bias_ref, rate_ref,
+    carry_ref, bterm_ref, across_ref, down_ref, step_ref, first_ref,
+):
+    tok = keep_ref.shape[0]
+    heads = bias_ref.shape[0]
+    spans = tok // stretch
+    pair = keep_ref[...] + u_ref[:tok, :].astype(F32) + z_ref[:tok, :].astype(F32)
+    keys = pair[:, :HEAD_DIM]
+    values = pair[:, HEAD_DIM:].astype(BF16)
+    bterm = keys.astype(BF16)
+    carry_ref[:tok, :HEAD_DIM] = turn(keys, cos_ref[...], sin_ref[...]).astype(BF16)
+    carry_ref[:tok, HEAD_DIM:] = values
+    bterm_ref[...] = bterm
+    both = own_rates(ids, raw_ref, u_ref) + unfolded(z_ref[tok:, :].astype(F32))
+    raw = jnp.where(ids[1] == 0, both[:heads], both[heads:])
+    step = jax.nn.softplus(raw + bias_ref[...])
+    decay = -rate_ref[...] * step
+    rows = lax.broadcasted_iota(jnp.int32, (stretch, stretch), 0)
+    cols = lax.broadcasted_iota(jnp.int32, (stretch, stretch), 1)
+    below = (cols <= rows).astype(F32).astype(BF16)
+    fold = lambda a: jnp.concatenate([a[:, i * stretch : (i + 1) * stretch] for i in range(spans)], axis=0)
+    across = split_sum(fold(decay), below)
+    steps = fold(step)
+    tails = jnp.exp(across[:, stretch - 1 :] - across) * steps
+    across_ref[...] = across
+    step_ref[...] = steps
+    count = heads * spans
+    filler = jnp.zeros((LANES - 2 * count, stretch), F32)
+    down = jnp.transpose(jnp.concatenate([across, tails, filler], axis=0))
+    down_ref[...] = down
+    states = [None] * heads
+    for index in range(spans):
+        span = slice(index * stretch, (index + 1) * stretch)
+        part = bterm[span].astype(F32)
+        weighted = jnp.concatenate(
+            [
+                (part * down[:, count + index * heads + h : count + index * heads + h + 1]).astype(BF16)
+                for h in range(heads)
+            ],
+            axis=1,
+        )
+        fresh = lax.dot_general(
+            weighted, values[span], (((0,), (0,)), ((), ())), preferred_element_type=F32
+        )
+        for h in range(heads):
+            new = fresh[h * HEAD_DIM : (h + 1) * HEAD_DIM]
+            if index > 0:
+                at = index * heads + h
+                new = new + jnp.exp(across[at : at + 1, stretch - 1 :]) * states[h]
+            else:
+                first_ref[h] = new
+            states[h] = new
+    for h in range(heads):
+        row, col = tok + (h // 2) * HEAD_DIM, (h % 2) * HEAD_DIM
+        carry_ref[row : row + HEAD_DIM, col : col + HEAD_DIM] = states[h].astype(BF16)
+
+
+def heads_kernel(stretch, numbers, ids, *refs):
+    refs = list(refs)
+    pieces = refs[: 3 * len(numbers)]
+    (cos_ref, sin_ref, carry_ref, bterm_ref, came_ref, across_ref, down_ref, step_ref,
+     first_ref, skip_ref) = refs[3 * len(numbers) : 3 * len(numbers) + 10]
+    teacher_ref, student_ref = refs[-2:]
+    tok = bterm_ref.shape[0]
+    heads = first_ref.shape[0]
+    scale = HEAD_DIM ** (-0.5)
+    power = scale * 1.4426950408889634
+    later = (ids[2] > 0).astype(F32)
+    blocked = (1.0 - later) * FAR_BELOW
+    rows = lax.broadcasted_iota(jnp.int32, (stretch, stretch), 0)
+    cols = lax.broadcasted_iota(jnp.int32, (stretch, stretch), 1)
+    causal = cols <= rows
+    ones = jnp.ones((tok, HEAD_DIM), BF16)
+    own_keys = carry_ref[:tok, :HEAD_DIM]
+    prev_keys = came_ref[:tok, :HEAD_DIM]
+    own_values = jnp.concatenate([carry_ref[:tok, HEAD_DIM:], ones], axis=1)
+    prev_values = jnp.concatenate([came_ref[:tok, HEAD_DIM:], ones], axis=1)
+    for at, head in enumerate(numbers):
+        keep_ref, u_ref, z_ref = pieces[3 * at : 3 * at + 3]
+        place = slice(at * HEAD_DIM, (at + 1) * HEAD_DIM)
+        query = keep_ref[...] + u_ref[...].astype(F32) + z_ref[...].astype(F32)
+        turned = turn(query, cos_ref[...], sin_ref[...]).astype(BF16)
+        cterm = query.astype(BF16)
+        row, col = tok + (head // 2) * HEAD_DIM, (head % 2) * HEAD_DIM
+        state = came_ref[row : row + HEAD_DIM, col : col + HEAD_DIM].astype(F32) * later
+        skip = skip_ref[0, head]
+        for index in range(tok // stretch):
+            span = slice(index * stretch, (index + 1) * stretch)
+            reach = (index + 1) * stretch
+            queries = turned[span]
+            far = lax.dot_general(queries, prev_keys, LAST, preferred_element_type=F32) + blocked
+            near = lax.dot_general(queries, own_keys[:reach], LAST, preferred_element_type=F32)
+            diagonal = jnp.where(causal, near[:, index * stretch :], FAR_BELOW)
+            if index > 0:
+                near = jnp.concatenate([near[:, : index * stretch], diagonal], axis=1)
+            else:
+                near = diagonal
+            top = jnp.maximum(
+                jnp.max(far, axis=1, keepdims=True), jnp.max(near, axis=1, keepdims=True)
+            )
+            far = jnp.exp2((far - top) * power).astype(BF16)
+            near = jnp.exp2((near - top) * power).astype(BF16)
+            mixed = jnp.dot(far, prev_values, preferred_element_type=F32) + jnp.dot(
+                near, own_values[:reach], preferred_element_type=F32
+            )
+            teacher_ref[span, place] = (mixed[:, :HEAD_DIM] / mixed[:, HEAD_DIM:]).astype(BF16)
+            values = carry_ref[span, HEAD_DIM:]
+            which = index * heads + head
+            down = down_ref[:, which : which + 1]
+            across = across_ref[which : which + 1, :]
+            gram = lax.dot_general(
+                cterm[span], bterm_ref[span, :], LAST, preferred_element_type=F32
+            ) * (step_ref[which : which + 1, :] * scale)
+            mix = jnp.where(causal, jnp.exp(jnp.where(causal, down - across, -1e4)) * gram, 0.0)
+            inner = jnp.dot(mix.astype(BF16), values, preferred_element_type=F32)
+            high = state.astype(BF16)
+            low = (state - high.astype(F32)).astype(BF16)
+            carried = jnp.dot(
+                cterm[span], jnp.concatenate([high, low], axis=1), preferred_element_type=F32
+            )
+            carried = (carried[:, :HEAD_DIM] + carried[:, HEAD_DIM:]) * (jnp.exp(down) * scale)
+            student_ref[span, place] = (inner + carried + skip * values.astype(F32)).astype(BF16)
+            if index == 0:
+                state = jnp.exp(across[:, stretch - 1 :]) * state + first_ref[head]
+
+
+def heads_call(ids, group_at, numbers, pieces, shared, total, before):
+    tok = pieces[0][0].shape[0]
+    column = lambda col: pl.BlockSpec((tok, LANES), lambda step, ids, col=col: (0, col))
+    specs, args = [], []
+    for keep, u, z in pieces:
+        specs += [column(1), column(1), column(0)]
+        args += [keep, u, z]
+    specs += [flat(a.shape) for a in shared[:-1]] + [pl.BlockSpec(memory_space=pltpu.SMEM)]
+    args += list(shared)
+    aliases = {}
+    if before is not None:
+        aliases = {1 + len(args): 0, 2 + len(args): 1}
+        specs += [pl.BlockSpec(memory_space=pl.ANY)] * 2
+        args += list(before)
+    wide = len(numbers) * LANES
+    block = pl.BlockSpec((tok, wide), lambda step, ids: (0, group_at))
+    return call(
+        functools.partial(heads_kernel, STRETCH, numbers),
+        ids, specs, args, [((tok, total), BF16)] * 2, 2 * 10**9, aliases, [block] * 2,
+    )
+
+
+def pair_body(*args):
+    return pair_steps(*args)
+
+
+def pair_steps(layer_input, attn_weight, rate_weight, rate_bias, decay_rate, skip_gain):
+    tok, _ = layer_input.shape
+    heads = rate_bias.shape[0]
+    group = HEADS // KV_HEADS
+    grp = lax.axis_index("grp")
+    seq = lax.axis_index("seq")
+    ids = jnp.stack([grp // 2, grp % 2, seq]).astype(jnp.int32)
+    count = lax.axis_size("grp")
+    swap_high = [(g, g ^ 2) for g in range(count)]
+    swap_low = [(g, g ^ 1) for g in range(count)]
+    over_high = lambda a: lax.ppermute(a, "grp", swap_high)
+    over_low = lambda a: lax.ppermute(a, "grp", swap_low)
+    over_seq = lambda a: lax.ppermute(a, "seq", [(0, 1), (1, 0)])
+    own_block = lambda step, ids: (0, ids[2])
+
+    other = over_seq(layer_input)
+    queries = group * HEAD_DIM
+    pair_weights = jnp.transpose(attn_weight[:, :, queries:], (1, 0, 2))
+    head_weights = jnp.transpose(attn_weight[:, :, :queries], (1, 0, 2))
+    args = [layer_input, rate_weight.T]
+    shapes = [((EXTRA, tok), F32), ((tok, HEAD_DIM), F32), ((tok, HEAD_DIM), F32)]
+    raw, cosine, sine = call(
+        prepare_kernel, ids, [flat(a.shape) for a in args], args, shapes, 10**9
+    )
+
+    pair_places = [
+        lambda h, l: (1 - h, 0, 0), lambda h, l: (1 - h, 0, 1),
+        lambda h, l: (h, 0, 0), lambda h, l: (h, 0, 1),
+    ]
+
+    def high_places(j):
+        return [
+            lambda h, l: (1 - h, 0, (1 - l) * heads + j), lambda h, l: (1 - h, 0, l * heads + j),
+            lambda h, l: (h, 0, (1 - l) * heads + j), lambda h, l: (h, 0, l * heads + j),
+        ]
+
+    def low_places(j):
+        return [
+            lambda h, l: (1 - h, 0, (1 - l) * heads + j), lambda h, l: (h, 0, (1 - l) * heads + j),
+            lambda h, l: (1 - h, 0, l * heads + j), lambda h, l: (h, 0, l * heads + j),
+        ]
+
+    other, pair_weights, head_weights = lax.optimization_barrier((other, pair_weights, head_weights))
+    plan = [(None, pair_weights, pair_places, over_high, over_low)]
+    for pair in range(heads // 2):
+        plan.append((2 * pair + 1, head_weights, low_places(2 * pair + 1), over_low, over_high))
+        plan.append((2 * pair, head_weights, high_places(2 * pair), over_high, over_low))
+    ahead = [ids]
+
+    def queued(make):
+        ready, _ = lax.optimization_barrier((ids, ahead[0]))
+        outs = make(ready)
+        ahead[0] = outs[0]
+        return outs
+
+    crossed, parts, arrived, pieces, kept = {}, {}, {}, {}, {}
+
+    def cross(at):
+        _, weights, places, _, _ = plan[at]
+        out = queued(lambda ready: [project(ready, other, own_block, weights, places)])[0]
+        crossed[at] = over_seq(out)
+
+    def mine(at):
+        j, weights, places, first, _ = plan[at]
+        send, kept[at] = queued(
+            lambda ready: project_add(
+                ready, layer_input, own_block, weights, places, crossed[at],
+                raw if j is None else None,
+            )
+        )
+        parts[at] = first(send)
+
+    def middle(at):
+        j, _, _, _, second = plan[at]
+        keep, u = kept[at], parts[at]
+        if j is None:
+            args = [raw, keep, u]
+            shapes = [((tok + EXTRA, 2 * HEAD_DIM), BF16)]
+            send = queued(
+                lambda ready: call(
+                    pair_middle_kernel, ready, [flat(a.shape) for a in args], args, shapes, 10**7
+                )
+            )[0]
+        else:
+            specs = [pl.BlockSpec((tok, LANES), lambda step, ids: (0, 0))] * 2
+            send = queued(
+                lambda ready: call(
+                    middle_kernel, ready, specs, [keep, u], [((tok, LANES), BF16)], 10**7
+                )
+            )[0]
+        arrived[at] = second(send)
+        if j is not None:
+            pieces[j] = (keep, u, arrived[at])
+
+    def context():
+        args = [
+            raw, kept[0], parts[0], arrived[0], cosine, sine, rate_bias[:, None], decay_rate[:, None],
+        ]
+        spans = tok // STRETCH
+        shapes = [
+            ((tok + heads // 2 * HEAD_DIM, 2 * HEAD_DIM), BF16), ((tok, HEAD_DIM), BF16),
+            ((heads * spans, STRETCH), F32), ((STRETCH, LANES), F32), ((heads * spans, STRETCH), F32),
+            ((heads, HEAD_DIM, HEAD_DIM), F32),
+        ]
+        carry, *rest = queued(
+            lambda ready: call(
+                functools.partial(context_kernel, STRETCH), ready,
+                [flat(a.shape) for a in args], args, shapes, 10**9,
+            )
+        )
+        came = over_seq(carry)
+        bterm, across, down, step, first_state = rest
+        return (
+            cosine, sine, carry, bterm, came, across, down, step, first_state, skip_gain[None, :],
+        )
+
+    def tail(pair, shared, before):
+        numbers = (2 * pair, 2 * pair + 1)
+        return queued(
+            lambda ready: heads_call(
+                ready, pair, numbers, [pieces[n] for n in numbers], shared,
+                heads * HEAD_DIM, before,
+            )
+        )
+
+    cross(0)
+    cross(1)
+    mine(0)
+    mine(1)
+    cross(2)
+    cross(3)
+    mine(2)
+    cross(4)
+    middle(0)
+    mine(3)
+    mine(4)
+    middle(1)
+    middle(2)
+    shared = context()
+    middle(3)
+    outs = tail(0, shared, None)
+    middle(4)
+    outs = tail(1, shared, outs)
+    return outs[0], outs[1]
+
+
 def solution(mesh):
     placed = (
         P("seq", "grp"),
@@ -175,8 +630,15 @@
         P(("mdl", "grp")),
         P(("mdl", "grp")),
     )
+    chips = mesh.shape["grp"] * mesh.shape["mdl"]
+    paired = (
+        mesh.shape["seq"] == 2
+        and mesh.shape["grp"] == 4
+        and KV_HEADS == 2 * mesh.shape["mdl"]
+        and HEADS // chips == 4
+    )
     return jax.shard_map(
-        body,
+        pair_body if paired else body,
         mesh=mesh,
         in_specs=placed,
         out_specs=(P("seq", ("mdl", "grp")), P("seq", ("mdl", "grp"))),

time: 194 us -> 89.6 us (0.46)
  waiting for transfers between devices: 74 us -> 18.8 us
  Pallas kernels: 0 us -> 37.4 us
  matrix products: 35.9 us -> 0 us
  blocking collectives: 25.5 us -> 0 us
  other arithmetic: 16.1 us -> 0.08 us
  starting transfers between devices: 0.08 us -> 15.8 us
  between operations: 14.4 us -> 0.97 us
  local copies, waits for them, and re-layouts: 27.5 us -> 16.3 us
    psum x1 -> x0, waiting for transfers between devices: 67.8 us -> none  [body(): lax.psum(merged.astype(jnp.bfloat16), 'grp').astype(jnp.float32)]
    pallas_call x0 -> x19, Pallas kernels: none -> 37.4 us  [call(): pl.pallas_call(kernel, grid_spec=pltpu.PrefetchScalarGridSpec(num_scalar_...]
    dot_general x14 -> x0, matrix products: 35.9 us -> none  [the longest x1 10.8 us: body(): jnp.einsum('td,dkc->tkc', layer_input, lax.all_gather(attn_weight, 'seq',...]
    ppermute x0 -> x17, waiting for transfers between devices: none -> 18.8 us  [the longest x5 12.1 us: pair_steps(): over_low = lambda a: lax.ppermute(a, 'grp', swap_low)]
    psum x1 -> x0, blocking collectives: 17.5 us -> none  [body(): lax.psum(rate_part.astype(jnp.bfloat16), 'grp').astype(jnp.float32)]
    ppermute x0 -> x17, starting transfers between devices: none -> 15.8 us  [the longest x5 8.27 us: pair_steps(): over_high = lambda a: lax.ppermute(a, 'grp', swap_high)]
    all_gather x4 -> x0, blocking collectives: 7.97 us -> none  [the longest x1 2.17 us: body(): lax.all_gather(rot_keys, 'seq', axis=0, tiled=True)]
    all_gather x1 -> x0, waiting for transfers between devices: 6.21 us -> none  [body(): lax.all_gather(attn_weight, 'seq', axis=0, tiled=True)]
  transfers between devices with their start and end apart: 2 -> 17, of which waited for: 2 -> 5; matrix products, arithmetic and copies ran while one was open for 5% -> 12% of each run, Pallas kernels for 0% -> 28%
where the time goes in v2:
time: 89.6 us; the launch traced here: 89.3 us
  Pallas kernels  37.4 us (42%)
  waiting for transfers between devices  18.8 us (21%)
  local copies, waits for them, and re-layouts  16.3 us (18%)
  starting transfers between devices  15.8 us (18%)
  between operations  0.97 us (1%)
    pallas_call x19, Pallas kernels, call(): pl.pallas_call(kernel, grid_spec=pltpu.PrefetchScalarGridSpec(num_scalar_...  37.4 us
    ppermute x5, waiting for transfers between devices, pair_steps(): over_low = lambda a: lax.ppermute(a, 'grp', swap_low)  12.1 us
    unnamed x42, local copies, waits for them, and re-layouts  9.08 us
    ppermute x5, starting transfers between devices, pair_steps(): over_high = lambda a: lax.ppermute(a, 'grp', swap_high)  8.27 us
    slice x1, local copies, waits for them, and re-layouts, pair_steps(): head_weights = jnp.transpose(attn_weight[:, :, :queries], (1, 0, 2))  7.02 us
    ppermute x5, waiting for transfers between devices, pair_steps(): over_high = lambda a: lax.ppermute(a, 'grp', swap_high)  6.69 us
    ppermute x5, starting transfers between devices, pair_steps(): over_low = lambda a: lax.ppermute(a, 'grp', swap_low)  5.61 us
    ppermute x7, starting transfers between devices, pair_steps(): over_seq = lambda a: lax.ppermute(a, 'seq', [(0, 1), (1, 0)])  1.89 us
  transfers between devices with their start and end apart: 17, of which 5 were waited for; matrix products, arithmetic and copies ran while one was open for 12% of the time, Pallas kernels for 28%

profile of v2, /device:TPU:0, one launch (start us, length us, event | category | flops | bytes accessed | tf_op | source)
XLA Modules:
  0.0 89.3 jit_solution(8095669503800274196)
XLA Ops:
  1.2 7.0 %slice.7 = bf16[1024,2,1024]{2,1,0:T(2,128)(2,1)} slice(bf16[1024,2,1280]{2,1,0:T(2,128)(2,1)} %param.7), slice={[0:1024], [0:2], [0:1024]} | slice | bytes 8388608 | tf_op jit(solution)/shard_map/slice | solution.py:496
  8.3 3.6 %copy.18 = bf16[1024,2,1024]{2,0,1:T(8,128)(2,1)S(1)} copy(bf16[1024,2,1024]{2,1,0:T(2,128)(2,1)} %slice.7) | data formatting | bytes 8388608
  12.0 1.4 %shard_map.77 = bf16[512,512]{1,0:T(8,128)(2,1)S(1)} custom-call(s32[3]{0:T(128)S(1)} %pad_add_fusion.ids, bf16[512,2048]{1,0:T(8,128)(2,1)S(1)} %collective-permute-done.x_ref, bf16[2,1024,256]{2,1,0:T(8,128)(2,1)S(1)} %bitcast.45, bf16[2,1024,256]{2,1,0:T(8,128)(2,1)S(1)} %bitcast.46, bf16[2,1024,256]{2,1,0:T(8,128)(2,1)S(1)} %bitcast.47, ...), custom_call_target="tpu_custom_call" | custom-call | flops 536870912 | bytes 3000000 | tf_op jit(solution)/shard_map/pallas_call | solution.py:271
  13.4 1.4 %copy-done.3 = bf16[512,2048]{1,0:T(8,128)(2,1)} copy-done((bf16[512,2048]{1,0:T(8,128)(2,1)}, bf16[512,2048]{1,0:T(8,128)(2,1)S(1)}, u32[]{:S(2)}) %copy-start.3) | copy-done | bytes 2097176
  14.8 1.7 %copy-done.4 = bf16[512,2048]{1,0:T(8,128)(2,1)S(1)} copy-done((bf16[512,2048]{1,0:T(8,128)(2,1)S(1)}, bf16[512,2048]{1,0:T(8,128)(2,1)}, u32[]{:S(2)}) %copy-start.4) | copy-done | bytes 2097176
  16.6 1.5 %shard_map.78 = bf16[512,512]{1,0:T(8,128)(2,1)S(1)} custom-call(s32[3]{0:T(128)S(1)} %pad_add_fusion.ids, bf16[512,2048]{1,0:T(8,128)(2,1)S(1)} %copy-done.4, bf16[2,1024,1024]{2,1,0:T(8,128)(2,1)S(1)} %bitcast.13, bf16[2,1024,1024]{2,1,0:T(8,128)(2,1)S(1)} %bitcast.14, bf16[2,1024,1024]{2,1,0:T(8,128)(2,1)S(1)} %bitcast.15, bf16[2,1024,1024]{2,1,0:T(8,128)(2,1)S(1)} %bitcast.16), custom_call_target="tpu_custom_call" | custom-call | flops 536870912 | bytes 3000000 | tf_op jit(solution)/shard_map/pallas_call | solution.py:271
  18.6 2.1 %shard_map.79 = (f32[16,512]{1,0:T(8,128)S(1)}, f32[512,128]{1,0:T(8,128)S(1)}, f32[512,128]{1,0:T(8,128)S(1)}) custom-call(s32[3]{0:T(128)S(1)} %pad_add_fusion.ids, bf16[512,2048]{1,0:T(8,128)(2,1)S(1)} %copy-done.2, bf16[16,2048]{1,0:T(8,128)(2,1)S(1)} %bitcast.53), custom_call_target="tpu_custom_call" | custom-call | flops 1000000000 | bytes 3000000 | tf_op jit(solution)/shard_map/pallas_call | solution.py:271
  20.7 1.4 %shard_map.80 = (bf16[528,256]{1,0:T(8,128)(2,1)S(1)}, f32[512,256]{1,0:T(8,128)S(1)}) custom-call(s32[3]{0:T(128)S(1)} %pad_add_fusion.ids, f32[16,512]{1,0:T(8,128)S(1)} %get-tuple-element.50.raw_ref, bf16[512,2048]{1,0:T(8,128)(2,1)S(1)} %copy-done.2, bf16[2,1024,256]{2,1,0:T(8,128)(2,1)S(1)} %bitcast.49, bf16[2,1024,256]{2,1,0:T(8,128)(2,1)S(1)} %bitcast.50, ...), custom_call_target="tpu_custom_call" | custom-call | flops 536870912 | bytes 3000000 | tf_op jit(solution)/shard_map/pallas_call | solution.py:271
  22.1 2.2 %shard_map.81 = (bf16[512,256]{1,0:T(8,128)(2,1)}, f32[512,256]{1,0:T(8,128)S(1)}) custom-call(s32[3]{0:T(128)S(1)} %pad_add_fusion.ids, bf16[512,2048]{1,0:T(8,128)(2,1)S(1)} %copy-done.2, bf16[2,1024,1024]{2,1,0:T(8,128)(2,1)S(1)} %bitcast.17, bf16[2,1024,1024]{2,1,0:T(8,128)(2,1)S(1)} %bitcast.18, bf16[2,1024,1024]{2,1,0:T(8,128)(2,1)S(1)} %bitcast.19, ...), custom_call_target="tpu_custom_call" | custom-call | flops 536870912 | bytes 3000000 | tf_op jit(solution)/shard_map/pallas_call | solution.py:271
  24.3 1.5 %shard_map.82 = bf16[512,512]{1,0:T(8,128)(2,1)S(1)} custom-call(s32[3]{0:T(128)S(1)} %pad_add_fusion.ids, bf16[512,2048]{1,0:T(8,128)(2,1)S(1)} %copy-done.5, bf16[2,1024,1024]{2,1,0:T(8,128)(2,1)S(1)} %bitcast.21, bf16[2,1024,1024]{2,1,0:T(8,128)(2,1)S(1)} %bitcast.22, bf16[2,1024,1024]{2,1,0:T(8,128)(2,1)S(1)} %bitcast.23, bf16[2,1024,1024]{2,1,0:T(8,128)(2,1)S(1)} %bitcast.24), custom_call_target="tpu_custom_call" | custom-call | flops 536870912 | bytes 3000000 | tf_op jit(solution)/shard_map/pallas_call | solution.py:271
  25.8 1.4 %shard_map.83 = bf16[512,512]{1,0:T(8,128)(2,1)S(1)} custom-call(s32[3]{0:T(128)S(1)} %pad_add_fusion.ids, bf16[512,2048]{1,0:T(8,128)(2,1)S(1)} %copy-done.5, bf16[2,1024,1024]{2,1,0:T(8,128)(2,1)S(1)} %bitcast.28, bf16[2,1024,1024]{2,1,0:T(8,128)(2,1)S(1)} %bitcast.26, bf16[2,1024,1024]{2,1,0:T(8,128)(2,1)S(1)} %bitcast.27, bf16[2,1024,1024]{2,1,0:T(8,128)(2,1)S(1)} %bitcast.25), custom_call_target="tpu_custom_call" | custom-call | flops 536870912 | bytes 3000000 | tf_op jit(solution)/shard_map/pallas_call | solution.py:271
  27.8 2.2 %shard_map.84 = (bf16[512,256]{1,0:T(8,128)(2,1)}, f32[512,256]{1,0:T(8,128)S(1)}) custom-call(s32[3]{0:T(128)S(1)} %pad_add_fusion.ids, bf16[512,2048]{1,0:T(8,128)(2,1)S(1)} %copy-done.2, bf16[2,1024,1024]{2,1,0:T(8,128)(2,1)S(1)} %bitcast.29, bf16[2,1024,1024]{2,1,0:T(8,128)(2,1)S(1)} %bitcast.30, bf16[2,1024,1024]{2,1,0:T(8,128)(2,1)S(1)} %bitcast.31, ...), custom_call_target="tpu_custom_call" | custom-call | flops 536870912 | bytes 3000000 | tf_op jit(solution)/shard_map/pallas_call | solution.py:271
  30.0 2.2 %shard_map.85 = bf16[512,512]{1,0:T(8,128)(2,1)} custom-call(s32[3]{0:T(128)S(1)} %pad_add_fusion.ids, bf16[512,2048]{1,0:T(8,128)(2,1)S(1)} %copy-done.5, bf16[2,1024,1024]{2,1,0:T(8,128)(2,1)S(1)} %bitcast.33, bf16[2,1024,1024]{2,1,0:T(8,128)(2,1)S(1)} %bitcast.34, bf16[2,1024,1024]{2,1,0:T(8,128)(2,1)S(1)} %bitcast.35, bf16[2,1024,1024]{2,1,0:T(8,128)(2,1)S(1)} %bitcast.36), custom_call_target="tpu_custom_call" | custom-call | flops 536870912 | bytes 3000000 | tf_op jit(solution)/shard_map/pallas_call | solution.py:271
  32.3 3.0 %collective-permute-start.4 = (bf16[528,256]{1,0:T(8,128)(2,1)S(1)}, bf16[528,256]{1,0:T(8,128)(2,1)S(1)}, u32[]{:S(2)}, u32[]{:S(2)}) collective-permute-start(bf16[528,256]{1,0:T(8,128)(2,1)S(1)} %get-tuple-element.51), channel_id=1, source_target_pairs={{0,16},{8,24},{16,0},{24,8},{1,17},{9,25},{17,1},{25,9},{2,18},{10... | collective-permute-start | bytes 811016 | tf_op jit(solution)/shard_map/ppermute | solution.py:488
  35.2 6.7 %collective-permute-done.4.u_ref = bf16[528,256]{1,0:T(8,128)(2,1)S(1)} collective-permute-done((bf16[528,256]{1,0:T(8,128)(2,1)S(1)}, bf16[528,256]{1,0:T(8,128)(2,1)S(1)}, u32[]{:S(2)}, u32[]{:S(2)}) %collective-permute-start.4) | collective-permute-done | bytes 270368 | tf_op jit(solution)/shard_map/ppermute | solution.py:488
  43.2 1.7 %collective-permute-start.9 = (bf16[528,256]{1,0:T(8,128)(2,1)}, bf16[528,256]{1,0:T(8,128)(2,1)}, u32[]{:S(2)}, u32[]{:S(2)}) collective-permute-start(bf16[528,256]{1,0:T(8,128)(2,1)} %shard_map.86), channel_id=1, source_target_pairs={{0,8},{8,0},{16,24},{24,16},{1,9},{9,1},{17,25},{25,17},{2,10},{10... | collective-permute-start | bytes 811016 | tf_op jit(solution)/shard_map/ppermute | solution.py:489
  45.2 1.7 %collective-permute-start.8 = (bf16[512,256]{1,0:T(8,128)(2,1)}, bf16[512,256]{1,0:T(8,128)(2,1)}, u32[]{:S(2)}, u32[]{:S(2)}) collective-permute-start(bf16[512,256]{1,0:T(8,128)(2,1)} %get-tuple-element.57), channel_id=1, source_target_pairs={{0,16},{8,24},{16,0},{24,8},{1,17},{9,25},{17,1},{25,9},{2,18},{10... | collective-permute-start | bytes 786440 | tf_op jit(solution)/shard_map/ppermute | solution.py:488
  47.2 2.2 %copy-done.1 = bf16[1024,2,1024]{2,0,1:T(8,128)(2,1)S(1)} copy-done((bf16[1024,2,1024]{2,0,1:T(8,128)(2,1)S(1)}, bf16[1024,2,1024]{2,0,1:T(8,128)(2,1)}, u32[]{:S(2)}) %copy-start.1) | copy-done | bytes 4194328
  49.4 1.6 %shard_map.87 = (bf16[512,256]{1,0:T(8,128)(2,1)S(1)}, f32[512,256]{1,0:T(8,128)S(1)}) custom-call(s32[3]{0:T(128)S(1)} %pad_add_fusion.ids, bf16[512,2048]{1,0:T(8,128)(2,1)S(1)} %copy-done.2, bf16[2,1024,1024]{2,1,0:T(8,128)(2,1)S(1)} %bitcast.37, bf16[2,1024,1024]{2,1,0:T(8,128)(2,1)S(1)} %bitcast.38, bf16[2,1024,1024]{2,1,0:T(8,128)(2,1)S(1)} %bitcast.39, ...), custom_call_target="tpu_custom_call" | custom-call | flops 536870912 | bytes 3000000 | tf_op jit(solution)/shard_map/pallas_call | solution.py:271
  51.0 2.6 %shard_map.88 = (bf16[512,256]{1,0:T(8,128)(2,1)S(1)}, f32[512,256]{1,0:T(8,128)S(1)}) custom-call(s32[3]{0:T(128)S(1)} %pad_add_fusion.ids, bf16[512,2048]{1,0:T(8,128)(2,1)S(1)} %copy-done.2, bf16[2,1024,1024]{2,1,0:T(8,128)(2,1)S(1)} %bitcast.41, bf16[2,1024,1024]{2,1,0:T(8,128)(2,1)S(1)} %bitcast.42, bf16[2,1024,1024]{2,1,0:T(8,128)(2,1)S(1)} %bitcast.43, ...), custom_call_target="tpu_custom_call" | custom-call | flops 536870912 | bytes 3000000 | tf_op jit(solution)/shard_map/pallas_call | solution.py:271
  53.7 3.3 %collective-permute-done.7.u_ref.refs_4_ = bf16[512,256]{1,0:T(8,128)(2,1)} collective-permute-done((bf16[512,256]{1,0:T(8,128)(2,1)}, bf16[512,256]{1,0:T(8,128)(2,1)}, u32[]{:S(2)}, u32[]{:S(2)}) %collective-permute-start.7) | collective-permute-done | bytes 262176 | tf_op jit(solution)/shard_map/ppermute | solution.py:489
  57.0 1.5 %shard_map.89 = bf16[512,128]{1,0:T(8,128)(2,1)S(1)} custom-call(s32[3]{0:T(128)S(1)} %pad_add_fusion.ids, f32[512,256]{1,0:T(8,128)S(1)} %copy-done.7, bf16[512,256]{1,0:T(8,128)(2,1)} %collective-permute-done.7.u_ref.refs_4_), custom_call_target="tpu_custom_call" | custom-call | flops 10000000 | bytes 3000000 | tf_op jit(solution)/shard_map/pallas_call | solution.py:271
  58.5 1.5 %shard_map.90 = bf16[512,128]{1,0:T(8,128)(2,1)S(1)} custom-call(s32[3]{0:T(128)S(1)} %pad_add_fusion.ids, f32[512,256]{1,0:T(8,128)S(1)} %copy-done.9, bf16[512,256]{1,0:T(8,128)(2,1)} %collective-permute-done.8.u_ref.refs_1_), custom_call_target="tpu_custom_call" | custom-call | flops 10000000 | bytes 3000000 | tf_op jit(solution)/shard_map/pallas_call | solution.py:271
  60.0 2.7 %shard_map.91 = (bf16[768,256]{1,0:T(8,128)(2,1)S(1)}, bf16[512,128]{1,0:T(8,128)(2,1)S(1)}, f32[8,256]{1,0:T(8,128)S(1)}, f32[256,128]{1,0:T(8,128)S(1)}, f32[8...) custom-call(s32[3]{0:T(128)S(1)} %pad_add_fusion.ids, f32[16,512]{1,0:T(8,128)S(1)} %get-tuple-element.50.raw_ref, ...), custom_call_target="tpu_custom_call" | custom-call | flops 1000000000 | bytes 3000000 | tf_op jit(solution)/shard_map/pallas_call | solution.py:271
  62.8 1.5 %collective-permute-start.10 = (bf16[512,256]{1,0:T(8,128)(2,1)S(1)}, bf16[512,256]{1,0:T(8,128)(2,1)S(1)}, u32[]{:S(2)}, u32[]{:S(2)}) collective-permute-start(bf16[512,256]{1,0:T(8,128)(2,1)S(1)} %get-tuple-element.62), channel_id=1, source_target_pairs={{0,8},{8,0},{16,24},{24,16},{1,9},{9,1},{17,25},{25,17},{2,10},{10... | collective-permute-start | bytes 786440 | tf_op jit(solution)/shard_map/ppermute | solution.py:489
  64.9 1.5 %collective-permute-start.12 = (bf16[512,128]{1,0:T(8,128)(2,1)S(1)}, bf16[512,128]{1,0:T(8,128)(2,1)S(1)}, u32[]{:S(2)}, u32[]{:S(2)}) collective-permute-start(bf16[512,128]{1,0:T(8,128)(2,1)S(1)} %shard_map.89), channel_id=1, source_target_pairs={{0,16},{8,24},{16,0},{24,8},{1,17},{9,25},{17,1},{25,9},{2,18},{10... | collective-permute-start | bytes 393224 | tf_op jit(solution)/shard_map/ppermute | solution.py:488
  66.9 5.1 %collective-permute-done.10.u_ref.refs_4_ = bf16[512,256]{1,0:T(8,128)(2,1)S(1)} collective-permute-done((bf16[512,256]{1,0:T(8,128)(2,1)S(1)}, bf16[512,256]{1,0:T(8,128)(2,1)S(1)}, u32[]{:S(2)}, u32[]{:S(2)}) %collective-permute-start.10) | collective-permute-done | bytes 262176 | tf_op jit(solution)/shard_map/ppermute | solution.py:489
  72.7 1.5 %collective-permute-start.16 = (bf16[512,128]{1,0:T(8,128)(2,1)S(1)}, bf16[512,128]{1,0:T(8,128)(2,1)S(1)}, u32[]{:S(2)}, u32[]{:S(2)}) collective-permute-start(bf16[512,128]{1,0:T(8,128)(2,1)S(1)} %shard_map.92), channel_id=1, source_target_pairs={{0,16},{8,24},{16,0},{24,8},{1,17},{9,25},{17,1},{25,9},{2,18},{10... | collective-permute-start | bytes 393224 | tf_op jit(solution)/shard_map/ppermute | solution.py:488
  74.4 4.9 %shard_map.93 = (bf16[512,512]{1,0:T(8,128)(2,1)}, bf16[512,512]{1,0:T(8,128)(2,1)}) custom-call(s32[3]{0:T(128)S(1)} %pad_add_fusion.ids, f32[512,256]{1,0:T(8,128)S(1)} %copy-done.9, bf16[512,256]{1,0:T(8,128)(2,1)} %collective-permute-done.8.u_ref.refs_1_, bf16[512,128]{1,0:T(8,128)(2,1)S(1)} %collective-permute-done.11.refs_2_, ...), custom_call_target="tpu_custom_call" | custom-call | flops 2000000000 | bytes 3000000 | tf_op jit(solution)/shard_map/pallas_call | solution.py:271
  79.9 1.5 %collective-permute-start.15 = (bf16[512,128]{1,0:T(8,128)(2,1)S(1)}, bf16[512,128]{1,0:T(8,128)(2,1)S(1)}, u32[]{:S(2)}, u32[]{:S(2)}) collective-permute-start(bf16[512,128]{1,0:T(8,128)(2,1)S(1)} %shard_map.94), channel_id=1, source_target_pairs={{0,8},{8,0},{16,24},{24,16},{1,9},{9,1},{17,25},{25,17},{2,10},{10... | collective-permute-start | bytes 393224 | tf_op jit(solution)/shard_map/ppermute | solution.py:489
  81.4 3.5 %collective-permute-done.15.refs_2_ = bf16[512,128]{1,0:T(8,128)(2,1)S(1)} collective-permute-done((bf16[512,128]{1,0:T(8,128)(2,1)S(1)}, bf16[512,128]{1,0:T(8,128)(2,1)S(1)}, u32[]{:S(2)}, u32[]{:S(2)}) %collective-permute-start.15) | collective-permute-done | bytes 131104 | tf_op jit(solution)/shard_map/ppermute | solution.py:489
  84.9 4.4 %shard_map.95 = (bf16[512,512]{1,0:T(8,128)(2,1)}, bf16[512,512]{1,0:T(8,128)(2,1)}) custom-call(s32[3]{0:T(128)S(1)} %pad_add_fusion.ids, f32[512,256]{1,0:T(8,128)S(1)} %get-tuple-element.83.keep_ref.refs_0_, bf16[512,256]{1,0:T(8,128)(2,1)S(1)} %collective-permute-done.14.u_ref.refs_1_, ...), custom_call_target="tpu_custom_call", output_to_operand_aliasing={{0}: (17, {}), {1}: (18, {})} | custom-call | flops 2000000000 | bytes 3000000 | tf_op jit(solution)/shard_map/pallas_call | solution.py:271
  (69 shorter events, 6.5 us)
Async XLA Ops:
  0.6 11.4 %collective-permute-start = (bf16[512,2048]{1,0:T(8,128)(2,1)}, bf16[512,2048]{1,0:T(8,128)(2,1)S(1)}, u32[]{:S(2)}, u32[]{:S(2)}) collective-permute-start(bf16[512,2048]{1,0:T(8,128)(2,1)} %refs_0_.9), channel_id=1, source_target_pairs={{0,4},{4,0},{1,5},{5,1},{2,6},{6,2},{3,7},{7,3},{8,12},{12,8},{9,1... | collective-permute-start | bytes 6291464 | tf_op jit(solution)/shard_map/ppermute | solution.py:490
  8.3 3.6 %slice-start = ((bf16[1024,2,1280]{2,1,0:T(2,128)(2,1)}), bf16[1024,2,256]{2,1,0:T(2,128)(2,1)S(1)}, s32[]{:S(2)}) async-start(bf16[1024,2,1280]{2,1,0:T(2,128)(2,1)} %param.7), calls=%async_computation | async-start | bytes 2097152 | tf_op jit(solution)/shard_map/slice | solution.py:495
  11.9 18.1 %copy-start = (bf16[1024,2,1024]{2,0,1:T(8,128)(2,1)}, bf16[1024,2,1024]{2,0,1:T(8,128)(2,1)S(1)}, u32[]{:S(2)}) copy-start(bf16[1024,2,1024]{2,0,1:T(8,128)(2,1)S(1)} %copy.18) | copy-start | bytes 12582916
  14.8 3.8 %copy-start.2 = (bf16[512,2048]{1,0:T(8,128)(2,1)S(1)}, bf16[512,2048]{1,0:T(8,128)(2,1)}, u32[]{:S(2)}) copy-start(bf16[512,2048]{1,0:T(8,128)(2,1)} %refs_0_.9) | copy-start | bytes 6291460
  14.8 5.9 %collective-permute-start.1 = (bf16[512,512]{1,0:T(8,128)(2,1)S(1)}, bf16[512,512]{1,0:T(8,128)(2,1)S(1)}, u32[]{:S(2)}, u32[]{:S(2)}) collective-permute-start(bf16[512,512]{1,0:T(8,128)(2,1)S(1)} %shard_map.77), channel_id=1, source_target_pairs={{0,4},{4,0},{1,5},{5,1},{2,6},{6,2},{3,7},{7,3},{8,12},{12,8},{9,1... | collective-permute-start | bytes 1572872 | tf_op jit(solution)/shard_map/ppermute | solution.py:490
  18.0 4.1 %collective-permute-start.2 = (bf16[512,512]{1,0:T(8,128)(2,1)S(1)}, bf16[512,512]{1,0:T(8,128)(2,1)S(1)}, u32[]{:S(2)}, u32[]{:S(2)}) collective-permute-start(bf16[512,512]{1,0:T(8,128)(2,1)S(1)} %shard_map.78), channel_id=1, source_target_pairs={{0,4},{4,0},{1,5},{5,1},{2,6},{6,2},{3,7},{7,3},{8,12},{12,8},{9,1... | collective-permute-start | bytes 1572872 | tf_op jit(solution)/shard_map/ppermute | solution.py:490
  20.7 3.6 %copy-start.16 = (f32[512,128]{1,0:T(8,128)}, f32[512,128]{1,0:T(8,128)S(1)}, u32[]{:S(2)}) copy-start(f32[512,128]{1,0:T(8,128)S(1)} %get-tuple-element.71.sin_ref.refs_7_) | copy-start | bytes 786436
  22.1 19.8 %copy-start.10 = (f32[512,256]{1,0:T(8,128)}, f32[512,256]{1,0:T(8,128)S(1)}, u32[]{:S(2)}) copy-start(f32[512,256]{1,0:T(8,128)S(1)} %get-tuple-element.60.keep_ref) | copy-start | bytes 1572868
  25.7 2.1 %collective-permute-start.3 = (bf16[512,512]{1,0:T(8,128)(2,1)S(1)}, bf16[512,512]{1,0:T(8,128)(2,1)S(1)}, u32[]{:S(2)}, u32[]{:S(2)}) collective-permute-start(bf16[512,512]{1,0:T(8,128)(2,1)S(1)} %shard_map.82), channel_id=1, source_target_pairs={{0,4},{4,0},{1,5},{5,1},{2,6},{6,2},{3,7},{7,3},{8,12},{12,8},{9,1... | collective-permute-start | bytes 1572872 | tf_op jit(solution)/shard_map/ppermute | solution.py:490
  27.3 19.9 %collective-permute-start.5 = (bf16[512,512]{1,0:T(8,128)(2,1)S(1)}, bf16[512,512]{1,0:T(8,128)(2,1)S(1)}, u32[]{:S(2)}, u32[]{:S(2)}) collective-permute-start(bf16[512,512]{1,0:T(8,128)(2,1)S(1)} %shard_map.83), channel_id=1, source_target_pairs={{0,4},{4,0},{1,5},{5,1},{2,6},{6,2},{3,7},{7,3},{8,12},{12,8},{9,1... | collective-permute-start | bytes 1572872 | tf_op jit(solution)/shard_map/ppermute | solution.py:490
  30.0 2.2 %copy-start.8 = (f32[512,256]{1,0:T(8,128)}, f32[512,256]{1,0:T(8,128)S(1)}, u32[]{:S(2)}) copy-start(f32[512,256]{1,0:T(8,128)S(1)} %get-tuple-element.68.keep_ref.refs_0_) | copy-start | bytes 1572868
  30.0 17.0 %copy-start.18 = (f32[4]{0:T(128)S(1)}, f32[4]{0:T(128)}, u32[]{:S(2)}) copy-start(f32[4]{0:T(128)} %param.9) | copy-start | bytes 52
  30.0 17.1 %copy-start.19 = (f32[4]{0:T(128)S(1)}, f32[4]{0:T(128)}, u32[]{:S(2)}) copy-start(f32[4]{0:T(128)} %param.10) | copy-start | bytes 52
  32.2 18.8 %collective-permute-start.6 = (bf16[512,512]{1,0:T(8,128)(2,1)}, bf16[512,512]{1,0:T(8,128)(2,1)}, u32[]{:S(2)}, u32[]{:S(2)}) collective-permute-start(bf16[512,512]{1,0:T(8,128)(2,1)} %shard_map.85), channel_id=1, source_target_pairs={{0,4},{4,0},{1,5},{5,1},{2,6},{6,2},{3,7},{7,3},{8,12},{12,8},{9,1... | collective-permute-start | bytes 1572872 | tf_op jit(solution)/shard_map/ppermute | solution.py:490
  32.3 9.7 %collective-permute-start.4 = (bf16[528,256]{1,0:T(8,128)(2,1)S(1)}, bf16[528,256]{1,0:T(8,128)(2,1)S(1)}, u32[]{:S(2)}, u32[]{:S(2)}) collective-permute-start(bf16[528,256]{1,0:T(8,128)(2,1)S(1)} %get-tuple-element.51), channel_id=1, source_target_pairs={{0,16},{8,24},{16,0},{24,8},{1,17},{9,25},{17,1},{25,9},{2,18},{10... | collective-permute-start | bytes 811016 | tf_op jit(solution)/shard_map/ppermute | solution.py:488
  43.2 16.8 %collective-permute-start.9 = (bf16[528,256]{1,0:T(8,128)(2,1)}, bf16[528,256]{1,0:T(8,128)(2,1)}, u32[]{:S(2)}, u32[]{:S(2)}) collective-permute-start(bf16[528,256]{1,0:T(8,128)(2,1)} %shard_map.86), channel_id=1, source_target_pairs={{0,8},{8,0},{16,24},{24,16},{1,9},{9,1},{17,25},{25,17},{2,10},{10... | collective-permute-start | bytes 811016 | tf_op jit(solution)/shard_map/ppermute | solution.py:489
  44.9 12.1 %collective-permute-start.7 = (bf16[512,256]{1,0:T(8,128)(2,1)}, bf16[512,256]{1,0:T(8,128)(2,1)}, u32[]{:S(2)}, u32[]{:S(2)}) collective-permute-start(bf16[512,256]{1,0:T(8,128)(2,1)} %get-tuple-element.53), channel_id=1, source_target_pairs={{0,8},{8,0},{16,24},{24,16},{1,9},{9,1},{17,25},{25,17},{2,10},{10... | collective-permute-start | bytes 786440 | tf_op jit(solution)/shard_map/ppermute | solution.py:489
  45.2 13.2 %collective-permute-start.8 = (bf16[512,256]{1,0:T(8,128)(2,1)}, bf16[512,256]{1,0:T(8,128)(2,1)}, u32[]{:S(2)}, u32[]{:S(2)}) collective-permute-start(bf16[512,256]{1,0:T(8,128)(2,1)} %get-tuple-element.57), channel_id=1, source_target_pairs={{0,16},{8,24},{16,0},{24,8},{1,17},{9,25},{17,1},{25,9},{2,18},{10... | collective-permute-start | bytes 786440 | tf_op jit(solution)/shard_map/ppermute | solution.py:488
  47.2 2.2 %copy-start.1 = (bf16[1024,2,1024]{2,0,1:T(8,128)(2,1)S(1)}, bf16[1024,2,1024]{2,0,1:T(8,128)(2,1)}, u32[]{:S(2)}) copy-start(bf16[1024,2,1024]{2,0,1:T(8,128)(2,1)} %copy-done) | copy-start | bytes 12582916
  51.0 6.0 %copy-start.7 = (f32[512,256]{1,0:T(8,128)S(1)}, f32[512,256]{1,0:T(8,128)}, u32[]{:S(2)}) copy-start(f32[512,256]{1,0:T(8,128)} %copy-done.6) | copy-start | bytes 1572868
  51.0 7.5 %copy-start.9 = (f32[512,256]{1,0:T(8,128)S(1)}, f32[512,256]{1,0:T(8,128)}, u32[]{:S(2)}) copy-start(f32[512,256]{1,0:T(8,128)} %copy-done.8) | copy-start | bytes 1572868
  51.0 9.0 %copy-start.11 = (f32[512,256]{1,0:T(8,128)S(1)}, f32[512,256]{1,0:T(8,128)}, u32[]{:S(2)}) copy-start(f32[512,256]{1,0:T(8,128)} %copy-done.10) | copy-start | bytes 1572868
  51.0 9.0 %copy-start.15 = (f32[512,128]{1,0:T(8,128)S(1)}, f32[512,128]{1,0:T(8,128)}, u32[]{:S(2)}) copy-start(f32[512,128]{1,0:T(8,128)} %copy-done.14) | copy-start | bytes 786436
  51.0 9.0 %copy-start.17 = (f32[512,128]{1,0:T(8,128)S(1)}, f32[512,128]{1,0:T(8,128)}, u32[]{:S(2)}) copy-start(f32[512,128]{1,0:T(8,128)} %copy-done.16) | copy-start | bytes 786436
  53.7 20.7 %copy-start.13 = (f32[4]{0:T(128)S(1)}, f32[4]{0:T(128)}, u32[]{:S(2)}) copy-start(f32[4]{0:T(128)} %param.11) | copy-start | bytes 52
  62.8 11.6 %collective-permute-start.13 = (bf16[768,256]{1,0:T(8,128)(2,1)S(1)}, bf16[768,256]{1,0:T(8,128)(2,1)S(1)}, u32[]{:S(2)}, u32[]{:S(2)}) collective-permute-start(bf16[768,256]{1,0:T(8,128)(2,1)S(1)} %get-tuple-element.72.refs_8_), channel_id=1, source_target_pairs={{0,4},{4,0},{1,5},{5,1},{2,6},{6,2},{3,7},{7,3},{8,12},{12,8},{9,1... | collective-permute-start | bytes 1179656 | tf_op jit(solution)/shard_map/ppermute | solution.py:490
  62.8 9.2 %collective-permute-start.10 = (bf16[512,256]{1,0:T(8,128)(2,1)S(1)}, bf16[512,256]{1,0:T(8,128)(2,1)S(1)}, u32[]{:S(2)}, u32[]{:S(2)}) collective-permute-start(bf16[512,256]{1,0:T(8,128)(2,1)S(1)} %get-tuple-element.62), channel_id=1, source_target_pairs={{0,8},{8,0},{16,24},{24,16},{1,9},{9,1},{17,25},{25,17},{2,10},{10... | collective-permute-start | bytes 786440 | tf_op jit(solution)/shard_map/ppermute | solution.py:489
  64.3 10.0 %collective-permute-start.11 = (bf16[512,128]{1,0:T(8,128)(2,1)S(1)}, bf16[512,128]{1,0:T(8,128)(2,1)S(1)}, u32[]{:S(2)}, u32[]{:S(2)}) collective-permute-start(bf16[512,128]{1,0:T(8,128)(2,1)S(1)} %shard_map.90), channel_id=1, source_target_pairs={{0,8},{8,0},{16,24},{24,16},{1,9},{9,1},{17,25},{25,17},{2,10},{10... | collective-permute-start | bytes 393224 | tf_op jit(solution)/shard_map/ppermute | solution.py:489
  64.9 9.4 %collective-permute-start.12 = (bf16[512,128]{1,0:T(8,128)(2,1)S(1)}, bf16[512,128]{1,0:T(8,128)(2,1)S(1)}, u32[]{:S(2)}, u32[]{:S(2)}) collective-permute-start(bf16[512,128]{1,0:T(8,128)(2,1)S(1)} %shard_map.89), channel_id=1, source_target_pairs={{0,16},{8,24},{16,0},{24,8},{1,17},{9,25},{17,1},{25,9},{2,18},{10... | collective-permute-start | bytes 393224 | tf_op jit(solution)/shard_map/ppermute | solution.py:488
  66.4 12.9 %collective-permute-start.14 = (bf16[512,256]{1,0:T(8,128)(2,1)S(1)}, bf16[512,256]{1,0:T(8,128)(2,1)S(1)}, u32[]{:S(2)}, u32[]{:S(2)}) collective-permute-start(bf16[512,256]{1,0:T(8,128)(2,1)S(1)} %get-tuple-element.64), channel_id=1, source_target_pairs={{0,16},{8,24},{16,0},{24,8},{1,17},{9,25},{17,1},{25,9},{2,18},{10... | collective-permute-start | bytes 786440 | tf_op jit(solution)/shard_map/ppermute | solution.py:488
  72.7 8.7 %collective-permute-start.16 = (bf16[512,128]{1,0:T(8,128)(2,1)S(1)}, bf16[512,128]{1,0:T(8,128)(2,1)S(1)}, u32[]{:S(2)}, u32[]{:S(2)}) collective-permute-start(bf16[512,128]{1,0:T(8,128)(2,1)S(1)} %shard_map.92), channel_id=1, source_target_pairs={{0,16},{8,24},{16,0},{24,8},{1,17},{9,25},{17,1},{25,9},{2,18},{10... | collective-permute-start | bytes 393224 | tf_op jit(solution)/shard_map/ppermute | solution.py:488
  79.9 5.0 %collective-permute-start.15 = (bf16[512,128]{1,0:T(8,128)(2,1)S(1)}, bf16[512,128]{1,0:T(8,128)(2,1)S(1)}, u32[]{:S(2)}, u32[]{:S(2)}) collective-permute-start(bf16[512,128]{1,0:T(8,128)(2,1)S(1)} %shard_map.94), channel_id=1, source_target_pairs={{0,8},{8,0},{16,24},{24,16},{1,9},{9,1},{17,25},{25,17},{2,10},{10... | collective-permute-start | bytes 393224 | tf_op jit(solution)/shard_map/ppermute | solution.py:489
  (6 other events, 10.2 us)

commit v3 on v2

--- a/solution.py
+++ b/solution.py
@@ -174,7 +174,7 @@
 
 LANES = 128
 EXTRA = 16
-VMEM_GRANT = 24 * 1024 * 1024
+GRANTS = tuple(mib * 1024 * 1024 for mib in (6, 12, 16, 24))
 F32 = jnp.float32
 BF16 = jnp.bfloat16
 LAST = (((1,), (1,)), ((), ()))
@@ -267,7 +267,7 @@
     return pl.BlockSpec(shape, lambda step, ids, n=len(shape): (0,) * n)
 
 
-def call(kernel, ids, specs, args, shapes, flops, aliases={}, out_specs=None):
+def call(kernel, ids, specs, args, shapes, flops, aliases={}, out_specs=None, grant=GRANTS[1]):
     return pl.pallas_call(
         kernel,
         grid_spec=pltpu.PrefetchScalarGridSpec(
@@ -278,7 +278,7 @@
         ),
         out_shape=[jax.ShapeDtypeStruct(s, d) for s, d in shapes],
         input_output_aliases=aliases,
-        compiler_params=pltpu.CompilerParams(vmem_limit_bytes=VMEM_GRANT),
+        compiler_params=pltpu.CompilerParams(vmem_limit_bytes=grant),
         cost_estimate=cost(flops, 3 * 10**6),
     )(ids, *args)
 
@@ -338,8 +338,14 @@
     bterm_ref[...] = bterm
     both = own_rates(ids, raw_ref, u_ref) + unfolded(z_ref[tok:, :].astype(F32))
     raw = jnp.where(ids[1] == 0, both[:heads], both[heads:])
-    step = jax.nn.softplus(raw + bias_ref[...])
-    decay = -rate_ref[...] * step
+    which = lax.broadcasted_iota(jnp.int32, (heads, 1), 0)
+    bias = jnp.full((heads, 1), bias_ref[0], F32)
+    rate = jnp.full((heads, 1), rate_ref[0], F32)
+    for h in range(1, heads):
+        bias = jnp.where(which == h, bias_ref[h], bias)
+        rate = jnp.where(which == h, rate_ref[h], rate)
+    step = jax.nn.softplus(raw + bias)
+    decay = -rate * step
     rows = lax.broadcasted_iota(jnp.int32, (stretch, stretch), 0)
     cols = lax.broadcasted_iota(jnp.int32, (stretch, stretch), 1)
     below = (cols <= rows).astype(F32).astype(BF16)
@@ -408,7 +414,7 @@
         cterm = query.astype(BF16)
         row, col = tok + (head // 2) * HEAD_DIM, (head % 2) * HEAD_DIM
         state = came_ref[row : row + HEAD_DIM, col : col + HEAD_DIM].astype(F32) * later
-        skip = skip_ref[0, head]
+        skip = skip_ref[head]
         for index in range(tok // stretch):
             span = slice(index * stretch, (index + 1) * stretch)
             reach = (index + 1) * stretch
@@ -468,6 +474,7 @@
     return call(
         functools.partial(heads_kernel, STRETCH, numbers),
         ids, specs, args, [((tok, total), BF16)] * 2, 2 * 10**9, aliases, [block] * 2,
+        GRANTS[3],
     )
 
 
@@ -491,9 +498,7 @@
     own_block = lambda step, ids: (0, ids[2])
 
     other = over_seq(layer_input)
-    queries = group * HEAD_DIM
-    pair_weights = jnp.transpose(attn_weight[:, :, queries:], (1, 0, 2))
-    head_weights = jnp.transpose(attn_weight[:, :, :queries], (1, 0, 2))
+    weights_all = jnp.transpose(attn_weight, (1, 0, 2))
     args = [layer_input, rate_weight.T]
     shapes = [((EXTRA, tok), F32), ((tok, HEAD_DIM), F32), ((tok, HEAD_DIM), F32)]
     raw, cosine, sine = call(
@@ -501,8 +506,8 @@
     )
 
     pair_places = [
-        lambda h, l: (1 - h, 0, 0), lambda h, l: (1 - h, 0, 1),
-        lambda h, l: (h, 0, 0), lambda h, l: (h, 0, 1),
+        lambda h, l: (1 - h, 0, group), lambda h, l: (1 - h, 0, group + 1),
+        lambda h, l: (h, 0, group), lambda h, l: (h, 0, group + 1),
     ]
 
     def high_places(j):
@@ -517,11 +522,11 @@
             lambda h, l: (1 - h, 0, l * heads + j), lambda h, l: (h, 0, l * heads + j),
         ]
 
-    other, pair_weights, head_weights = lax.optimization_barrier((other, pair_weights, head_weights))
-    plan = [(None, pair_weights, pair_places, over_high, over_low)]
+    other, weights_all = lax.optimization_barrier((other, weights_all))
+    plan = [(None, weights_all, pair_places, over_high, over_low)]
     for pair in range(heads // 2):
-        plan.append((2 * pair + 1, head_weights, low_places(2 * pair + 1), over_low, over_high))
-        plan.append((2 * pair, head_weights, high_places(2 * pair), over_high, over_low))
+        plan.append((2 * pair + 1, weights_all, low_places(2 * pair + 1), over_low, over_high))
+        plan.append((2 * pair, weights_all, high_places(2 * pair), over_high, over_low))
     ahead = [ids]
 
     def queued(make):
@@ -562,7 +567,7 @@
             specs = [pl.BlockSpec((tok, LANES), lambda step, ids: (0, 0))] * 2
             send = queued(
                 lambda ready: call(
-                    middle_kernel, ready, specs, [keep, u], [((tok, LANES), BF16)], 10**7
+                    middle_kernel, ready, specs, [keep, u], [((tok, LANES), BF16)], 10**7, grant=GRANTS[0]
                 )
             )[0]
         arrived[at] = second(send)
@@ -571,8 +576,10 @@
 
     def context():
         args = [
-            raw, kept[0], parts[0], arrived[0], cosine, sine, rate_bias[:, None], decay_rate[:, None],
+            raw, kept[0], parts[0], arrived[0], cosine, sine, rate_bias, decay_rate,
         ]
+        scalars = pl.BlockSpec(memory_space=pltpu.SMEM)
+        specs = [flat(a.shape) for a in args[:-2]] + [scalars] * 2
         spans = tok // STRETCH
         shapes = [
             ((tok + heads // 2 * HEAD_DIM, 2 * HEAD_DIM), BF16), ((tok, HEAD_DIM), BF16),
@@ -582,13 +589,13 @@
         carry, *rest = queued(
             lambda ready: call(
                 functools.partial(context_kernel, STRETCH), ready,
-                [flat(a.shape) for a in args], args, shapes, 10**9,
+                specs, args, shapes, 10**9, grant=GRANTS[2],
             )
         )
         came = over_seq(carry)
         bterm, across, down, step, first_state = rest
         return (
-            cosine, sine, carry, bterm, came, across, down, step, first_state, skip_gain[None, :],
+            cosine, sine, carry, bterm, came, across, down, step, first_state, skip_gain,
         )
 
     def tail(pair, shared, before):

time: 89.6 us -> 74.1 us (0.83)
  local copies, waits for them, and re-layouts: 16.3 us -> 3.18 us
  Pallas kernels: 37.4 us -> 30 us
  waiting for transfers between devices: 18.8 us -> 23.8 us
    pallas_call x19, Pallas kernels: 37.4 us -> 30 us  [call(): pl.pallas_call(kernel, grid_spec=pltpu.PrefetchScalarGridSpec(num_scalar_...]
    slice x3 -> x0, local copies, waits for them, and re-layouts: 7.02 us -> none  [the longest x1 7.02 us: pair_steps(): head_weights = jnp.transpose(attn_weight[:, :, :queries], (1, 0, 2))]
    unnamed x42 -> x11, local copies, waits for them, and re-layouts: 9.08 us -> 3.18 us
    ppermute x5, waiting for transfers between devices: 12.1 us -> 16 us  [pair_steps(): over_low = lambda a: lax.ppermute(a, 'grp', swap_low)]
  transfers between devices with their start and end apart: 17 -> 17, of which waited for: 5 -> 6; matrix products, arithmetic and copies ran while one was open for 12% -> 4% of each run, Pallas kernels for 28% -> 26%
where the time goes in v3:
time: 74.1 us; the launch traced here: 73.9 us
  Pallas kernels  30 us (40%)
  waiting for transfers between devices  23.8 us (32%)
  starting transfers between devices  16 us (22%)
  local copies, waits for them, and re-layouts  3.18 us (4%)
  between operations  0.88 us (1%)
    pallas_call x19, Pallas kernels, call(): pl.pallas_call(kernel, grid_spec=pltpu.PrefetchScalarGridSpec(num_scalar_...  30 us
    ppermute x5, waiting for transfers between devices, pair_steps(): over_low = lambda a: lax.ppermute(a, 'grp', swap_low)  16 us
    ppermute x5, starting transfers between devices, pair_steps(): over_high = lambda a: lax.ppermute(a, 'grp', swap_high)  7.94 us
    ppermute x5, waiting for transfers between devices, pair_steps(): over_high = lambda a: lax.ppermute(a, 'grp', swap_high)  7.03 us
    ppermute x5, starting transfers between devices, pair_steps(): over_low = lambda a: lax.ppermute(a, 'grp', swap_low)  5.69 us
    unnamed x11, local copies, waits for them, and re-layouts  3.18 us
    ppermute x7, starting transfers between devices, pair_steps(): over_seq = lambda a: lax.ppermute(a, 'seq', [(0, 1), (1, 0)])  2.35 us
  transfers between devices with their start and end apart: 17, of which 6 were waited for; matrix products, arithmetic and copies ran while one was open for 4% of the time, Pallas kernels for 26%

profile of v3, /device:TPU:0, one launch (start us, length us, event | category | flops | bytes accessed | tf_op | source)
XLA Modules:
  0.0 73.9 jit_solution(12979515977207419668)
XLA Ops:
  1.3 3.1 %copy.12 = bf16[1024,2,1280]{2,0,1:T(8,128)(2,1)S(1)} copy(bf16[1024,2,1280]{2,1,0:T(2,128)(2,1)} %param.7) | data formatting | bytes 10485760 | tf_op args[1]
  4.4 0.8 %collective-permute-done.x_ref = bf16[512,2048]{1,0:T(8,128)(2,1)S(1)} collective-permute-done((bf16[512,2048]{1,0:T(8,128)(2,1)}, bf16[512,2048]{1,0:T(8,128)(2,1)S(1)}, u32[]{:S(2)}, u32[]{:S(2)}) %collective-permute-start) | collective-permute-done | bytes 2097184 | tf_op jit(solution)/shard_map/ppermute | solution.py:497
  5.2 1.4 %shard_map.77 = bf16[512,512]{1,0:T(8,128)(2,1)S(1)} custom-call(s32[3]{0:T(128)S(1)} %pad_add_fusion.ids, bf16[512,2048]{1,0:T(8,128)(2,1)S(1)} %collective-permute-done.x_ref, bf16[2,1024,1280]{2,1,0:T(8,128)(2,1)S(1)} %bitcast.7, bf16[2,1024,1280]{2,1,0:T(8,128)(2,1)S(1)} %bitcast.8, bf16[2,1024,1280]{2,1,0:T(8,128)(2,1)S(1)} %bitcast.9, ...), custom_call_target="tpu_custom_call" | custom-call | flops 536870912 | bytes 3000000 | tf_op jit(solution)/shard_map/pallas_call | solution.py:271
  7.0 1.4 %shard_map.78 = bf16[512,512]{1,0:T(8,128)(2,1)S(1)} custom-call(s32[3]{0:T(128)S(1)} %pad_add_fusion.ids, bf16[512,2048]{1,0:T(8,128)(2,1)S(1)} %collective-permute-done.x_ref, bf16[2,1024,1280]{2,1,0:T(8,128)(2,1)S(1)} %bitcast.11, bf16[2,1024,1280]{2,1,0:T(8,128)(2,1)S(1)} %bitcast.12, bf16[2,1024,1280]{2,1,0:T(8,128)(2,1)S(1)} %bitcast.13, ...), custom_call_target="tpu_custom_call" | custom-call | flops 536870912 | bytes 3000000 | tf_op jit(solution)/shard_map/pallas_call | solution.py:271
  8.6 2.1 %shard_map.79 = (f32[16,512]{1,0:T(8,128)S(1)}, f32[512,128]{1,0:T(8,128)S(1)}, f32[512,128]{1,0:T(8,128)S(1)}) custom-call(s32[3]{0:T(128)S(1)} %pad_add_fusion.ids, bf16[512,2048]{1,0:T(8,128)(2,1)S(1)} %copy-done, bf16[16,2048]{1,0:T(8,128)(2,1)S(1)} %bitcast.47), custom_call_target="tpu_custom_call" | custom-call | flops 1000000000 | bytes 3000000 | tf_op jit(solution)/shard_map/pallas_call | solution.py:271
  10.7 1.4 %shard_map.80 = (bf16[528,256]{1,0:T(8,128)(2,1)S(1)}, f32[512,256]{1,0:T(8,128)S(1)}) custom-call(s32[3]{0:T(128)S(1)} %pad_add_fusion.ids, f32[16,512]{1,0:T(8,128)S(1)} %get-tuple-element.48.raw_ref, bf16[512,2048]{1,0:T(8,128)(2,1)S(1)} %copy-done, bf16[2,1024,1280]{2,1,0:T(8,128)(2,1)S(1)} %bitcast.15, bf16[2,1024,1280]{2,1,0:T(8,128)(2,1)S(1)} %bitcast.16, ...), custom_call_target="tpu_custom_call" | custom-call | flops 536870912 | bytes 3000000 | tf_op jit(solution)/shard_map/pallas_call | solution.py:271
  12.1 1.4 %shard_map.81 = (bf16[512,256]{1,0:T(8,128)(2,1)S(1)}, f32[512,256]{1,0:T(8,128)S(1)}) custom-call(s32[3]{0:T(128)S(1)} %pad_add_fusion.ids, bf16[512,2048]{1,0:T(8,128)(2,1)S(1)} %copy-done, bf16[2,1024,1280]{2,1,0:T(8,128)(2,1)S(1)} %bitcast.19, bf16[2,1024,1280]{2,1,0:T(8,128)(2,1)S(1)} %bitcast.20, bf16[2,1024,1280]{2,1,0:T(8,128)(2,1)S(1)} %bitcast.21, ...), custom_call_target="tpu_custom_call" | custom-call | flops 536870912 | bytes 3000000 | tf_op jit(solution)/shard_map/pallas_call | solution.py:271
  13.5 1.4 %shard_map.82 = bf16[512,512]{1,0:T(8,128)(2,1)S(1)} custom-call(s32[3]{0:T(128)S(1)} %pad_add_fusion.ids, bf16[512,2048]{1,0:T(8,128)(2,1)S(1)} %collective-permute-done.x_ref, bf16[2,1024,1280]{2,1,0:T(8,128)(2,1)S(1)} %bitcast.26, bf16[2,1024,1280]{2,1,0:T(8,128)(2,1)S(1)} %bitcast.24, bf16[2,1024,1280]{2,1,0:T(8,128)(2,1)S(1)} %bitcast.25, ...), custom_call_target="tpu_custom_call" | custom-call | flops 536870912 | bytes 3000000 | tf_op jit(solution)/shard_map/pallas_call | solution.py:271
  15.3 1.4 %shard_map.83 = bf16[512,512]{1,0:T(8,128)(2,1)S(1)} custom-call(s32[3]{0:T(128)S(1)} %pad_add_fusion.ids, bf16[512,2048]{1,0:T(8,128)(2,1)S(1)} %collective-permute-done.x_ref, bf16[2,1024,1280]{2,1,0:T(8,128)(2,1)S(1)} %bitcast.27, bf16[2,1024,1280]{2,1,0:T(8,128)(2,1)S(1)} %bitcast.28, bf16[2,1024,1280]{2,1,0:T(8,128)(2,1)S(1)} %bitcast.29, ...), custom_call_target="tpu_custom_call" | custom-call | flops 536870912 | bytes 3000000 | tf_op jit(solution)/shard_map/pallas_call | solution.py:271
  16.9 1.4 %shard_map.84 = (bf16[512,256]{1,0:T(8,128)(2,1)S(1)}, f32[512,256]{1,0:T(8,128)S(1)}) custom-call(s32[3]{0:T(128)S(1)} %pad_add_fusion.ids, bf16[512,2048]{1,0:T(8,128)(2,1)S(1)} %copy-done, bf16[2,1024,1280]{2,1,0:T(8,128)(2,1)S(1)} %bitcast.31, bf16[2,1024,1280]{2,1,0:T(8,128)(2,1)S(1)} %bitcast.32, bf16[2,1024,1280]{2,1,0:T(8,128)(2,1)S(1)} %bitcast.33, ...), custom_call_target="tpu_custom_call" | custom-call | flops 536870912 | bytes 3000000 | tf_op jit(solution)/shard_map/pallas_call | solution.py:271
  18.2 1.4 %shard_map.85 = bf16[512,512]{1,0:T(8,128)(2,1)S(1)} custom-call(s32[3]{0:T(128)S(1)} %pad_add_fusion.ids, bf16[512,2048]{1,0:T(8,128)(2,1)S(1)} %collective-permute-done.x_ref, bf16[2,1024,1280]{2,1,0:T(8,128)(2,1)S(1)} %bitcast.35, bf16[2,1024,1280]{2,1,0:T(8,128)(2,1)S(1)} %bitcast.36, bf16[2,1024,1280]{2,1,0:T(8,128)(2,1)S(1)} %bitcast.37, ...), custom_call_target="tpu_custom_call" | custom-call | flops 536870912 | bytes 3000000 | tf_op jit(solution)/shard_map/pallas_call | solution.py:271
  20.0 2.6 %collective-permute-start.4 = (bf16[528,256]{1,0:T(8,128)(2,1)S(1)}, bf16[528,256]{1,0:T(8,128)(2,1)S(1)}, u32[]{:S(2)}, u32[]{:S(2)}) collective-permute-start(bf16[528,256]{1,0:T(8,128)(2,1)S(1)} %get-tuple-element.49), channel_id=1, source_target_pairs={{0,16},{8,24},{16,0},{24,8},{1,17},{9,25},{17,1},{25,9},{2,18},{10... | collective-permute-start | bytes 811016 | tf_op jit(solution)/shard_map/ppermute | solution.py:495
  22.7 7.0 %collective-permute-done.4.u_ref = bf16[528,256]{1,0:T(8,128)(2,1)S(1)} collective-permute-done((bf16[528,256]{1,0:T(8,128)(2,1)S(1)}, bf16[528,256]{1,0:T(8,128)(2,1)S(1)}, u32[]{:S(2)}, u32[]{:S(2)}) %collective-permute-start.4) | collective-permute-done | bytes 270368 | tf_op jit(solution)/shard_map/ppermute | solution.py:495
  29.7 0.6 shard_map.86
  30.3 1.8 %collective-permute-start.9 = (bf16[528,256]{1,0:T(8,128)(2,1)S(1)}, bf16[528,256]{1,0:T(8,128)(2,1)S(1)}, u32[]{:S(2)}, u32[]{:S(2)}) collective-permute-start(bf16[528,256]{1,0:T(8,128)(2,1)S(1)} %shard_map.86), channel_id=1, source_target_pairs={{0,8},{8,0},{16,24},{24,16},{1,9},{9,1},{17,25},{25,17},{2,10},{10... | collective-permute-start | bytes 811016 | tf_op jit(solution)/shard_map/ppermute | solution.py:496
  32.4 1.7 %collective-permute-start.8 = (bf16[512,256]{1,0:T(8,128)(2,1)S(1)}, bf16[512,256]{1,0:T(8,128)(2,1)S(1)}, u32[]{:S(2)}, u32[]{:S(2)}) collective-permute-start(bf16[512,256]{1,0:T(8,128)(2,1)S(1)} %get-tuple-element.55), channel_id=1, source_target_pairs={{0,16},{8,24},{16,0},{24,8},{1,17},{9,25},{17,1},{25,9},{2,18},{10... | collective-permute-start | bytes 786440 | tf_op jit(solution)/shard_map/ppermute | solution.py:495
  34.1 1.4 %shard_map.87 = (bf16[512,256]{1,0:T(8,128)(2,1)S(1)}, f32[512,256]{1,0:T(8,128)S(1)}) custom-call(s32[3]{0:T(128)S(1)} %pad_add_fusion.ids, bf16[512,2048]{1,0:T(8,128)(2,1)S(1)} %copy-done, bf16[2,1024,1280]{2,1,0:T(8,128)(2,1)S(1)} %bitcast.39, bf16[2,1024,1280]{2,1,0:T(8,128)(2,1)S(1)} %bitcast.40, bf16[2,1024,1280]{2,1,0:T(8,128)(2,1)S(1)} %bitcast.41, ...), custom_call_target="tpu_custom_call" | custom-call | flops 536870912 | bytes 3000000 | tf_op jit(solution)/shard_map/pallas_call | solution.py:271
  35.5 1.4 %shard_map.88 = (bf16[512,256]{1,0:T(8,128)(2,1)S(1)}, f32[512,256]{1,0:T(8,128)S(1)}) custom-call(s32[3]{0:T(128)S(1)} %pad_add_fusion.ids, bf16[512,2048]{1,0:T(8,128)(2,1)S(1)} %copy-done, bf16[2,1024,1280]{2,1,0:T(8,128)(2,1)S(1)} %bitcast.43, bf16[2,1024,1280]{2,1,0:T(8,128)(2,1)S(1)} %bitcast.44, bf16[2,1024,1280]{2,1,0:T(8,128)(2,1)S(1)} %bitcast.45, ...), custom_call_target="tpu_custom_call" | custom-call | flops 536870912 | bytes 3000000 | tf_op jit(solution)/shard_map/pallas_call | solution.py:271
  36.9 7.2 %collective-permute-done.7.u_ref.refs_4_ = bf16[512,256]{1,0:T(8,128)(2,1)S(1)} collective-permute-done((bf16[512,256]{1,0:T(8,128)(2,1)S(1)}, bf16[512,256]{1,0:T(8,128)(2,1)S(1)}, u32[]{:S(2)}, u32[]{:S(2)}) %collective-permute-start.7) | collective-permute-done | bytes 262176 | tf_op jit(solution)/shard_map/ppermute | solution.py:496
  44.2 0.6 shard_map.89
  44.8 0.6 shard_map.90
  45.4 2.2 %shard_map.91 = (bf16[768,256]{1,0:T(8,128)(2,1)S(1)}, bf16[512,128]{1,0:T(8,128)(2,1)S(1)}, f32[8,256]{1,0:T(8,128)S(1)}, f32[256,128]{1,0:T(8,128)S(1)}, f32[8...) custom-call(s32[3]{0:T(128)S(1)} %pad_add_fusion.ids, f32[16,512]{1,0:T(8,128)S(1)} %get-tuple-element.48.raw_ref, ...), custom_call_target="tpu_custom_call" | custom-call | flops 1000000000 | bytes 3000000 | tf_op jit(solution)/shard_map/pallas_call | solution.py:271
  47.7 1.5 %collective-permute-start.10 = (bf16[512,256]{1,0:T(8,128)(2,1)S(1)}, bf16[512,256]{1,0:T(8,128)(2,1)S(1)}, u32[]{:S(2)}, u32[]{:S(2)}) collective-permute-start(bf16[512,256]{1,0:T(8,128)(2,1)S(1)} %get-tuple-element.60), channel_id=1, source_target_pairs={{0,8},{8,0},{16,24},{24,16},{1,9},{9,1},{17,25},{25,17},{2,10},{10... | collective-permute-start | bytes 786440 | tf_op jit(solution)/shard_map/ppermute | solution.py:496
  49.8 1.5 %collective-permute-start.12 = (bf16[512,128]{1,0:T(8,128)(2,1)S(1)}, bf16[512,128]{1,0:T(8,128)(2,1)S(1)}, u32[]{:S(2)}, u32[]{:S(2)}) collective-permute-start(bf16[512,128]{1,0:T(8,128)(2,1)S(1)} %shard_map.89), channel_id=1, source_target_pairs={{0,16},{8,24},{16,0},{24,8},{1,17},{9,25},{17,1},{25,9},{2,18},{10... | collective-permute-start | bytes 393224 | tf_op jit(solution)/shard_map/ppermute | solution.py:495
  51.8 5.1 %collective-permute-done.10.u_ref.refs_4_ = bf16[512,256]{1,0:T(8,128)(2,1)S(1)} collective-permute-done((bf16[512,256]{1,0:T(8,128)(2,1)S(1)}, bf16[512,256]{1,0:T(8,128)(2,1)S(1)}, u32[]{:S(2)}, u32[]{:S(2)}) %collective-permute-start.10) | collective-permute-done | bytes 262176 | tf_op jit(solution)/shard_map/ppermute | solution.py:496
  56.9 0.6 shard_map.92
  57.5 1.5 %collective-permute-start.16 = (bf16[512,128]{1,0:T(8,128)(2,1)S(1)}, bf16[512,128]{1,0:T(8,128)(2,1)S(1)}, u32[]{:S(2)}, u32[]{:S(2)}) collective-permute-start(bf16[512,128]{1,0:T(8,128)(2,1)S(1)} %shard_map.92), channel_id=1, source_target_pairs={{0,16},{8,24},{16,0},{24,8},{1,17},{9,25},{17,1},{25,9},{2,18},{10... | collective-permute-start | bytes 393224 | tf_op jit(solution)/shard_map/ppermute | solution.py:495
  59.2 4.6 %shard_map.93 = (bf16[512,512]{1,0:T(8,128)(2,1)}, bf16[512,512]{1,0:T(8,128)(2,1)}) custom-call(s32[3]{0:T(128)S(1)} %pad_add_fusion.ids, f32[512,256]{1,0:T(8,128)S(1)} %get-tuple-element.66.keep_ref.refs_0_, bf16[512,256]{1,0:T(8,128)(2,1)S(1)} %collective-permute-done.8.u_ref.refs_1_, bf16[512,128]{1,0:T(8,128)(2,1)S(1)} %collective-permute-done.11.refs_2_, ...), custom_call_target="tpu_custom_call" | custom-call | flops 2000000000 | bytes 3000000 | tf_op jit(solution)/shard_map/pallas_call | solution.py:271
  63.8 0.6 shard_map.94
  64.4 1.5 %collective-permute-start.15 = (bf16[512,128]{1,0:T(8,128)(2,1)S(1)}, bf16[512,128]{1,0:T(8,128)(2,1)S(1)}, u32[]{:S(2)}, u32[]{:S(2)}) collective-permute-start(bf16[512,128]{1,0:T(8,128)(2,1)S(1)} %shard_map.94), channel_id=1, source_target_pairs={{0,8},{8,0},{16,24},{24,16},{1,9},{9,1},{17,25},{25,17},{2,10},{10... | collective-permute-start | bytes 393224 | tf_op jit(solution)/shard_map/ppermute | solution.py:496
  65.9 3.5 %collective-permute-done.15.refs_2_ = bf16[512,128]{1,0:T(8,128)(2,1)S(1)} collective-permute-done((bf16[512,128]{1,0:T(8,128)(2,1)S(1)}, bf16[512,128]{1,0:T(8,128)(2,1)S(1)}, u32[]{:S(2)}, u32[]{:S(2)}) %collective-permute-start.15) | collective-permute-done | bytes 131104 | tf_op jit(solution)/shard_map/ppermute | solution.py:496
  69.5 4.4 %shard_map.95 = (bf16[512,512]{1,0:T(8,128)(2,1)}, bf16[512,512]{1,0:T(8,128)(2,1)}) custom-call(s32[3]{0:T(128)S(1)} %pad_add_fusion.ids, f32[512,256]{1,0:T(8,128)S(1)} %get-tuple-element.81.keep_ref.refs_0_, bf16[512,256]{1,0:T(8,128)(2,1)S(1)} %collective-permute-done.14.u_ref.refs_1_, ...), custom_call_target="tpu_custom_call", output_to_operand_aliasing={{0}: (17, {}), {1}: (18, {})} | custom-call | flops 2000000000 | bytes 3000000 | tf_op jit(solution)/shard_map/pallas_call | solution.py:271
  (33 shorter events, 4.1 us)
Async XLA Ops:
  0.6 4.6 %collective-permute-start = (bf16[512,2048]{1,0:T(8,128)(2,1)}, bf16[512,2048]{1,0:T(8,128)(2,1)S(1)}, u32[]{:S(2)}, u32[]{:S(2)}) collective-permute-start(bf16[512,2048]{1,0:T(8,128)(2,1)} %refs_0_.9), channel_id=1, source_target_pairs={{0,4},{4,0},{1,5},{5,1},{2,6},{6,2},{3,7},{7,3},{8,12},{12,8},{9,1... | collective-permute-start | bytes 6291464 | tf_op jit(solution)/shard_map/ppermute | solution.py:497
  6.6 2.0 %copy-start = (bf16[512,2048]{1,0:T(8,128)(2,1)S(1)}, bf16[512,2048]{1,0:T(8,128)(2,1)}, u32[]{:S(2)}) copy-start(bf16[512,2048]{1,0:T(8,128)(2,1)} %refs_0_.9) | copy-start | bytes 6291460
  6.6 2.0 %copy-start.1 = (bf16[2048,16]{0,1:T(8,128)(2,1)S(1)}, bf16[2048,16]{0,1:T(8,128)(2,1)}, u32[]{:S(2)}) copy-start(bf16[2048,16]{0,1:T(8,128)(2,1)} %param.8) | copy-start | bytes 196612
  6.6 4.1 %collective-permute-start.1 = (bf16[512,512]{1,0:T(8,128)(2,1)S(1)}, bf16[512,512]{1,0:T(8,128)(2,1)S(1)}, u32[]{:S(2)}, u32[]{:S(2)}) collective-permute-start(bf16[512,512]{1,0:T(8,128)(2,1)S(1)} %shard_map.77), channel_id=1, source_target_pairs={{0,4},{4,0},{1,5},{5,1},{2,6},{6,2},{3,7},{7,3},{8,12},{12,8},{9,1... | collective-permute-start | bytes 1572872 | tf_op jit(solution)/shard_map/ppermute | solution.py:497
  8.4 3.7 %collective-permute-start.2 = (bf16[512,512]{1,0:T(8,128)(2,1)S(1)}, bf16[512,512]{1,0:T(8,128)(2,1)S(1)}, u32[]{:S(2)}, u32[]{:S(2)}) collective-permute-start(bf16[512,512]{1,0:T(8,128)(2,1)S(1)} %shard_map.78), channel_id=1, source_target_pairs={{0,4},{4,0},{1,5},{5,1},{2,6},{6,2},{3,7},{7,3},{8,12},{12,8},{9,1... | collective-permute-start | bytes 1572872 | tf_op jit(solution)/shard_map/ppermute | solution.py:497
  14.8 2.0 %collective-permute-start.3 = (bf16[512,512]{1,0:T(8,128)(2,1)S(1)}, bf16[512,512]{1,0:T(8,128)(2,1)S(1)}, u32[]{:S(2)}, u32[]{:S(2)}) collective-permute-start(bf16[512,512]{1,0:T(8,128)(2,1)S(1)} %shard_map.82), channel_id=1, source_target_pairs={{0,4},{4,0},{1,5},{5,1},{2,6},{6,2},{3,7},{7,3},{8,12},{12,8},{9,1... | collective-permute-start | bytes 1572872 | tf_op jit(solution)/shard_map/ppermute | solution.py:497
  16.6 17.5 %collective-permute-start.5 = (bf16[512,512]{1,0:T(8,128)(2,1)S(1)}, bf16[512,512]{1,0:T(8,128)(2,1)S(1)}, u32[]{:S(2)}, u32[]{:S(2)}) collective-permute-start(bf16[512,512]{1,0:T(8,128)(2,1)S(1)} %shard_map.83), channel_id=1, source_target_pairs={{0,4},{4,0},{1,5},{5,1},{2,6},{6,2},{3,7},{7,3},{8,12},{12,8},{9,1... | collective-permute-start | bytes 1572872 | tf_op jit(solution)/shard_map/ppermute | solution.py:497
  19.6 15.9 %collective-permute-start.6 = (bf16[512,512]{1,0:T(8,128)(2,1)S(1)}, bf16[512,512]{1,0:T(8,128)(2,1)S(1)}, u32[]{:S(2)}, u32[]{:S(2)}) collective-permute-start(bf16[512,512]{1,0:T(8,128)(2,1)S(1)} %shard_map.85), channel_id=1, source_target_pairs={{0,4},{4,0},{1,5},{5,1},{2,6},{6,2},{3,7},{7,3},{8,12},{12,8},{9,1... | collective-permute-start | bytes 1572872 | tf_op jit(solution)/shard_map/ppermute | solution.py:497
  20.0 9.7 %collective-permute-start.4 = (bf16[528,256]{1,0:T(8,128)(2,1)S(1)}, bf16[528,256]{1,0:T(8,128)(2,1)S(1)}, u32[]{:S(2)}, u32[]{:S(2)}) collective-permute-start(bf16[528,256]{1,0:T(8,128)(2,1)S(1)} %get-tuple-element.49), channel_id=1, source_target_pairs={{0,16},{8,24},{16,0},{24,8},{1,17},{9,25},{17,1},{25,9},{2,18},{10... | collective-permute-start | bytes 811016 | tf_op jit(solution)/shard_map/ppermute | solution.py:495
  30.3 15.1 %collective-permute-start.9 = (bf16[528,256]{1,0:T(8,128)(2,1)S(1)}, bf16[528,256]{1,0:T(8,128)(2,1)S(1)}, u32[]{:S(2)}, u32[]{:S(2)}) collective-permute-start(bf16[528,256]{1,0:T(8,128)(2,1)S(1)} %shard_map.86), channel_id=1, source_target_pairs={{0,8},{8,0},{16,24},{24,16},{1,9},{9,1},{17,25},{25,17},{2,10},{10... | collective-permute-start | bytes 811016 | tf_op jit(solution)/shard_map/ppermute | solution.py:496
  32.1 12.1 %collective-permute-start.7 = (bf16[512,256]{1,0:T(8,128)(2,1)S(1)}, bf16[512,256]{1,0:T(8,128)(2,1)S(1)}, u32[]{:S(2)}, u32[]{:S(2)}) collective-permute-start(bf16[512,256]{1,0:T(8,128)(2,1)S(1)} %get-tuple-element.51), channel_id=1, source_target_pairs={{0,8},{8,0},{16,24},{24,16},{1,9},{9,1},{17,25},{25,17},{2,10},{10... | collective-permute-start | bytes 786440 | tf_op jit(solution)/shard_map/ppermute | solution.py:496
  32.4 12.4 %collective-permute-start.8 = (bf16[512,256]{1,0:T(8,128)(2,1)S(1)}, bf16[512,256]{1,0:T(8,128)(2,1)S(1)}, u32[]{:S(2)}, u32[]{:S(2)}) collective-permute-start(bf16[512,256]{1,0:T(8,128)(2,1)S(1)} %get-tuple-element.55), channel_id=1, source_target_pairs={{0,16},{8,24},{16,0},{24,8},{1,17},{9,25},{17,1},{25,9},{2,18},{10... | collective-permute-start | bytes 786440 | tf_op jit(solution)/shard_map/ppermute | solution.py:495
  35.5 9.9 %copy-start.2 = (f32[4]{0:T(128)S(1)}, f32[4]{0:T(128)}, u32[]{:S(2)}) copy-start(f32[4]{0:T(128)} %bias_ref.1) | copy-start | bytes 52
  35.5 9.9 %copy-start.3 = (f32[4]{0:T(128)S(1)}, f32[4]{0:T(128)}, u32[]{:S(2)}) copy-start(f32[4]{0:T(128)} %rate_ref.1) | copy-start | bytes 52
  36.9 22.3 %copy-start.4 = (f32[4]{0:T(128)S(1)}, f32[4]{0:T(128)}, u32[]{:S(2)}) copy-start(f32[4]{0:T(128)} %refs_15_.3) | copy-start | bytes 52
  47.6 11.6 %collective-permute-start.13 = (bf16[768,256]{1,0:T(8,128)(2,1)S(1)}, bf16[768,256]{1,0:T(8,128)(2,1)S(1)}, u32[]{:S(2)}, u32[]{:S(2)}) collective-permute-start(bf16[768,256]{1,0:T(8,128)(2,1)S(1)} %get-tuple-element.70.refs_8_), channel_id=1, source_target_pairs={{0,4},{4,0},{1,5},{5,1},{2,6},{6,2},{3,7},{7,3},{8,12},{12,8},{9,1... | collective-permute-start | bytes 1179656 | tf_op jit(solution)/shard_map/ppermute | solution.py:497
  47.7 9.2 %collective-permute-start.10 = (bf16[512,256]{1,0:T(8,128)(2,1)S(1)}, bf16[512,256]{1,0:T(8,128)(2,1)S(1)}, u32[]{:S(2)}, u32[]{:S(2)}) collective-permute-start(bf16[512,256]{1,0:T(8,128)(2,1)S(1)} %get-tuple-element.60), channel_id=1, source_target_pairs={{0,8},{8,0},{16,24},{24,16},{1,9},{9,1},{17,25},{25,17},{2,10},{10... | collective-permute-start | bytes 786440 | tf_op jit(solution)/shard_map/ppermute | solution.py:496
  49.2 10.0 %collective-permute-start.11 = (bf16[512,128]{1,0:T(8,128)(2,1)S(1)}, bf16[512,128]{1,0:T(8,128)(2,1)S(1)}, u32[]{:S(2)}, u32[]{:S(2)}) collective-permute-start(bf16[512,128]{1,0:T(8,128)(2,1)S(1)} %shard_map.90), channel_id=1, source_target_pairs={{0,8},{8,0},{16,24},{24,16},{1,9},{9,1},{17,25},{25,17},{2,10},{10... | collective-permute-start | bytes 393224 | tf_op jit(solution)/shard_map/ppermute | solution.py:496
  49.8 9.4 %collective-permute-start.12 = (bf16[512,128]{1,0:T(8,128)(2,1)S(1)}, bf16[512,128]{1,0:T(8,128)(2,1)S(1)}, u32[]{:S(2)}, u32[]{:S(2)}) collective-permute-start(bf16[512,128]{1,0:T(8,128)(2,1)S(1)} %shard_map.89), channel_id=1, source_target_pairs={{0,16},{8,24},{16,0},{24,8},{1,17},{9,25},{17,1},{25,9},{2,18},{10... | collective-permute-start | bytes 393224 | tf_op jit(solution)/shard_map/ppermute | solution.py:495
  51.2 12.6 %collective-permute-start.14 = (bf16[512,256]{1,0:T(8,128)(2,1)S(1)}, bf16[512,256]{1,0:T(8,128)(2,1)S(1)}, u32[]{:S(2)}, u32[]{:S(2)}) collective-permute-start(bf16[512,256]{1,0:T(8,128)(2,1)S(1)} %get-tuple-element.62), channel_id=1, source_target_pairs={{0,16},{8,24},{16,0},{24,8},{1,17},{9,25},{17,1},{25,9},{2,18},{10... | collective-permute-start | bytes 786440 | tf_op jit(solution)/shard_map/ppermute | solution.py:495
  57.5 8.4 %collective-permute-start.16 = (bf16[512,128]{1,0:T(8,128)(2,1)S(1)}, bf16[512,128]{1,0:T(8,128)(2,1)S(1)}, u32[]{:S(2)}, u32[]{:S(2)}) collective-permute-start(bf16[512,128]{1,0:T(8,128)(2,1)S(1)} %shard_map.92), channel_id=1, source_target_pairs={{0,16},{8,24},{16,0},{24,8},{1,17},{9,25},{17,1},{25,9},{2,18},{10... | collective-permute-start | bytes 393224 | tf_op jit(solution)/shard_map/ppermute | solution.py:495
  64.4 5.0 %collective-permute-start.15 = (bf16[512,128]{1,0:T(8,128)(2,1)S(1)}, bf16[512,128]{1,0:T(8,128)(2,1)S(1)}, u32[]{:S(2)}, u32[]{:S(2)}) collective-permute-start(bf16[512,128]{1,0:T(8,128)(2,1)S(1)} %shard_map.94), channel_id=1, source_target_pairs={{0,8},{8,0},{16,24},{24,16},{1,9},{9,1},{17,25},{25,17},{2,10},{10... | collective-permute-start | bytes 393224 | tf_op jit(solution)/shard_map/ppermute | solution.py:496

commit v4 on v3

--- a/solution.py
+++ b/solution.py
@@ -184,26 +184,39 @@
     return pl.CostEstimate(flops=flops, bytes_accessed=moved, transcendentals=0)
 
 
-def joined(refs):
-    return jnp.concatenate([ref[(0,) * (len(ref.shape) - 2)] for ref in refs], axis=1)
-
-
-def project_kernel(ids, x_ref, w0, w1, w2, w3, out_ref):
+def place_of():
+    grp = lax.axis_index("grp")
+    return grp // 2, grp % 2, lax.axis_index("seq")
+
+
+def gathered(w_ref, blocks):
+    return jnp.concatenate(
+        [w_ref[kv, :, pl.ds(pl.multiple_of(col * LANES, LANES), LANES)] for kv, col in blocks], axis=1
+    )
+
+
+def own_columns(x_ref, rows):
+    first = pl.multiple_of(lax.axis_index("seq") * rows, LANES)
+    return x_ref[:, pl.ds(first, rows)]
+
+
+def project_kernel(places, order, x_ref, w_ref, out_ref):
+    high, low, _ = place_of()
+    weights = gathered(w_ref, places(high, low))
     out_ref[...] = jnp.dot(
-        x_ref[...], joined((w0, w1, w2, w3)), preferred_element_type=F32
+        own_columns(x_ref, w_ref.shape[1]), weights, preferred_element_type=F32
     ).astype(BF16)
 
 
-def add_halves(x_ref, w0, w1, w2, w3, r_ref, send_ref, keep_ref):
+def project_add_kernel(places, order, x_ref, w_ref, r_ref, send_ref, keep_ref):
+    high, low, _ = place_of()
+    blocks = places(high, low)
     tok, half = keep_ref.shape
-    first = jnp.dot(x_ref[...], joined((w0, w1)), preferred_element_type=F32)
+    tokens = own_columns(x_ref, w_ref.shape[1])
+    first = jnp.dot(tokens, gathered(w_ref, blocks[:2]), preferred_element_type=F32)
     send_ref[:tok, :] = (first + r_ref[:, :half].astype(F32)).astype(BF16)
-    second = jnp.dot(x_ref[...], joined((w2, w3)), preferred_element_type=F32)
+    second = jnp.dot(tokens, gathered(w_ref, blocks[2:]), preferred_element_type=F32)
     keep_ref[...] = second + r_ref[:, half:].astype(F32)
-
-
-def project_add_kernel(ids, *refs):
-    add_halves(*refs)
 
 
 def folded(rates):
@@ -216,95 +229,89 @@
     return jnp.concatenate([rows[:half], rows[half:]], axis=1)
 
 
-def project_pair_kernel(ids, raw_ref, *refs):
-    add_halves(*refs)
+def project_pair_kernel(places, order, raw_ref, *refs):
+    project_add_kernel(places, order, *refs)
     send_ref, tok = refs[-2], refs[-1].shape[0]
     away = EXTRA // 2
-    rates = jnp.where(ids[0] == 0, raw_ref[away:, :], raw_ref[:away, :])
+    rates = jnp.where(place_of()[0] == 0, raw_ref[away:, :], raw_ref[:away, :])
     send_ref[tok:, :] = folded(rates).astype(BF16)
 
 
-def own_rates(ids, raw_ref, u_ref):
+def own_rates(raw_ref, u_ref):
     tok = raw_ref.shape[1]
     own = EXTRA // 2
-    rates = jnp.where(ids[0] == 0, raw_ref[:own, :], raw_ref[own:, :])
+    rates = jnp.where(place_of()[0] == 0, raw_ref[:own, :], raw_ref[own:, :])
     return rates + unfolded(u_ref[tok:, :].astype(F32))
 
 
-def pair_middle_kernel(ids, raw_ref, keep_ref, u_ref, send_ref):
+def pair_middle_kernel(order, raw_ref, keep_ref, u_ref, send_ref):
     tok = keep_ref.shape[0]
     send_ref[:tok, :] = (keep_ref[...] + u_ref[:tok, :].astype(F32)).astype(BF16)
-    send_ref[tok:, :] = folded(own_rates(ids, raw_ref, u_ref)).astype(BF16)
-
-
-def middle_kernel(ids, keep_ref, u_ref, send_ref):
-    send_ref[...] = (keep_ref[...] + u_ref[...].astype(F32)).astype(BF16)
-
-
-def prepare_kernel(ids, x_ref, rates_ref, raw_ref, cos_ref, sin_ref):
+    send_ref[tok:, :] = folded(own_rates(raw_ref, u_ref)).astype(BF16)
+
+
+def middle_kernel(order, keep_ref, u_ref, send_ref):
+    send_ref[...] = (keep_ref[:, :LANES] + u_ref[:, :LANES].astype(F32)).astype(BF16)
+
+
+def prepare_kernel(order, x_ref, rates_ref, raw_ref, cos_ref, sin_ref):
     raw_ref[...] = lax.dot_general(
         rates_ref[...], x_ref[...], LAST, preferred_element_type=F32
     )
     tok, wide = cos_ref.shape
     half = wide // 2
-    row = lax.broadcasted_iota(jnp.int32, (tok, wide), 0) + ids[2] * tok
+    fine = EXTRA
     lane = lax.broadcasted_iota(jnp.int32, (1, wide), 1)
     slot = jnp.where(lane < half, lane, lane - half).astype(F32)
     freq = jnp.exp(slot * (-2.0 / wide * math.log(ROPE_BASE)))
-    angle = row.astype(F32) * freq
-    cos_ref[...] = jnp.cos(angle)
-    sine = jnp.sin(angle)
-    sin_ref[...] = jnp.where(lane < half, -sine, sine)
-
-
-def weight_spec(weights, place):
-    ndim = weights.ndim
-    block = (1,) * (ndim - 2) + (weights.shape[-2], LANES)
-    return pl.BlockSpec(block, lambda step, ids: place(ids[0], ids[1]))
-
-
-def flat(shape):
-    return pl.BlockSpec(shape, lambda step, ids, n=len(shape): (0,) * n)
-
-
-def call(kernel, ids, specs, args, shapes, flops, aliases={}, out_specs=None, grant=GRANTS[1]):
+    start = lax.axis_index("seq") * tok
+    coarse = lax.broadcasted_iota(jnp.int32, (tok // fine, wide), 0) * fine + start
+    coarse = coarse.astype(F32) * freq
+    small = lax.broadcasted_iota(jnp.int32, (fine, wide), 0).astype(F32) * freq
+    cos_big, sin_big = jnp.cos(coarse), jnp.sin(coarse)
+    cos_small, sin_small = jnp.cos(small), jnp.sin(small)
+    sign = jnp.where(lane < half, -1.0, 1.0)
+    for at in range(tok // fine):
+        c, d = cos_big[at : at + 1, :], sin_big[at : at + 1, :]
+        span = slice(at * fine, (at + 1) * fine)
+        cos_ref[span, :] = c * cos_small - d * sin_small
+        sin_ref[span, :] = (d * cos_small + c * sin_small) * sign
+
+
+VMEM = pl.BlockSpec(memory_space=pltpu.VMEM)
+SMEM = pl.BlockSpec(memory_space=pltpu.SMEM)
+ANY = pl.BlockSpec(memory_space=pl.ANY)
+
+
+def call(kernel, order, args, shapes, flops, in_specs=None, **rest):
     return pl.pallas_call(
         kernel,
-        grid_spec=pltpu.PrefetchScalarGridSpec(
-            num_scalar_prefetch=1,
-            grid=(1,),
-            in_specs=specs,
-            out_specs=out_specs or [flat(s) for s, _ in shapes],
-        ),
+        in_specs=[ANY] + (in_specs or [VMEM] * len(args)),
+        out_specs=rest.pop("out_specs", [VMEM] * len(shapes)),
         out_shape=[jax.ShapeDtypeStruct(s, d) for s, d in shapes],
-        input_output_aliases=aliases,
-        compiler_params=pltpu.CompilerParams(vmem_limit_bytes=grant),
+        compiler_params=pltpu.CompilerParams(vmem_limit_bytes=rest.pop("grant", GRANTS[1])),
         cost_estimate=cost(flops, 3 * 10**6),
-    )(ids, *args)
-
-
-def project(ids, x, x_block, weights, places):
-    tok, rows = x.shape[0], weights.shape[-2]
-    wide = len(places) * LANES
-    specs = [pl.BlockSpec((tok, rows), x_block)]
-    specs += [weight_spec(weights, place) for place in places]
-    args = [x] + [weights] * len(places)
-    return call(project_kernel, ids, specs, args, [((tok, wide), BF16)], 2 * tok * rows * wide)[0]
-
-
-def project_add(ids, x, x_block, weights, places, received, raw=None):
-    tok, rows = x.shape[0], weights.shape[-2]
-    wide = len(places) * LANES
-    half = wide // 2
-    specs = [pl.BlockSpec((tok, rows), x_block)]
-    specs += [weight_spec(weights, place) for place in places] + [flat(received.shape)]
-    args = [x] + [weights] * len(places) + [received]
-    tall, kernel = tok, project_add_kernel
+        **rest,
+    )(order, *args)
+
+
+def project(order, x, weights, places):
+    tok, rows = x.shape[0], weights.shape[1]
+    wide = 4 * LANES
+    return call(
+        functools.partial(project_kernel, places), order, [x, weights],
+        [((tok, wide), BF16)], 2 * tok * rows * wide,
+    )
+
+
+def project_add(order, x, weights, places, received, raw):
+    tok, rows = x.shape[0], weights.shape[1]
+    wide = 4 * LANES
+    args, tall, kernel = [x, weights, received], tok, project_add_kernel
     if raw is not None:
-        specs, args = [flat(raw.shape)] + specs, [raw] + args
-        tall, kernel = tok + EXTRA, project_pair_kernel
-    shapes = [((tall, half), BF16), ((tok, half), F32)]
-    return call(kernel, ids, specs, args, shapes, 2 * tok * rows * wide)
+        args, tall, kernel = [raw] + args, tok + EXTRA, project_pair_kernel
+    shapes = [((tall, wide // 2), BF16), ((tok, wide // 2), F32)]
+    return call(functools.partial(kernel, places), order, args, shapes, 2 * tok * rows * wide)
 
 
 def turn(vectors, cosine, sine):
@@ -323,7 +330,7 @@
 
 
 def context_kernel(
-    stretch, ids, raw_ref, keep_ref, u_ref, z_ref, cos_ref, sin_ref, bias_ref, rate_ref,
+    stretch, order, raw_ref, keep_ref, u_ref, z_ref, cos_ref, sin_ref, bias_ref, rate_ref,
     carry_ref, bterm_ref, across_ref, down_ref, step_ref, first_ref,
 ):
     tok = keep_ref.shape[0]
@@ -336,8 +343,8 @@
     carry_ref[:tok, :HEAD_DIM] = turn(keys, cos_ref[...], sin_ref[...]).astype(BF16)
     carry_ref[:tok, HEAD_DIM:] = values
     bterm_ref[...] = bterm
-    both = own_rates(ids, raw_ref, u_ref) + unfolded(z_ref[tok:, :].astype(F32))
-    raw = jnp.where(ids[1] == 0, both[:heads], both[heads:])
+    both = own_rates(raw_ref, u_ref) + unfolded(z_ref[tok:, :].astype(F32))
+    raw = jnp.where(place_of()[1] == 0, both[:heads], both[heads:])
     which = lax.broadcasted_iota(jnp.int32, (heads, 1), 0)
     bias = jnp.full((heads, 1), bias_ref[0], F32)
     rate = jnp.full((heads, 1), rate_ref[0], F32)
@@ -386,17 +393,16 @@
         carry_ref[row : row + HEAD_DIM, col : col + HEAD_DIM] = states[h].astype(BF16)
 
 
-def heads_kernel(stretch, numbers, ids, *refs):
-    refs = list(refs)
-    pieces = refs[: 3 * len(numbers)]
-    (cos_ref, sin_ref, carry_ref, bterm_ref, came_ref, across_ref, down_ref, step_ref,
-     first_ref, skip_ref) = refs[3 * len(numbers) : 3 * len(numbers) + 10]
-    teacher_ref, student_ref = refs[-2:]
+def head_kernel(
+    stretch, head, order, keep_ref, u_ref, z_ref, cos_ref, sin_ref, carry_ref, bterm_ref, came_ref,
+    across_ref, down_ref, step_ref, first_ref, skip_ref, *rest,
+):
+    teacher_out, student_out, teacher_ref, student_ref, sems = rest[-5:]
     tok = bterm_ref.shape[0]
     heads = first_ref.shape[0]
     scale = HEAD_DIM ** (-0.5)
     power = scale * 1.4426950408889634
-    later = (ids[2] > 0).astype(F32)
+    later = (lax.axis_index("seq") > 0).astype(F32)
     blocked = (1.0 - later) * FAR_BELOW
     rows = lax.broadcasted_iota(jnp.int32, (stretch, stretch), 0)
     cols = lax.broadcasted_iota(jnp.int32, (stretch, stretch), 1)
@@ -406,75 +412,73 @@
     prev_keys = came_ref[:tok, :HEAD_DIM]
     own_values = jnp.concatenate([carry_ref[:tok, HEAD_DIM:], ones], axis=1)
     prev_values = jnp.concatenate([came_ref[:tok, HEAD_DIM:], ones], axis=1)
-    for at, head in enumerate(numbers):
-        keep_ref, u_ref, z_ref = pieces[3 * at : 3 * at + 3]
-        place = slice(at * HEAD_DIM, (at + 1) * HEAD_DIM)
-        query = keep_ref[...] + u_ref[...].astype(F32) + z_ref[...].astype(F32)
-        turned = turn(query, cos_ref[...], sin_ref[...]).astype(BF16)
-        cterm = query.astype(BF16)
-        row, col = tok + (head // 2) * HEAD_DIM, (head % 2) * HEAD_DIM
-        state = came_ref[row : row + HEAD_DIM, col : col + HEAD_DIM].astype(F32) * later
-        skip = skip_ref[head]
-        for index in range(tok // stretch):
-            span = slice(index * stretch, (index + 1) * stretch)
-            reach = (index + 1) * stretch
-            queries = turned[span]
-            far = lax.dot_general(queries, prev_keys, LAST, preferred_element_type=F32) + blocked
-            near = lax.dot_general(queries, own_keys[:reach], LAST, preferred_element_type=F32)
-            diagonal = jnp.where(causal, near[:, index * stretch :], FAR_BELOW)
-            if index > 0:
-                near = jnp.concatenate([near[:, : index * stretch], diagonal], axis=1)
-            else:
-                near = diagonal
-            top = jnp.maximum(
-                jnp.max(far, axis=1, keepdims=True), jnp.max(near, axis=1, keepdims=True)
-            )
-            far = jnp.exp2((far - top) * power).astype(BF16)
-            near = jnp.exp2((near - top) * power).astype(BF16)
-            mixed = jnp.dot(far, prev_values, preferred_element_type=F32) + jnp.dot(
-                near, own_values[:reach], preferred_element_type=F32
-            )
-            teacher_ref[span, place] = (mixed[:, :HEAD_DIM] / mixed[:, HEAD_DIM:]).astype(BF16)
-            values = carry_ref[span, HEAD_DIM:]
-            which = index * heads + head
-            down = down_ref[:, which : which + 1]
-            across = across_ref[which : which + 1, :]
-            gram = lax.dot_general(
-                cterm[span], bterm_ref[span, :], LAST, preferred_element_type=F32
-            ) * (step_ref[which : which + 1, :] * scale)
-            mix = jnp.where(causal, jnp.exp(jnp.where(causal, down - across, -1e4)) * gram, 0.0)
-            inner = jnp.dot(mix.astype(BF16), values, preferred_element_type=F32)
-            high = state.astype(BF16)
-            low = (state - high.astype(F32)).astype(BF16)
-            carried = jnp.dot(
-                cterm[span], jnp.concatenate([high, low], axis=1), preferred_element_type=F32
-            )
-            carried = (carried[:, :HEAD_DIM] + carried[:, HEAD_DIM:]) * (jnp.exp(down) * scale)
-            student_ref[span, place] = (inner + carried + skip * values.astype(F32)).astype(BF16)
-            if index == 0:
-                state = jnp.exp(across[:, stretch - 1 :]) * state + first_ref[head]
-
-
-def heads_call(ids, group_at, numbers, pieces, shared, total, before):
-    tok = pieces[0][0].shape[0]
-    column = lambda col: pl.BlockSpec((tok, LANES), lambda step, ids, col=col: (0, col))
-    specs, args = [], []
-    for keep, u, z in pieces:
-        specs += [column(1), column(1), column(0)]
-        args += [keep, u, z]
-    specs += [flat(a.shape) for a in shared[:-1]] + [pl.BlockSpec(memory_space=pltpu.SMEM)]
-    args += list(shared)
+    query = keep_ref[:, LANES:] + u_ref[:, LANES:].astype(F32) + z_ref[...].astype(F32)
+    turned = turn(query, cos_ref[...], sin_ref[...]).astype(BF16)
+    cterm = query.astype(BF16)
+    row, col = tok + (head // 2) * HEAD_DIM, (head % 2) * HEAD_DIM
+    state = came_ref[row : row + HEAD_DIM, col : col + HEAD_DIM].astype(F32) * later
+    place = slice(head * HEAD_DIM, (head + 1) * HEAD_DIM)
+    copies = []
+    skip = skip_ref[head]
+    for index in range(tok // stretch):
+        span = slice(index * stretch, (index + 1) * stretch)
+        reach = (index + 1) * stretch
+        queries = turned[span]
+        far = lax.dot_general(queries, prev_keys, LAST, preferred_element_type=F32) + blocked
+        near = lax.dot_general(queries, own_keys[:reach], LAST, preferred_element_type=F32)
+        diagonal = jnp.where(causal, near[:, index * stretch :], FAR_BELOW)
+        if index > 0:
+            near = jnp.concatenate([near[:, : index * stretch], diagonal], axis=1)
+        else:
+            near = diagonal
+        top = jnp.maximum(
+            jnp.max(far, axis=1, keepdims=True), jnp.max(near, axis=1, keepdims=True)
+        )
+        far = jnp.exp2((far - top) * power).astype(BF16)
+        near = jnp.exp2((near - top) * power).astype(BF16)
+        mixed = jnp.dot(far, prev_values, preferred_element_type=F32) + jnp.dot(
+            near, own_values[:reach], preferred_element_type=F32
+        )
+        teacher_ref[span, :] = (mixed[:, :HEAD_DIM] / mixed[:, HEAD_DIM:]).astype(BF16)
+        values = carry_ref[span, HEAD_DIM:]
+        which = index * heads + head
+        down = down_ref[:, which : which + 1]
+        across = across_ref[which : which + 1, :]
+        gram = lax.dot_general(
+            cterm[span], bterm_ref[span, :], LAST, preferred_element_type=F32
+        ) * (step_ref[which : which + 1, :] * scale)
+        mix = jnp.where(causal, jnp.exp(jnp.where(causal, down - across, -1e4)) * gram, 0.0)
+        inner = jnp.dot(mix.astype(BF16), values, preferred_element_type=F32)
+        high = state.astype(BF16)
+        low = (state - high.astype(F32)).astype(BF16)
+        carried = jnp.dot(
+            cterm[span], jnp.concatenate([high, low], axis=1), preferred_element_type=F32
+        )
+        carried = (carried[:, :HEAD_DIM] + carried[:, HEAD_DIM:]) * (jnp.exp(down) * scale)
+        student_ref[span, :] = (inner + carried + skip * values.astype(F32)).astype(BF16)
+        if index == 0:
+            state = jnp.exp(across[:, stretch - 1 :]) * state + first_ref[head]
+        for kind, (held, out) in enumerate(((teacher_ref, teacher_out), (student_ref, student_out))):
+            copy = pltpu.make_async_copy(held.at[span, :], out.at[span, place], sems.at[kind, index])
+            copy.start()
+            copies.append(copy)
+    for copy in copies:
+        copy.wait()
+
+
+def head_call(order, head, piece, shared, total, before):
+    tok = piece[0].shape[0]
+    args = list(piece) + list(shared)
+    specs = [VMEM] * (len(args) - 1) + [SMEM]
     aliases = {}
     if before is not None:
         aliases = {1 + len(args): 0, 2 + len(args): 1}
-        specs += [pl.BlockSpec(memory_space=pl.ANY)] * 2
-        args += list(before)
-    wide = len(numbers) * LANES
-    block = pl.BlockSpec((tok, wide), lambda step, ids: (0, group_at))
+        args, specs = args + list(before), specs + [ANY] * 2
+    held = pltpu.VMEM((tok, HEAD_DIM), BF16)
     return call(
-        functools.partial(heads_kernel, STRETCH, numbers),
-        ids, specs, args, [((tok, total), BF16)] * 2, 2 * 10**9, aliases, [block] * 2,
-        GRANTS[3],
+        functools.partial(head_kernel, STRETCH, head), order, args, [((tok, total), BF16)] * 2, 10**9,
+        specs, out_specs=[ANY] * 2, input_output_aliases=aliases, grant=GRANTS[3],
+        scratch_shapes=[held, held, pltpu.SemaphoreType.DMA((2, tok // STRETCH))],
     )
 
 
@@ -486,40 +490,31 @@
     tok, _ = layer_input.shape
     heads = rate_bias.shape[0]
     group = HEADS // KV_HEADS
-    grp = lax.axis_index("grp")
-    seq = lax.axis_index("seq")
-    ids = jnp.stack([grp // 2, grp % 2, seq]).astype(jnp.int32)
+    ids = skip_gain[:1]
     count = lax.axis_size("grp")
     swap_high = [(g, g ^ 2) for g in range(count)]
     swap_low = [(g, g ^ 1) for g in range(count)]
     over_high = lambda a: lax.ppermute(a, "grp", swap_high)
     over_low = lambda a: lax.ppermute(a, "grp", swap_low)
     over_seq = lambda a: lax.ppermute(a, "seq", [(0, 1), (1, 0)])
-    own_block = lambda step, ids: (0, ids[2])
 
     other = over_seq(layer_input)
     weights_all = jnp.transpose(attn_weight, (1, 0, 2))
-    args = [layer_input, rate_weight.T]
     shapes = [((EXTRA, tok), F32), ((tok, HEAD_DIM), F32), ((tok, HEAD_DIM), F32)]
-    raw, cosine, sine = call(
-        prepare_kernel, ids, [flat(a.shape) for a in args], args, shapes, 10**9
-    )
-
-    pair_places = [
-        lambda h, l: (1 - h, 0, group), lambda h, l: (1 - h, 0, group + 1),
-        lambda h, l: (h, 0, group), lambda h, l: (h, 0, group + 1),
-    ]
+
+    def pair_places(h, l):
+        return [(1 - h, group), (1 - h, group + 1), (h, group), (h, group + 1)]
 
     def high_places(j):
-        return [
-            lambda h, l: (1 - h, 0, (1 - l) * heads + j), lambda h, l: (1 - h, 0, l * heads + j),
-            lambda h, l: (h, 0, (1 - l) * heads + j), lambda h, l: (h, 0, l * heads + j),
+        return lambda h, l: [
+            (1 - h, (1 - l) * heads + j), (1 - h, l * heads + j),
+            (h, (1 - l) * heads + j), (h, l * heads + j),
         ]
 
     def low_places(j):
-        return [
-            lambda h, l: (1 - h, 0, (1 - l) * heads + j), lambda h, l: (h, 0, (1 - l) * heads + j),
-            lambda h, l: (1 - h, 0, l * heads + j), lambda h, l: (h, 0, l * heads + j),
+        return lambda h, l: [
+            (1 - h, (1 - l) * heads + j), (h, (1 - l) * heads + j),
+            (1 - h, l * heads + j), (h, l * heads + j),
         ]
 
     other, weights_all = lax.optimization_barrier((other, weights_all))
@@ -539,14 +534,14 @@
 
     def cross(at):
         _, weights, places, _, _ = plan[at]
-        out = queued(lambda ready: [project(ready, other, own_block, weights, places)])[0]
+        out = queued(lambda ready: project(ready, other, weights, places))[0]
         crossed[at] = over_seq(out)
 
     def mine(at):
         j, weights, places, first, _ = plan[at]
         send, kept[at] = queued(
             lambda ready: project_add(
-                ready, layer_input, own_block, weights, places, crossed[at],
+                ready, layer_input, weights, places, crossed[at],
                 raw if j is None else None,
             )
         )
@@ -556,20 +551,11 @@
         j, _, _, _, second = plan[at]
         keep, u = kept[at], parts[at]
         if j is None:
-            args = [raw, keep, u]
             shapes = [((tok + EXTRA, 2 * HEAD_DIM), BF16)]
-            send = queued(
-                lambda ready: call(
-                    pair_middle_kernel, ready, [flat(a.shape) for a in args], args, shapes, 10**7
-                )
-            )[0]
+            send = queued(lambda ready: call(pair_middle_kernel, ready, [raw, keep, u], shapes, 10**7))[0]
         else:
-            specs = [pl.BlockSpec((tok, LANES), lambda step, ids: (0, 0))] * 2
-            send = queued(
-                lambda ready: call(
-                    middle_kernel, ready, specs, [keep, u], [((tok, LANES), BF16)], 10**7, grant=GRANTS[0]
-                )
-            )[0]
+            shapes = [((tok, LANES), BF16)]
+            send = queued(lambda ready: call(middle_kernel, ready, [keep, u], shapes, 10**7))[0]
         arrived[at] = second(send)
         if j is not None:
             pieces[j] = (keep, u, arrived[at])
@@ -578,8 +564,7 @@
         args = [
             raw, kept[0], parts[0], arrived[0], cosine, sine, rate_bias, decay_rate,
         ]
-        scalars = pl.BlockSpec(memory_space=pltpu.SMEM)
-        specs = [flat(a.shape) for a in args[:-2]] + [scalars] * 2
+        specs = [VMEM] * (len(args) - 2) + [SMEM] * 2
         spans = tok // STRETCH
         shapes = [
             ((tok + heads // 2 * HEAD_DIM, 2 * HEAD_DIM), BF16), ((tok, HEAD_DIM), BF16),
@@ -588,8 +573,8 @@
         ]
         carry, *rest = queued(
             lambda ready: call(
-                functools.partial(context_kernel, STRETCH), ready,
-                specs, args, shapes, 10**9, grant=GRANTS[2],
+                functools.partial(context_kernel, STRETCH), ready, args, shapes, 10**9, specs,
+                grant=GRANTS[2],
             )
         )
         came = over_seq(carry)
@@ -598,17 +583,19 @@
             cosine, sine, carry, bterm, came, across, down, step, first_state, skip_gain,
         )
 
-    def tail(pair, shared, before):
-        numbers = (2 * pair, 2 * pair + 1)
+    def tail(j, shared, before):
         return queued(
-            lambda ready: heads_call(
-                ready, pair, numbers, [pieces[n] for n in numbers], shared,
-                heads * HEAD_DIM, before,
-            )
+            lambda ready: head_call(ready, j, pieces[j], shared, heads * HEAD_DIM, before)
+        )
+
+    def prepare():
+        return queued(
+            lambda ready: call(prepare_kernel, ready, [layer_input, rate_weight.T], shapes, 10**9)
         )
 
     cross(0)
     cross(1)
+    raw, cosine, sine = prepare()
     mine(0)
     mine(1)
     cross(2)
@@ -621,10 +608,12 @@
     middle(1)
     middle(2)
     shared = context()
+    outs = tail(1, shared, None)
     middle(3)
-    outs = tail(0, shared, None)
+    outs = tail(0, shared, outs)
     middle(4)
-    outs = tail(1, shared, outs)
+    outs = tail(3, shared, outs)
+    outs = tail(2, shared, outs)
     return outs[0], outs[1]
 
 

time: 74.1 us -> 62.9 us (0.85)
  Pallas kernels: 30 us -> 21.1 us
  waiting for transfers between devices: 23.8 us -> 22.1 us
    pallas_call x19 -> x21, Pallas kernels: 30 us -> 21.1 us  [call(): pl.pallas_call(kernel, in_specs=[ANY] + (in_specs or [VMEM] * len(args)),...]
    ppermute x5, waiting for transfers between devices: 16 us -> 9.91 us  [pair_steps(): over_low = lambda a: lax.ppermute(a, 'grp', swap_low)]
    ppermute x5, waiting for transfers between devices: 7.03 us -> 10.7 us  [pair_steps(): over_high = lambda a: lax.ppermute(a, 'grp', swap_high)]
  transfers between devices with their start and end apart: 17 -> 17, of which waited for: 6 -> 7; matrix products, arithmetic and copies ran while one was open for 4% -> 5% of each run, Pallas kernels for 26% -> 23%
where the time goes in v4:
time: 62.9 us; the launch traced here: 62.7 us
  waiting for transfers between devices  22.1 us (35%)
  Pallas kernels  21.1 us (34%)
  starting transfers between devices  15.3 us (24%)
  local copies, waits for them, and re-layouts  3.33 us (5%)
  between operations  0.89 us (1%)
    pallas_call x21, Pallas kernels, call(): pl.pallas_call(kernel, in_specs=[ANY] + (in_specs or [VMEM] * len(args)),...  21.1 us
    ppermute x5, waiting for transfers between devices, pair_steps(): over_high = lambda a: lax.ppermute(a, 'grp', swap_high)  10.7 us
    ppermute x5, waiting for transfers between devices, pair_steps(): over_low = lambda a: lax.ppermute(a, 'grp', swap_low)  9.91 us
    ppermute x5, starting transfers between devices, pair_steps(): over_high = lambda a: lax.ppermute(a, 'grp', swap_high)  8.09 us
    ppermute x5, starting transfers between devices, pair_steps(): over_low = lambda a: lax.ppermute(a, 'grp', swap_low)  5 us
    unnamed x11, local copies, waits for them, and re-layouts  3.33 us
    ppermute x7, starting transfers between devices, pair_steps(): over_seq = lambda a: lax.ppermute(a, 'seq', [(0, 1), (1, 0)])  2.25 us
    ppermute x7, waiting for transfers between devices, pair_steps(): over_seq = lambda a: lax.ppermute(a, 'seq', [(0, 1), (1, 0)])  1.5 us
  transfers between devices with their start and end apart: 17, of which 7 were waited for; matrix products, arithmetic and copies ran while one was open for 5% of the time, Pallas kernels for 23%

profile of v4, /device:TPU:0, one launch (start us, length us, event | category | flops | bytes accessed | tf_op | source)
XLA Modules:
  0.0 62.7 jit_solution(17448571182024298471)
XLA Ops:
  0.6 0.6 collective-permute-start
  1.2 3.2 %copy.16 = bf16[1024,2,1280]{2,0,1:T(8,128)(2,1)S(1)} copy(bf16[1024,2,1280]{2,1,0:T(2,128)(2,1)} %param.7) | data formatting | bytes 10485760 | tf_op args[1]
  4.4 0.8 %collective-permute-done.x_ref = bf16[512,2048]{1,0:T(8,128)(2,1)S(1)} collective-permute-done((bf16[512,2048]{1,0:T(8,128)(2,1)}, bf16[512,2048]{1,0:T(8,128)(2,1)S(1)}, u32[]{:S(2)}, u32[]{:S(2)}) %collective-permute-start) | collective-permute-done | bytes 2097184 | tf_op jit(solution)/shard_map/ppermute | solution.py:499
  5.2 0.8 %shard_map.77 = bf16[512,512]{1,0:T(8,128)(2,1)S(1)} custom-call(f32[1]{0:T(128)S(1)} %bitcast.15, bf16[512,2048]{1,0:T(8,128)(2,1)S(1)} %collective-permute-done.x_ref, bf16[2,1024,1280]{2,1,0:T(8,128)(2,1)S(1)} %bitcast.5), custom_call_target="tpu_custom_call" | custom-call | flops 536870912 | bytes 3000000 | tf_op jit(solution)/shard_map/pallas_call | solution.py:287
  6.4 0.8 %shard_map.78 = bf16[512,512]{1,0:T(8,128)(2,1)S(1)} custom-call(f32[1]{0:T(128)S(1)} %bitcast.16, bf16[512,2048]{1,0:T(8,128)(2,1)S(1)} %collective-permute-done.x_ref, bf16[2,1024,1280]{2,1,0:T(8,128)(2,1)S(1)} %bitcast.6), custom_call_target="tpu_custom_call" | custom-call | flops 536870912 | bytes 3000000 | tf_op jit(solution)/shard_map/pallas_call | solution.py:287
  7.6 0.7 %shard_map.79 = (f32[16,512]{1,0:T(8,128)S(1)}, f32[512,128]{1,0:T(8,128)S(1)}, f32[512,128]{1,0:T(8,128)S(1)}) custom-call(f32[1]{0:T(128)S(1)} %bitcast.17, bf16[512,2048]{1,0:T(8,128)(2,1)S(1)} %copy-done, bf16[16,2048]{1,0:T(8,128)(2,1)S(1)} %bitcast.36), custom_call_target="tpu_custom_call" | custom-call | flops 1000000000 | bytes 3000000 | tf_op jit(solution)/shard_map/pallas_call | solution.py:287
  8.3 0.8 %shard_map.80 = (bf16[528,256]{1,0:T(8,128)(2,1)S(1)}, f32[512,256]{1,0:T(8,128)S(1)}) custom-call(f32[1]{0:T(128)S(1)} %bitcast.18, f32[16,512]{1,0:T(8,128)S(1)} %get-tuple-element.55.raw_ref, bf16[512,2048]{1,0:T(8,128)(2,1)S(1)} %copy-done, bf16[2,1024,1280]{2,1,0:T(8,128)(2,1)S(1)} %bitcast.7, bf16[512,512]{1,0:T(8,128)(2,1)S(1)} %collective-permute-done.1.refs_2_), custom_call_target="tpu_custom_call" | custom-call | flops 536870912 | bytes 3000000 | tf_op jit(solution)/shard_map/pallas_call | solution.py:287
  9.2 0.8 %shard_map.81 = (bf16[512,256]{1,0:T(8,128)(2,1)S(1)}, f32[512,256]{1,0:T(8,128)S(1)}) custom-call(f32[1]{0:T(128)S(1)} %bitcast.19, bf16[512,2048]{1,0:T(8,128)(2,1)S(1)} %copy-done, bf16[2,1024,1280]{2,1,0:T(8,128)(2,1)S(1)} %bitcast.8, bf16[512,512]{1,0:T(8,128)(2,1)S(1)} %collective-permute-done.2.r_ref), custom_call_target="tpu_custom_call" | custom-call | flops 536870912 | bytes 3000000 | tf_op jit(solution)/shard_map/pallas_call | solution.py:287
  9.9 0.8 %shard_map.82 = bf16[512,512]{1,0:T(8,128)(2,1)S(1)} custom-call(f32[1]{0:T(128)S(1)} %bitcast.20, bf16[512,2048]{1,0:T(8,128)(2,1)S(1)} %collective-permute-done.x_ref, bf16[2,1024,1280]{2,1,0:T(8,128)(2,1)S(1)} %bitcast.9), custom_call_target="tpu_custom_call" | custom-call | flops 536870912 | bytes 3000000 | tf_op jit(solution)/shard_map/pallas_call | solution.py:287
  11.1 0.8 %shard_map.83 = bf16[512,512]{1,0:T(8,128)(2,1)S(1)} custom-call(f32[1]{0:T(128)S(1)} %bitcast.21, bf16[512,2048]{1,0:T(8,128)(2,1)S(1)} %collective-permute-done.x_ref, bf16[2,1024,1280]{2,1,0:T(8,128)(2,1)S(1)} %bitcast.10), custom_call_target="tpu_custom_call" | custom-call | flops 536870912 | bytes 3000000 | tf_op jit(solution)/shard_map/pallas_call | solution.py:287
  12.2 0.6 collective-permute-done.3.r_ref
  12.7 0.8 %shard_map.84 = (bf16[512,256]{1,0:T(8,128)(2,1)S(1)}, f32[512,256]{1,0:T(8,128)S(1)}) custom-call(f32[1]{0:T(128)S(1)} %bitcast.22, bf16[512,2048]{1,0:T(8,128)(2,1)S(1)} %copy-done, bf16[2,1024,1280]{2,1,0:T(8,128)(2,1)S(1)} %bitcast.11, bf16[512,512]{1,0:T(8,128)(2,1)S(1)} %collective-permute-done.3.r_ref), custom_call_target="tpu_custom_call" | custom-call | flops 536870912 | bytes 3000000 | tf_op jit(solution)/shard_map/pallas_call | solution.py:287
  13.5 0.8 %shard_map.85 = bf16[512,512]{1,0:T(8,128)(2,1)S(1)} custom-call(f32[1]{0:T(128)S(1)} %bitcast.23, bf16[512,2048]{1,0:T(8,128)(2,1)S(1)} %collective-permute-done.x_ref, bf16[2,1024,1280]{2,1,0:T(8,128)(2,1)S(1)} %bitcast.12), custom_call_target="tpu_custom_call" | custom-call | flops 536870912 | bytes 3000000 | tf_op jit(solution)/shard_map/pallas_call | solution.py:287
  14.6 2.7 %collective-permute-start.4 = (bf16[528,256]{1,0:T(8,128)(2,1)S(1)}, bf16[528,256]{1,0:T(8,128)(2,1)S(1)}, u32[]{:S(2)}, u32[]{:S(2)}) collective-permute-start(bf16[528,256]{1,0:T(8,128)(2,1)S(1)} %get-tuple-element.57), channel_id=1, source_target_pairs={{0,16},{8,24},{16,0},{24,8},{1,17},{9,25},{17,1},{25,9},{2,18},{10... | collective-permute-start | bytes 811016 | tf_op jit(solution)/shard_map/ppermute | solution.py:497
  17.4 6.9 %collective-permute-done.4.u_ref = bf16[528,256]{1,0:T(8,128)(2,1)S(1)} collective-permute-done((bf16[528,256]{1,0:T(8,128)(2,1)S(1)}, bf16[528,256]{1,0:T(8,128)(2,1)S(1)}, u32[]{:S(2)}, u32[]{:S(2)}) %collective-permute-start.4) | collective-permute-done | bytes 270368 | tf_op jit(solution)/shard_map/ppermute | solution.py:497
  24.4 1.8 %collective-permute-start.9 = (bf16[528,256]{1,0:T(8,128)(2,1)S(1)}, bf16[528,256]{1,0:T(8,128)(2,1)S(1)}, u32[]{:S(2)}, u32[]{:S(2)}) collective-permute-start(bf16[528,256]{1,0:T(8,128)(2,1)S(1)} %shard_map.86), channel_id=1, source_target_pairs={{0,8},{8,0},{16,24},{24,16},{1,9},{9,1},{17,25},{25,17},{2,10},{10... | collective-permute-start | bytes 811016 | tf_op jit(solution)/shard_map/ppermute | solution.py:498
  26.5 1.7 %collective-permute-start.8 = (bf16[512,256]{1,0:T(8,128)(2,1)S(1)}, bf16[512,256]{1,0:T(8,128)(2,1)S(1)}, u32[]{:S(2)}, u32[]{:S(2)}) collective-permute-start(bf16[512,256]{1,0:T(8,128)(2,1)S(1)} %get-tuple-element.63), channel_id=1, source_target_pairs={{0,16},{8,24},{16,0},{24,8},{1,17},{9,25},{17,1},{25,9},{2,18},{10... | collective-permute-start | bytes 786440 | tf_op jit(solution)/shard_map/ppermute | solution.py:497
  28.2 0.8 %shard_map.87 = (bf16[512,256]{1,0:T(8,128)(2,1)S(1)}, f32[512,256]{1,0:T(8,128)S(1)}) custom-call(f32[1]{0:T(128)S(1)} %bitcast.25, bf16[512,2048]{1,0:T(8,128)(2,1)S(1)} %copy-done, bf16[2,1024,1280]{2,1,0:T(8,128)(2,1)S(1)} %bitcast.13, bf16[512,512]{1,0:T(8,128)(2,1)S(1)} %collective-permute-done.5.r_ref), custom_call_target="tpu_custom_call" | custom-call | flops 536870912 | bytes 3000000 | tf_op jit(solution)/shard_map/pallas_call | solution.py:287
  29.0 0.8 %shard_map.88 = (bf16[512,256]{1,0:T(8,128)(2,1)S(1)}, f32[512,256]{1,0:T(8,128)S(1)}) custom-call(f32[1]{0:T(128)S(1)} %bitcast.26, bf16[512,2048]{1,0:T(8,128)(2,1)S(1)} %copy-done, bf16[2,1024,1280]{2,1,0:T(8,128)(2,1)S(1)} %bitcast.14, bf16[512,512]{1,0:T(8,128)(2,1)S(1)} %collective-permute-done.6.r_ref), custom_call_target="tpu_custom_call" | custom-call | flops 536870912 | bytes 3000000 | tf_op jit(solution)/shard_map/pallas_call | solution.py:287
  29.8 8.3 %collective-permute-done.7.u_ref = bf16[512,256]{1,0:T(8,128)(2,1)S(1)} collective-permute-done((bf16[512,256]{1,0:T(8,128)(2,1)S(1)}, bf16[512,256]{1,0:T(8,128)(2,1)S(1)}, u32[]{:S(2)}, u32[]{:S(2)}) %collective-permute-start.7) | collective-permute-done | bytes 262176 | tf_op jit(solution)/shard_map/ppermute | solution.py:498
  38.3 1.7 %shard_map.91 = (bf16[768,256]{1,0:T(8,128)(2,1)S(1)}, bf16[512,128]{1,0:T(8,128)(2,1)S(1)}, f32[8,256]{1,0:T(8,128)S(1)}, f32[256,128]{1,0:T(8,128)S(1)}, f32[8...) custom-call(f32[1]{0:T(128)S(1)} %bitcast.29, f32[16,512]{1,0:T(8,128)S(1)} %get-tuple-element.55.raw_ref, ...), custom_call_target="tpu_custom_call" | custom-call | flops 1000000000 | bytes 3000000 | tf_op jit(solution)/shard_map/pallas_call | solution.py:287
  40.1 1.5 %collective-permute-start.12 = (bf16[512,256]{1,0:T(8,128)(2,1)S(1)}, bf16[512,256]{1,0:T(8,128)(2,1)S(1)}, u32[]{:S(2)}, u32[]{:S(2)}) collective-permute-start(bf16[512,256]{1,0:T(8,128)(2,1)S(1)} %get-tuple-element.68), channel_id=1, source_target_pairs={{0,8},{8,0},{16,24},{24,16},{1,9},{9,1},{17,25},{25,17},{2,10},{10... | collective-permute-start | bytes 786440 | tf_op jit(solution)/shard_map/ppermute | solution.py:498
  41.6 1.5 %collective-permute-start.10 = (bf16[512,128]{1,0:T(8,128)(2,1)S(1)}, bf16[512,128]{1,0:T(8,128)(2,1)S(1)}, u32[]{:S(2)}, u32[]{:S(2)}) collective-permute-start(bf16[512,128]{1,0:T(8,128)(2,1)S(1)} %shard_map.89), channel_id=1, source_target_pairs={{0,16},{8,24},{16,0},{24,8},{1,17},{9,25},{17,1},{25,9},{2,18},{10... | collective-permute-start | bytes 393224 | tf_op jit(solution)/shard_map/ppermute | solution.py:497
  43.6 0.6 collective-permute-start.13
  44.2 3.8 %collective-permute-done.10.z_ref = bf16[512,128]{1,0:T(8,128)(2,1)S(1)} collective-permute-done((bf16[512,128]{1,0:T(8,128)(2,1)S(1)}, bf16[512,128]{1,0:T(8,128)(2,1)S(1)}, u32[]{:S(2)}, u32[]{:S(2)}) %collective-permute-start.10) | collective-permute-done | bytes 131104 | tf_op jit(solution)/shard_map/ppermute | solution.py:497
  48.0 2.7 %shard_map.92 = (bf16[512,512]{1,0:T(8,128)(2,1)}, bf16[512,512]{1,0:T(8,128)(2,1)}) custom-call(f32[1]{0:T(128)S(1)} %bitcast.30, f32[512,256]{1,0:T(8,128)S(1)} %get-tuple-element.72.keep_ref, bf16[512,256]{1,0:T(8,128)(2,1)S(1)} %collective-permute-done.7.u_ref, bf16[512,128]{1,0:T(8,128)(2,1)S(1)} %collective-permute-done.10.z_ref, ...), custom_call_target="tpu_custom_call" | custom-call | flops 1000000000 | bytes 3000000 | tf_op jit(solution)/shard_map/pallas_call | solution.py:287
  50.7 1.6 %collective-permute-start.15 = (bf16[512,128]{1,0:T(8,128)(2,1)S(1)}, bf16[512,128]{1,0:T(8,128)(2,1)S(1)}, u32[]{:S(2)}, u32[]{:S(2)}) collective-permute-start(bf16[512,128]{1,0:T(8,128)(2,1)S(1)} %shard_map.93), channel_id=1, source_target_pairs={{0,16},{8,24},{16,0},{24,8},{1,17},{9,25},{17,1},{25,9},{2,18},{10... | collective-permute-start | bytes 393224 | tf_op jit(solution)/shard_map/ppermute | solution.py:497
  52.3 2.6 %shard_map.94 = (bf16[512,512]{1,0:T(8,128)(2,1)}, bf16[512,512]{1,0:T(8,128)(2,1)}) custom-call(f32[1]{0:T(128)S(1)} %bitcast.32, f32[512,256]{1,0:T(8,128)S(1)} %get-tuple-element.74.keep_ref, bf16[512,256]{1,0:T(8,128)(2,1)S(1)} %collective-permute-done.8.u_ref, ...), custom_call_target="tpu_custom_call", output_to_operand_aliasing={{0}: (14, {}), {1}: (15, {})} | custom-call | flops 1000000000 | bytes 3000000 | tf_op jit(solution)/shard_map/pallas_call | solution.py:287
  55.0 0.8 %collective-permute-start.16 = (bf16[512,128]{1,0:T(8,128)(2,1)S(1)}, bf16[512,128]{1,0:T(8,128)(2,1)S(1)}, u32[]{:S(2)}, u32[]{:S(2)}) collective-permute-start(bf16[512,128]{1,0:T(8,128)(2,1)S(1)} %shard_map.95), channel_id=1, source_target_pairs={{0,8},{8,0},{16,24},{24,16},{1,9},{9,1},{17,25},{25,17},{2,10},{10... | collective-permute-start | bytes 393224 | tf_op jit(solution)/shard_map/ppermute | solution.py:498
  55.9 2.7 %shard_map.96 = (bf16[512,512]{1,0:T(8,128)(2,1)}, bf16[512,512]{1,0:T(8,128)(2,1)}) custom-call(f32[1]{0:T(128)S(1)} %bitcast.34, f32[512,256]{1,0:T(8,128)S(1)} %get-tuple-element.87.keep_ref, bf16[512,256]{1,0:T(8,128)(2,1)S(1)} %collective-permute-done.12.u_ref, ...), custom_call_target="tpu_custom_call", output_to_operand_aliasing={{0}: (14, {}), {1}: (15, {})} | custom-call | flops 1000000000 | bytes 3000000 | tf_op jit(solution)/shard_map/pallas_call | solution.py:287
  58.5 1.6 %collective-permute-done.16.z_ref = bf16[512,128]{1,0:T(8,128)(2,1)S(1)} collective-permute-done((bf16[512,128]{1,0:T(8,128)(2,1)S(1)}, bf16[512,128]{1,0:T(8,128)(2,1)S(1)}, u32[]{:S(2)}, u32[]{:S(2)}) %collective-permute-start.16) | collective-permute-done | bytes 131104 | tf_op jit(solution)/shard_map/ppermute | solution.py:498
  60.1 2.7 %shard_map.97 = (bf16[512,512]{1,0:T(8,128)(2,1)}, bf16[512,512]{1,0:T(8,128)(2,1)}) custom-call(f32[1]{0:T(128)S(1)} %bitcast.35, f32[512,256]{1,0:T(8,128)S(1)} %get-tuple-element.92.keep_ref, bf16[512,256]{1,0:T(8,128)(2,1)S(1)} %collective-permute-done.14.u_ref, ...), custom_call_target="tpu_custom_call", output_to_operand_aliasing={{0}: (14, {}), {1}: (15, {})} | custom-call | flops 1000000000 | bytes 3000000 | tf_op jit(solution)/shard_map/pallas_call | solution.py:287
  (34 shorter events, 3.1 us)
Async XLA Ops:
  0.6 4.6 %collective-permute-start = (bf16[512,2048]{1,0:T(8,128)(2,1)}, bf16[512,2048]{1,0:T(8,128)(2,1)S(1)}, u32[]{:S(2)}, u32[]{:S(2)}) collective-permute-start(bf16[512,2048]{1,0:T(8,128)(2,1)} %x_ref.9), channel_id=1, source_target_pairs={{0,4},{4,0},{1,5},{5,1},{2,6},{6,2},{3,7},{7,3},{8,12},{12,8},{9,1... | collective-permute-start | bytes 6291464 | tf_op jit(solution)/shard_map/ppermute | solution.py:499
  1.2 4.0 %copy-start.1 = (f32[4]{0:T(128)S(1)}, f32[4]{0:T(128)}, u32[]{:S(2)}) copy-start(f32[4]{0:T(128)} %skip_ref.7) | copy-start | bytes 52
  6.0 1.6 %copy-start = (bf16[512,2048]{1,0:T(8,128)(2,1)S(1)}, bf16[512,2048]{1,0:T(8,128)(2,1)}, u32[]{:S(2)}) copy-start(bf16[512,2048]{1,0:T(8,128)(2,1)} %x_ref.9) | copy-start | bytes 6291460
  6.0 1.6 %copy-start.2 = (bf16[2048,16]{0,1:T(8,128)(2,1)S(1)}, bf16[2048,16]{0,1:T(8,128)(2,1)}, u32[]{:S(2)}) copy-start(bf16[2048,16]{0,1:T(8,128)(2,1)} %param.8) | copy-start | bytes 196612
  6.0 2.3 %collective-permute-start.1 = (bf16[512,512]{1,0:T(8,128)(2,1)S(1)}, bf16[512,512]{1,0:T(8,128)(2,1)S(1)}, u32[]{:S(2)}, u32[]{:S(2)}) collective-permute-start(bf16[512,512]{1,0:T(8,128)(2,1)S(1)} %shard_map.77), channel_id=1, source_target_pairs={{0,4},{4,0},{1,5},{5,1},{2,6},{6,2},{3,7},{7,3},{8,12},{12,8},{9,1... | collective-permute-start | bytes 1572872 | tf_op jit(solution)/shard_map/ppermute | solution.py:499
  7.2 2.0 %collective-permute-start.2 = (bf16[512,512]{1,0:T(8,128)(2,1)S(1)}, bf16[512,512]{1,0:T(8,128)(2,1)S(1)}, u32[]{:S(2)}, u32[]{:S(2)}) collective-permute-start(bf16[512,512]{1,0:T(8,128)(2,1)S(1)} %shard_map.78), channel_id=1, source_target_pairs={{0,4},{4,0},{1,5},{5,1},{2,6},{6,2},{3,7},{7,3},{8,12},{12,8},{9,1... | collective-permute-start | bytes 1572872 | tf_op jit(solution)/shard_map/ppermute | solution.py:499
  10.7 2.0 %collective-permute-start.3 = (bf16[512,512]{1,0:T(8,128)(2,1)S(1)}, bf16[512,512]{1,0:T(8,128)(2,1)S(1)}, u32[]{:S(2)}, u32[]{:S(2)}) collective-permute-start(bf16[512,512]{1,0:T(8,128)(2,1)S(1)} %shard_map.82), channel_id=1, source_target_pairs={{0,4},{4,0},{1,5},{5,1},{2,6},{6,2},{3,7},{7,3},{8,12},{12,8},{9,1... | collective-permute-start | bytes 1572872 | tf_op jit(solution)/shard_map/ppermute | solution.py:499
  11.9 16.4 %collective-permute-start.5 = (bf16[512,512]{1,0:T(8,128)(2,1)S(1)}, bf16[512,512]{1,0:T(8,128)(2,1)S(1)}, u32[]{:S(2)}, u32[]{:S(2)}) collective-permute-start(bf16[512,512]{1,0:T(8,128)(2,1)S(1)} %shard_map.83), channel_id=1, source_target_pairs={{0,4},{4,0},{1,5},{5,1},{2,6},{6,2},{3,7},{7,3},{8,12},{12,8},{9,1... | collective-permute-start | bytes 1572872 | tf_op jit(solution)/shard_map/ppermute | solution.py:499
  14.3 14.7 %collective-permute-start.6 = (bf16[512,512]{1,0:T(8,128)(2,1)S(1)}, bf16[512,512]{1,0:T(8,128)(2,1)S(1)}, u32[]{:S(2)}, u32[]{:S(2)}) collective-permute-start(bf16[512,512]{1,0:T(8,128)(2,1)S(1)} %shard_map.85), channel_id=1, source_target_pairs={{0,4},{4,0},{1,5},{5,1},{2,6},{6,2},{3,7},{7,3},{8,12},{12,8},{9,1... | collective-permute-start | bytes 1572872 | tf_op jit(solution)/shard_map/ppermute | solution.py:499
  14.6 9.7 %collective-permute-start.4 = (bf16[528,256]{1,0:T(8,128)(2,1)S(1)}, bf16[528,256]{1,0:T(8,128)(2,1)S(1)}, u32[]{:S(2)}, u32[]{:S(2)}) collective-permute-start(bf16[528,256]{1,0:T(8,128)(2,1)S(1)} %get-tuple-element.57), channel_id=1, source_target_pairs={{0,16},{8,24},{16,0},{24,8},{1,17},{9,25},{17,1},{25,9},{2,18},{10... | collective-permute-start | bytes 811016 | tf_op jit(solution)/shard_map/ppermute | solution.py:497
  24.4 13.9 %collective-permute-start.9 = (bf16[528,256]{1,0:T(8,128)(2,1)S(1)}, bf16[528,256]{1,0:T(8,128)(2,1)S(1)}, u32[]{:S(2)}, u32[]{:S(2)}) collective-permute-start(bf16[528,256]{1,0:T(8,128)(2,1)S(1)} %shard_map.86), channel_id=1, source_target_pairs={{0,8},{8,0},{16,24},{24,16},{1,9},{9,1},{17,25},{25,17},{2,10},{10... | collective-permute-start | bytes 811016 | tf_op jit(solution)/shard_map/ppermute | solution.py:498
  26.2 12.0 %collective-permute-start.7 = (bf16[512,256]{1,0:T(8,128)(2,1)S(1)}, bf16[512,256]{1,0:T(8,128)(2,1)S(1)}, u32[]{:S(2)}, u32[]{:S(2)}) collective-permute-start(bf16[512,256]{1,0:T(8,128)(2,1)S(1)} %get-tuple-element.59), channel_id=1, source_target_pairs={{0,8},{8,0},{16,24},{24,16},{1,9},{9,1},{17,25},{25,17},{2,10},{10... | collective-permute-start | bytes 786440 | tf_op jit(solution)/shard_map/ppermute | solution.py:498
  26.5 11.8 %collective-permute-start.8 = (bf16[512,256]{1,0:T(8,128)(2,1)S(1)}, bf16[512,256]{1,0:T(8,128)(2,1)S(1)}, u32[]{:S(2)}, u32[]{:S(2)}) collective-permute-start(bf16[512,256]{1,0:T(8,128)(2,1)S(1)} %get-tuple-element.63), channel_id=1, source_target_pairs={{0,16},{8,24},{16,0},{24,8},{1,17},{9,25},{17,1},{25,9},{2,18},{10... | collective-permute-start | bytes 786440 | tf_op jit(solution)/shard_map/ppermute | solution.py:497
  29.0 9.3 %copy-start.3 = (f32[4]{0:T(128)S(1)}, f32[4]{0:T(128)}, u32[]{:S(2)}) copy-start(f32[4]{0:T(128)} %bias_ref.1) | copy-start | bytes 52
  29.0 9.3 %copy-start.4 = (f32[4]{0:T(128)S(1)}, f32[4]{0:T(128)}, u32[]{:S(2)}) copy-start(f32[4]{0:T(128)} %rate_ref.1) | copy-start | bytes 52
  40.0 8.0 %collective-permute-start.11 = (bf16[768,256]{1,0:T(8,128)(2,1)S(1)}, bf16[768,256]{1,0:T(8,128)(2,1)S(1)}, u32[]{:S(2)}, u32[]{:S(2)}) collective-permute-start(bf16[768,256]{1,0:T(8,128)(2,1)S(1)} %get-tuple-element.78.carry_ref), channel_id=1, source_target_pairs={{0,4},{4,0},{1,5},{5,1},{2,6},{6,2},{3,7},{7,3},{8,12},{12,8},{9,1... | collective-permute-start | bytes 1179656 | tf_op jit(solution)/shard_map/ppermute | solution.py:499
  40.1 10.5 %collective-permute-start.12 = (bf16[512,256]{1,0:T(8,128)(2,1)S(1)}, bf16[512,256]{1,0:T(8,128)(2,1)S(1)}, u32[]{:S(2)}, u32[]{:S(2)}) collective-permute-start(bf16[512,256]{1,0:T(8,128)(2,1)S(1)} %get-tuple-element.68), channel_id=1, source_target_pairs={{0,8},{8,0},{16,24},{24,16},{1,9},{9,1},{17,25},{25,17},{2,10},{10... | collective-permute-start | bytes 786440 | tf_op jit(solution)/shard_map/ppermute | solution.py:498
  41.6 6.4 %collective-permute-start.10 = (bf16[512,128]{1,0:T(8,128)(2,1)S(1)}, bf16[512,128]{1,0:T(8,128)(2,1)S(1)}, u32[]{:S(2)}, u32[]{:S(2)}) collective-permute-start(bf16[512,128]{1,0:T(8,128)(2,1)S(1)} %shard_map.89), channel_id=1, source_target_pairs={{0,16},{8,24},{16,0},{24,8},{1,17},{9,25},{17,1},{25,9},{2,18},{10... | collective-permute-start | bytes 393224 | tf_op jit(solution)/shard_map/ppermute | solution.py:497
  43.1 11.8 %collective-permute-start.14 = (bf16[512,256]{1,0:T(8,128)(2,1)S(1)}, bf16[512,256]{1,0:T(8,128)(2,1)S(1)}, u32[]{:S(2)}, u32[]{:S(2)}) collective-permute-start(bf16[512,256]{1,0:T(8,128)(2,1)S(1)} %get-tuple-element.70), channel_id=1, source_target_pairs={{0,16},{8,24},{16,0},{24,8},{1,17},{9,25},{17,1},{25,9},{2,18},{10... | collective-permute-start | bytes 786440 | tf_op jit(solution)/shard_map/ppermute | solution.py:497
  43.6 8.7 %collective-permute-start.13 = (bf16[512,128]{1,0:T(8,128)(2,1)S(1)}, bf16[512,128]{1,0:T(8,128)(2,1)S(1)}, u32[]{:S(2)}, u32[]{:S(2)}) collective-permute-start(bf16[512,128]{1,0:T(8,128)(2,1)S(1)} %shard_map.90), channel_id=1, source_target_pairs={{0,8},{8,0},{16,24},{24,16},{1,9},{9,1},{17,25},{25,17},{2,10},{10... | collective-permute-start | bytes 393224 | tf_op jit(solution)/shard_map/ppermute | solution.py:498
  50.7 5.1 %collective-permute-start.15 = (bf16[512,128]{1,0:T(8,128)(2,1)S(1)}, bf16[512,128]{1,0:T(8,128)(2,1)S(1)}, u32[]{:S(2)}, u32[]{:S(2)}) collective-permute-start(bf16[512,128]{1,0:T(8,128)(2,1)S(1)} %shard_map.93), channel_id=1, source_target_pairs={{0,16},{8,24},{16,0},{24,8},{1,17},{9,25},{17,1},{25,9},{2,18},{10... | collective-permute-start | bytes 393224 | tf_op jit(solution)/shard_map/ppermute | solution.py:497
  55.0 5.0 %collective-permute-start.16 = (bf16[512,128]{1,0:T(8,128)(2,1)S(1)}, bf16[512,128]{1,0:T(8,128)(2,1)S(1)}, u32[]{:S(2)}, u32[]{:S(2)}) collective-permute-start(bf16[512,128]{1,0:T(8,128)(2,1)S(1)} %shard_map.95), channel_id=1, source_target_pairs={{0,8},{8,0},{16,24},{24,16},{1,9},{9,1},{17,25},{25,17},{2,10},{10... | collective-permute-start | bytes 393224 | tf_op jit(solution)/shard_map/ppermute | solution.py:498
